TPU v7x, 256 devices: a whole 4x4x8 slice. The times are simulated.
256 devices in a mesh: grp: 8 (over y, core), shard: 32 (over x, z).
Axes of the slice: x: 4, y: 4, z: 8, core: 2. Of those that a mesh axis runs over, the one named last changes fastest.
Arguments:
- grads: float32 [8, 32, 3456, 512], P('grp', 'shard'), may hold values from -6 to 6
- master: float32 [3456, 512], P('shard'), may hold values from -0.109375 to 0.109375
- moment_one: float32 [3456, 512], P('shard'), may hold values from -0.0004510549 to 0.0004510549
- moment_two: float32 [3456, 512], P('shard'), may hold values from 1.13028066e-10 to 2.8257017e-09
- step_count: int32 [1], replicated, may hold values from 1 to 59
Outputs:
- new_master: float32 [3456, 512], P('shard')
- new_moment_one: float32 [3456, 512], P('shard')
- new_moment_two: float32 [3456, 512], P('shard')
- weights: bfloat16 [3456, 512], replicated
All inputs are finite; a program needn't handle non-finite values.
Results may differ from a plain program's by a relative error of at most 0.0004.
Values may be sent and summed in bfloat16 or wider, within the bound.
No kernel may reach another device: no remote copies, remote signals or barrier semaphores. Data moves between devices by JAX's collectives and lax.ppermute only.
A program may use at most 128 MiB of HBM per device.

v0:
```python
import jax
import jax.numpy as jnp
from jax import lax
from jax.sharding import Mesh
from jax.sharding import PartitionSpec as P

SHARD = ("shard_0", "shard_1")


def sum_by_axis(value, axes, dim):
    for axis in axes:
        value = lax.psum_scatter(value, axis, scatter_dimension=dim, tiled=True)
    return value


def sent_to_all(value, axis):
    copies = jnp.broadcast_to(value, (lax.axis_size(axis), *value.shape))
    return lax.all_to_all(copies, axis, split_axis=0, concat_axis=0, tiled=True)


def of_everyone(value, axis):
    return sent_to_all(value, axis).sum(axis=0)


def in_order(blocks, dim):
    blocks = jnp.moveaxis(blocks, 0, dim)
    lengths = blocks.shape
    return blocks.reshape(*lengths[:dim], lengths[dim] * lengths[dim + 1], *lengths[dim + 2 :])


def gather_in_order(value, axes, turns):
    blocks = value
    for k in turns:
        blocks = lax.all_gather(blocks, axes[k])
    done = turns[::-1]
    back = [done.index(k) for k in range(len(axes))]
    blocks = blocks.transpose(*back, *range(len(axes), blocks.ndim))
    return blocks.reshape(-1, *value.shape)


def gathered_by_axis(value, axes, turns, dim):
    return in_order(gather_in_order(value, axes, turns), dim)


def shards(grads, master, moment_one, moment_two, step_count):
    local = grads[0, 0]
    partial_rows = sum_by_axis(local, SHARD, 0)
    gradient = of_everyone(partial_rows, "grp")
    squares = of_everyone(jnp.sum(gradient * gradient), SHARD)
    norm = jnp.sqrt(squares)
    clip = jnp.minimum(jnp.float32(1.0), 1.0 / (norm + 1e-06))
    gradient = clip * gradient
    new_one = 0.9 * moment_one + 0.1 * gradient
    new_two = 0.999 * moment_two + 0.001 * gradient * gradient
    steps = step_count[0].astype(jnp.float32)
    first_fix = 1.0 - jnp.power(jnp.float32(0.9), steps)
    second_fix = 1.0 - jnp.power(jnp.float32(0.999), steps)
    update = new_one / first_fix / (jnp.sqrt(new_two / second_fix) + 1e-08)
    new_master = master - 0.01 * (update + 0.01 * master)
    weights = gathered_by_axis(new_master.astype(jnp.bfloat16), SHARD, (0, 1), 0)
    return (new_master, new_one, new_two, weights)


def solution(mesh):
    finer = Mesh(mesh.devices.reshape(mesh.shape["grp"], 4, 8), ("grp", "shard_0", "shard_1"))
    in_specs = (P("grp", SHARD, None, None), P(SHARD, None), P(SHARD, None), P(SHARD, None), P())
    out_specs = (P(SHARD, None), P(SHARD, None), P(SHARD, None), P())
    return jax.shard_map(
        shards, mesh=finer, in_specs=in_specs, out_specs=out_specs, check_vma=False
    )
```

profile of v0, /device:TPU:1, one launch (start us, length us, event | category | flops | bytes accessed | tf_op | source)
XLA Modules:
  0.0 246.5 jit_solution(18048320441037691581)
XLA Ops:
  7.2 0.0 reduce-scatter.4.cloned.1.call-start
  7.2 0.7 reduce-scatter.4.cloned.1.call-update
  7.9 0.0 copy-start.3
  7.9 79.3 %reduce-scatter.4.cloned.1.call-done = f32[864,512]{1,0:T(8,128)} async-done(((f32[3456,512]{1,0:T(8,128)}), f32[864,512]{1,0:T(8,128)}) %reduce-scatter.4.cloned.1.call-update) | async-done | bytes 1769488 | tf_op jit(solution)/shard_map/reduce_scatter | solution.py:12
  87.2 26.8 %fusion = f32[112,512]{1,0:T(8,128)S(1)} fusion(f32[864,512]{1,0:T(8,128)} %reduce-scatter.4.cloned.1.call-done), kind=kCustom, calls=%all-reduce-scatter | all-reduce-scatter fusion | flops 458753 | bytes 1999872
  114.1 2.5 %collective-permute-start = (f32[28,512]{1,0:T(8,128)S(1)}, f32[28,512]{1,0:T(8,128)S(1)}, u32[]{:S(2)}, u32[]{:S(2)}) collective-permute-start(f32[28,512]{1,0:T(8,128)S(1)} %slice), channel_id=1, source_target_pairs={{0,1},{1,2},{2,3},{3,4},{4,5},{5,6},{6,7},{8,9},{9,10},{10,11},{11... | collective-permute-start | bytes 172040
  116.6 0.0 copy-done.3
  116.6 0.6 dynamic-slice.4
  117.8 0.1 collective-permute-done
  117.9 0.3 concatenate
  118.2 1.5 broadcast_in_dim.6
  119.6 7.0 %all-to-all-start = ((f32[8,108,512]{2,1,0:T(8,128)}), f32[8,108,512]{2,1,0:T(8,128)S(1)}, u32[]{:S(2)}, u32[]{:S(2)}) async-start(f32[8,108,512]{2,1,0:T(8,128)} %broadcast_in_dim.6), calls=%async_computation.1 | async-start | bytes 3670016 | tf_op jit(solution)/shard_map/all_to_all | solution.py:18
  126.7 0.0 copy-start
  126.7 0.0 copy-start.1
  126.7 0.0 copy-start.2
  127.4 22.6 %all-to-all-done = f32[8,108,512]{2,1,0:T(8,128)S(1)} async-done(((f32[8,108,512]{2,1,0:T(8,128)}), f32[8,108,512]{2,1,0:T(8,128)S(1)}, u32[]{:S(2)}, u32[]{:S(2)}) %all-to-all-start) | async-done | bytes 1769504 | tf_op jit(solution)/shard_map/all_to_all | solution.py:18
  150.1 0.2 reduce_sum.27
  150.2 0.7 multiply_reduce_fusion
  150.9 1.3 broadcast_in_dim.7
  152.2 8.7 %all-to-all-start.1 = ((f32[32,1,1]{2,1,0:T(1,128)}), f32[32,1,1]{2,1,0:T(1,128)S(1)}, u32[]{:S(2)}, u32[]{:S(2)}) async-start(f32[32,1,1]{2,1,0:T(1,128)} %broadcast_in_dim.7), calls=%async_computation.2 | async-start | bytes 32768 | tf_op jit(solution)/shard_map/all_to_all | solution.py:18
  160.9 0.0 all-gather.5.cloned.1.call-start
  161.0 8.5 %all-to-all-done.1 = f32[32,1,1]{2,1,0:T(1,128)S(1)} async-done(((f32[32,1,1]{2,1,0:T(1,128)}), f32[32,1,1]{2,1,0:T(1,128)S(1)}, u32[]{:S(2)}, u32[]{:S(2)}) %all-to-all-start.1) | async-done | bytes 160 | tf_op jit(solution)/shard_map/all_to_all | solution.py:18
  169.5 0.6 reduce_sum.29
  170.9 0.0 copy-done
  170.9 0.0 copy-done.1
  170.9 0.0 copy-done.2
  170.9 1.0 convert_bitcast_fusion
  171.8 11.8 %all-gather.2 = bf16[4,108,512]{2,1,0:T(8,128)(2,1)} all-gather(bf16[1,108,512]{2,1,0:T(8,128)(2,1)S(1)} %get-tuple-element.4), channel_id=2, replica_groups=mesh['grp'=8,'shard_0'=4,'shard_1'=8] {'shard_0'}, dimensions={0}, use_global_device_ids=true | all-gather | bytes 552960 | tf_op jit(solution)/shard_map/all_gather | solution.py:34
  183.6 0.0 all-gather.5.cloned.1.call-update
  183.7 46.3 %all-gather.5.cloned.1.call-done = bf16[32,108,512]{2,1,0:T(8,128)(2,1)} async-done(((bf16[4,108,512]{2,1,0:T(8,128)(2,1)}), bf16[32,108,512]{2,1,0:T(8,128)(2,1)}) %all-gather.5.cloned.1.call-update) | async-done | bytes 3538960 | tf_op jit(solution)/shard_map/all_gather | solution.py:34
  229.9 4.2 %copy.19 = bf16[8,4,108,512]{3,2,0,1:T(8,128)(2,1)} copy(bf16[8,4,108,512]{3,2,1,0:T(8,128)(2,1)} %bitcast.14) | data formatting | bytes 7077888 | tf_op jit(solution)/shard_map/all_gather | solution.py:34
  234.1 5.6 %reshape_reshape.3 = bf16[3456,512]{1,0:T(8,128)(2,1)} reshape(bf16[4,8,108,512]{3,2,1,0:T(8,128)(2,1)} %bitcast.12) | data formatting | bytes 7077888 | tf_op jit(solution)/shard_map/reshape;reshape | solution.py:28
  (2 shorter events, 0.0 us)
Async XLA Ops:
  7.2 80.0 %reduce-scatter.4.cloned.1.call-start = ((), (), s32[]{:S(2)}) async-start(), calls=%async_computation.3 | async-start | bytes 8847360 | tf_op jit(solution)/shard_map/reduce_scatter | solution.py:12
  7.9 108.7 %copy-start.3 = (u32[256]{0:T(256)S(1)}, u32[256]{0:T(256)}, u32[]{:S(2)}) copy-start(u32[256]{0:T(256)} %constant.33) | copy-start | bytes 3076
  114.1 3.8 %collective-permute-start = (f32[28,512]{1,0:T(8,128)S(1)}, f32[28,512]{1,0:T(8,128)S(1)}, u32[]{:S(2)}, u32[]{:S(2)}) collective-permute-start(f32[28,512]{1,0:T(8,128)S(1)} %slice), channel_id=1, source_target_pairs={{0,1},{1,2},{2,3},{3,4},{4,5},{5,6},{6,7},{8,9},{9,10},{10,11},{11... | collective-permute-start | bytes 172040
  119.6 30.4 %all-to-all-start = ((f32[8,108,512]{2,1,0:T(8,128)}), f32[8,108,512]{2,1,0:T(8,128)S(1)}, u32[]{:S(2)}, u32[]{:S(2)}) async-start(f32[8,108,512]{2,1,0:T(8,128)} %broadcast_in_dim.6), calls=%async_computation.1 | async-start | bytes 3670016 | tf_op jit(solution)/shard_map/all_to_all | solution.py:18
  126.7 44.2 %copy-start = (f32[108,512]{1,0:T(8,128)S(1)}, f32[108,512]{1,0:T(8,128)}, u32[]{:S(2)}) copy-start(f32[108,512]{1,0:T(8,128)} %param.6) | copy-start | bytes 663556
  126.7 44.2 %copy-start.1 = (f32[108,512]{1,0:T(8,128)S(1)}, f32[108,512]{1,0:T(8,128)}, u32[]{:S(2)}) copy-start(f32[108,512]{1,0:T(8,128)} %param.8) | copy-start | bytes 663556
  126.7 44.2 %copy-start.2 = (f32[108,512]{1,0:T(8,128)S(1)}, f32[108,512]{1,0:T(8,128)}, u32[]{:S(2)}) copy-start(f32[108,512]{1,0:T(8,128)} %param.7) | copy-start | bytes 663556
  152.2 17.3 %all-to-all-start.1 = ((f32[32,1,1]{2,1,0:T(1,128)}), f32[32,1,1]{2,1,0:T(1,128)S(1)}, u32[]{:S(2)}, u32[]{:S(2)}) async-start(f32[32,1,1]{2,1,0:T(1,128)} %broadcast_in_dim.7), calls=%async_computation.2 | async-start | bytes 32768 | tf_op jit(solution)/shard_map/all_to_all | solution.py:18
  160.9 69.0 %all-gather.5.cloned.1.call-start = ((), (), s32[]{:S(2)}) async-start(), calls=%async_computation.4 | async-start | bytes 4128768 | tf_op jit(solution)/shard_map/all_gather | solution.py:34
Sparse Core Ops, SparseCore 0:
  10.5 76.6 reduce-scatter.3
  183.8 46.0 all-gather.4
where the time goes:
time: 247 us
  waiting for transfers between devices  157 us (64%)
  blocking collectives  38.6 us (16%)
  starting transfers between devices  18.3 us (7%)
  between operations  16.3 us (7%)
  local copies, waits for them, and re-layouts  13.4 us (5%)
    reduce_scatter x1, waiting for transfers between devices, sum_by_axis(): value = lax.psum_scatter(value, axis, scatter_dimension=dim, tiled=True)  79.3 us
    all_gather x1, waiting for transfers between devices, gather_in_order(): blocks = lax.all_gather(blocks, axes[k])  46.3 us
    all_to_all x2, waiting for transfers between devices, sent_to_all(): return lax.all_to_all(copies, axis, split_axis=0, concat_axis=0, tiled=True)  31.1 us
    unnamed x1, blocking collectives  26.8 us
    all_to_all x2, starting transfers between devices, sent_to_all(): return lax.all_to_all(copies, axis, split_axis=0, concat_axis=0, tiled=True)  15.8 us
    all_gather x1, blocking collectives, gather_in_order(): blocks = lax.all_gather(blocks, axes[k])  11.8 us
    another operation x1, local copies, waits for them, and re-layouts, in_order(): blocks.reshape(*lengths[:dim], lengths[dim] * lengths[dim + 1], *lengths[...  5.56 us
  transfers between devices with their start and end apart: 5, of which 5 were waited for; matrix products, arithmetic and copies ran while one was open for 0% of the time, Pallas kernels for 0%

commit v1 on v0

v1 whole, which is shorter than its diff:
```python
import jax
import jax.numpy as jnp
from jax import lax
from jax.experimental import pallas as pl
from jax.experimental.pallas import tpu as pltpu
from jax.sharding import Mesh
from jax.sharding import PartitionSpec as P

GRP = ("y", "c")
SHARD = ("x", "zp", "zl")
PLANE = ("x", "y")
PAIR = ("y", "c", "zl")
PAIRS = ("x", "zp")

STARTS = (0, 56, 112, 160)
PART = 56
HALF_STARTS = (0, 104)
HALF = 112


def add_halves_kernel(c_ref, mine_ref, theirs_ref, out_ref):
    for zp in range(4):
        for zl in range(2):
            for y in range(4):
                rows = pl.ds(zp * 216 + STARTS[y], PART)
                cols = pl.ds(zl * 128, 128)
                out_ref[0, y, pl.ds((zp * 2 + zl) * PART, PART), :] = mine_ref[rows, cols] + theirs_ref[rows, cols]


def add_halves(c, local, theirs):
    return pl.pallas_call(
        add_halves_kernel,
        grid_spec=pltpu.PrefetchScalarGridSpec(
            num_scalar_prefetch=1,
            grid=(4,),
            in_specs=[
                pl.BlockSpec((864, 256), lambda i, c: (i, c[0])),
                pl.BlockSpec((864, 256), lambda i, c: (i, 0)),
            ],
            out_specs=pl.BlockSpec((1, 4, 8 * PART, 128), lambda i, c: (i, 0, 0, 0)),
        ),
        out_shape=jax.ShapeDtypeStruct((4, 4, 8 * PART, 128), jnp.float32),
    )(c, local, theirs)


def place_pair(buf, parts_ref):
    for y in range(4):
        for tc in range(4):
            buf[pl.ds(STARTS[y], PART), pl.ds(tc * 128, 128)] = parts_ref[y * 4 + tc]


def squares_kernel(parts_ref, sum_ref, total_ref):
    place_pair(sum_ref, parts_ref)
    total = jnp.zeros((8, 512), jnp.float32)
    for t in range(27):
        row = sum_ref[pl.ds(t * 8, 8), :]
        total = total + row * row
    total = jnp.sum(total)
    total_ref[...] = jnp.full(total_ref.shape, total, jnp.float32)


def squares(parts):
    return pl.pallas_call(
        squares_kernel,
        out_shape=(
            jax.ShapeDtypeStruct((216, 512), jnp.float32),
            jax.ShapeDtypeStruct((16, 1, 128), jnp.float32),
        ),
    )(parts)


def adam_kernel(where_ref, fixes_ref, summed_ref, totals_ref, *refs):
    (w_own, w_other, a_own, a_other, b_own, b_other, w_out, a_out, b_out, send_ref, w, a, b) = refs
    y, c, zl = where_ref[0], where_ref[1], where_ref[2]
    first = zl == 0
    for buf, own, other in ((w, w_own, w_other), (a, a_own, a_other), (b, b_own, b_other)):
        buf[pl.ds(0, 108), :] = jnp.where(first, own[...], other[...])
        buf[pl.ds(108, 108), :] = jnp.where(first, other[...], own[...])
    total = jnp.sum(totals_ref[...], axis=0)
    norm = jnp.sqrt(total)
    clip = jnp.minimum(jnp.float32(1.0), 1.0 / (norm + 1e-06))
    clip = clip[:, :1]
    gradient = clip * summed_ref[...]
    new_one = 0.9 * a[...] + 0.1 * gradient
    new_two = 0.999 * b[...] + 0.001 * gradient * gradient
    update = new_one / fixes_ref[0] / (jnp.sqrt(new_two / fixes_ref[1]) + 1e-08)
    new_master = w[...] - 0.01 * (update + 0.01 * w[...])
    a[...] = new_one
    b[...] = new_two
    w[...] = new_master
    for buf, out in ((w, w_out), (a, a_out), (b, b_out)):
        out[...] = jnp.where(first, buf[pl.ds(0, 108), :], buf[pl.ds(108, 108), :])
    low = w[pl.ds(0, HALF), pl.ds(pl.multiple_of(y * 128, 128), 128)]
    high = w[pl.ds(HALF_STARTS[1], HALF), pl.ds(pl.multiple_of(y * 128, 128), 128)]
    part = jnp.where(c == 0, low, high).astype(jnp.bfloat16)
    for k in range(4):
        send_ref[k] = part


def adam(where, fixes, summed, totals, states):
    smem = pl.BlockSpec(memory_space=pltpu.SMEM)
    vmem = pl.BlockSpec(memory_space=pltpu.VMEM)
    rows = jax.ShapeDtypeStruct((108, 512), jnp.float32)
    return pl.pallas_call(
        adam_kernel,
        in_specs=[smem, smem] + [vmem] * 8,
        out_shape=(rows, rows, rows, jax.ShapeDtypeStruct((4, HALF, 128), jnp.bfloat16)),
        scratch_shapes=[pltpu.VMEM((216, 512), jnp.float32)] * 3,
    )(where, fixes, summed, totals, *states)


def assemble_kernel(c_ref, mine_ref, theirs_ref, out_ref):
    first = c_ref[0] == 0
    for zp in range(4):
        for y in range(4):
            for half in range(2):
                rows = pl.ds(zp * 216 + HALF_STARTS[half], HALF)
                mine, theirs = mine_ref[0, y, zp], theirs_ref[0, y, zp]
                value = jnp.where(first == (half == 0), mine, theirs)
                out_ref[rows, pl.ds(y * 128, 128)] = value


def assemble(c, mine, theirs):
    block = pl.BlockSpec((1, 4, 4, HALF, 128), lambda i, c: (i, 0, 0, 0, 0))
    return pl.pallas_call(
        assemble_kernel,
        grid_spec=pltpu.PrefetchScalarGridSpec(
            num_scalar_prefetch=1,
            grid=(4,),
            in_specs=[block, block],
            out_specs=pl.BlockSpec((864, 512), lambda i, c: (i, 0)),
        ),
        out_shape=jax.ShapeDtypeStruct((3456, 512), jnp.bfloat16),
    )(c, mine, theirs)


def exchanged(value, axes):
    return lax.all_to_all(value, axes, split_axis=0, concat_axis=0, tiled=True)


def swapped(value, axis):
    return lax.ppermute(value, axis, [(0, 1), (1, 0)])


def shards(grads, master, moment_one, moment_two, step_count):
    y, c, zl = (lax.axis_index(axis) for axis in PAIR)
    where = jnp.stack([y, c, zl]).astype(jnp.int32)
    side = where[1:2]
    local = grads[0, 0]
    theirs = swapped(lax.dynamic_slice(local, (0, 256 * (1 - c)), (3456, 256)), "c")
    states = []
    for own in (master, moment_one, moment_two):
        states += [own, swapped(own, "zl")]
    chunks = add_halves(side, local, theirs).reshape(16, 8 * PART, 128)
    columns = exchanged(chunks, PLANE).sum(axis=0)
    part = exchanged(columns.reshape(8, PART, 128), ("zp", "zl")).sum(axis=0)
    parts = exchanged(jnp.broadcast_to(part, (16, PART, 128)), PAIR)
    summed, total = squares(parts)
    totals = exchanged(total, PAIRS)
    steps = step_count[0].astype(jnp.float32)
    first_fix = 1.0 - jnp.power(jnp.float32(0.9), steps)
    second_fix = 1.0 - jnp.power(jnp.float32(0.999), steps)
    new_master, new_one, new_two, sent = adam(where, jnp.stack([first_fix, second_fix]), summed, totals, states)
    column = exchanged(sent, "zp")
    mine = exchanged(jnp.broadcast_to(column, (16, *column.shape)), PLANE)
    other = swapped(mine, "c")
    grouped = (4, 4, 4, HALF, 128)
    weights = assemble(side, mine.reshape(grouped), other.reshape(grouped))
    return (new_master, new_one, new_two, weights)


def solution(mesh):
    finer = Mesh(mesh.devices.reshape(4, 2, 4, 4, 2), ("y", "c", "x", "zp", "zl"))
    in_specs = (P(GRP, SHARD, None, None), P(SHARD, None), P(SHARD, None), P(SHARD, None), P())
    out_specs = (P(SHARD, None), P(SHARD, None), P(SHARD, None), P())
    return jax.shard_map(
        shards, mesh=finer, in_specs=in_specs, out_specs=out_specs, check_vma=False
    )
```

time: 247 us -> 177 us (0.72)
  waiting for transfers between devices: 157 us -> 22 us
  blocking collectives: 38.6 us -> 105 us
  between operations: 16.3 us -> 1.43 us
  Pallas kernels: 0 us -> 14.8 us
  local copies, waits for them, and re-layouts: 13.4 us -> 7.78 us
  starting transfers between devices: 18.3 us -> 21 us
    all_to_all x0 -> x4, blocking collectives: none -> 105 us  [exchanged(): return lax.all_to_all(value, axes, split_axis=0, concat_axis=0, tiled=True)]
    reduce_scatter x1 -> x0, waiting for transfers between devices: 79.3 us -> none  [sum_by_axis(): value = lax.psum_scatter(value, axis, scatter_dimension=dim, tiled=True)]
    all_gather x1 -> x0, waiting for transfers between devices: 46.3 us -> none  [gather_in_order(): blocks = lax.all_gather(blocks, axes[k])]
    unnamed x1 -> x0, blocking collectives: 26.8 us -> none
    all_to_all x2, waiting for transfers between devices: 31.1 us -> 6.46 us  [exchanged(): return lax.all_to_all(value, axes, split_axis=0, concat_axis=0, tiled=True)]
    ppermute x0 -> x5, waiting for transfers between devices: none -> 15.6 us  [swapped(): return lax.ppermute(value, axis, [(0, 1), (1, 0)])]
    pallas_call x0 -> x4, Pallas kernels: none -> 14.8 us  [the longest x1 5.29 us: add_halves(): pl.pallas_call(add_halves_kernel, grid_spec=pltpu.PrefetchScalarGridSpec(...]
    all_gather x1 -> x0, blocking collectives: 11.8 us -> none  [gather_in_order(): blocks = lax.all_gather(blocks, axes[k])]
  transfers between devices with their start and end apart: 5 -> 7, of which waited for: 5 -> 6; matrix products, arithmetic and copies ran while one was open for 0% -> 1% of each run, Pallas kernels for 0% -> 1%
where the time goes in v1:
time: 177 us; the launch traced here: 176 us
  blocking collectives  105 us (59%)
  waiting for transfers between devices  22 us (12%)
  starting transfers between devices  21 us (12%)
  Pallas kernels  14.8 us (8%)
  local copies, waits for them, and re-layouts  7.78 us (4%)
  other arithmetic  3.54 us (2%)
    all_to_all x4, blocking collectives, exchanged(): return lax.all_to_all(value, axes, split_axis=0, concat_axis=0, tiled=True)  105 us
    ppermute x5, waiting for transfers between devices, swapped(): return lax.ppermute(value, axis, [(0, 1), (1, 0)])  15.6 us
    ppermute x5, starting transfers between devices, swapped(): return lax.ppermute(value, axis, [(0, 1), (1, 0)])  10.8 us
    all_to_all x2, starting transfers between devices, exchanged(): return lax.all_to_all(value, axes, split_axis=0, concat_axis=0, tiled=True)  10.3 us
    all_to_all x2, waiting for transfers between devices, exchanged(): return lax.all_to_all(value, axes, split_axis=0, concat_axis=0, tiled=True)  6.46 us
    pallas_call x1, Pallas kernels, add_halves(): pl.pallas_call(add_halves_kernel, grid_spec=pltpu.PrefetchScalarGridSpec(...  5.29 us
    pallas_call x1, Pallas kernels, assemble(): pl.pallas_call(assemble_kernel, grid_spec=pltpu.PrefetchScalarGridSpec(nu...  4.54 us
    unnamed x22, local copies, waits for them, and re-layouts  4.4 us
  transfers between devices with their start and end apart: 7, of which 6 were waited for; matrix products, arithmetic and copies ran while one was open for 1% of the time, Pallas kernels for 1%

profile of v1, /device:TPU:1, one launch (start us, length us, event | category | flops | bytes accessed | tf_op | source)
XLA Modules:
  0.0 175.9 jit_solution(13600905149899824836)
XLA Ops:
  0.6 2.2 %dynamic-slice_bitcast_fusion = f32[3456,256]{1,0:T(8,128)S(1)} fusion(f32[1,1,3456,512]{3,2,1,0:T(8,128)} %param.5, s32[]{:T(128)S(6)} %select_n.3), kind=kLoop, calls=%fused_computation | loop fusion | bytes 7077892 | tf_op jit(solution)/shard_map/dynamic_slice | solution.py:150
  2.9 3.3 %collective-permute-start = (f32[3456,256]{1,0:T(8,128)S(1)}, f32[3456,256]{1,0:T(8,128)S(1)}, u32[]{:S(2)}, u32[]{:S(2)}) collective-permute-start(f32[3456,256]{1,0:T(8,128)S(1)} %dynamic-slice_bitcast_fusion), channel_id=1, source_target_pairs={{0,32},{32,0},{1,33},{33,1},{2,34},{34,2},{3,35},{35,3},{4,36},{36... | collective-permute-start | bytes 10616840 | tf_op jit(solution)/shard_map/ppermute | solution.py:142
  6.2 5.8 %collective-permute-done.theirs_ref = f32[3456,256]{1,0:T(8,128)S(1)} collective-permute-done((f32[3456,256]{1,0:T(8,128)S(1)}, f32[3456,256]{1,0:T(8,128)S(1)}, u32[]{:S(2)}, u32[]{:S(2)}) %collective-permute-start) | collective-permute-done | bytes 3538976 | tf_op jit(solution)/shard_map/ppermute | solution.py:142
  12.0 1.8 %copy-done.1 = f32[3456,256]{1,0:T(8,128)} copy-done((f32[3456,256]{1,0:T(8,128)}, f32[3456,256]{1,0:T(8,128)S(1)}, u32[]{:S(2)}) %copy-start.1) | copy-done | bytes 3538968
  13.8 5.3 %shard_map.84 = f32[4,4,448,128]{3,2,1,0:T(8,128)} custom-call(s32[1]{0:T(128)} %bitcast.1.c_ref, f32[3456,512]{1,0:T(8,128)} %bitcast.10, f32[3456,256]{1,0:T(8,128)} %copy-done.1), custom_call_target="tpu_custom_call" | custom-call | tf_op jit(solution)/shard_map/pallas_call | solution.py:31
  19.1 49.2 %all_to_all.30 = f32[16,448,128]{2,1,0:T(8,128)} all-to-all(f32[16,448,128]{2,1,0:T(8,128)} %bitcast.11), channel_id=1, replica_groups=mesh['y'=4,'c'=2,'x'=4,'zp'=4,'zl'=2] {'x','y'}, dimensions={0} | all-to-all | bytes 7340032 | tf_op jit(solution)/shard_map/all_to_all | solution.py:138
  68.3 2.3 %reduce_sum.18 = f32[448,128]{1,0:T(8,128)S(1)} reduce(f32[16,448,128]{2,1,0:T(8,128)} %all_to_all.30, f32[]{:T(128)} %constant.34.clone.1), dimensions={0}, to_apply=%region_0.0 | reduce | flops 860160 | bytes 3899396 | tf_op jit(solution)/shard_map/reduce_sum | solution.py:155
  70.6 17.0 %all_to_all.31 = f32[8,56,128]{2,1,0:T(8,128)S(1)} all-to-all(f32[8,56,128]{2,1,0:T(8,128)S(1)} %bitcast.14), channel_id=1, replica_groups=mesh['y'=4,'c'=2,'x'=4,'zp'=4,'zl'=2] {'zp','zl'}, dimensions={0} | all-to-all | bytes 458752 | tf_op jit(solution)/shard_map/all_to_all | solution.py:138
  87.7 0.8 broadcast_in_dim.6
  88.5 6.8 %all-to-all-start.2 = ((f32[16,56,128]{2,1,0:T(8,128)}), f32[16,56,128]{2,1,0:T(8,128)S(1)}, u32[]{:S(2)}, u32[]{:S(2)}) async-start(f32[16,56,128]{2,1,0:T(8,128)} %broadcast_in_dim.6), calls=%async_computation.2 | async-start | bytes 917504 | tf_op jit(solution)/shard_map/all_to_all | solution.py:138
  95.3 1.4 collective-permute-start.1
  96.7 0.1 collective-permute-start.2
  96.8 1.4 collective-permute-start.3
  98.9 0.6 pad_add_fusion.where_ref
  99.5 4.7 %all-to-all-done.2.parts_ref = f32[16,56,128]{2,1,0:T(8,128)S(1)} async-done(((f32[16,56,128]{2,1,0:T(8,128)}), f32[16,56,128]{2,1,0:T(8,128)S(1)}, u32[]{:S(2)}, u32[]{:S(2)}) %all-to-all-start.2) | async-done | bytes 458784 | tf_op jit(solution)/shard_map/all_to_all | solution.py:138
  104.2 0.8 copy-done.3
  105.0 1.8 %shard_map.85 = (f32[216,512]{1,0:T(8,128)}, f32[16,1,128]{2,1,0:T(1,128)}) custom-call(f32[16,56,128]{2,1,0:T(8,128)} %copy-done.3), custom_call_target="tpu_custom_call" | custom-call | tf_op jit(solution)/shard_map/pallas_call | solution.py:63
  106.8 3.5 %all-to-all-start.3 = ((f32[16,1,128]{2,1,0:T(1,128)}), f32[16,1,128]{2,1,0:T(1,128)S(1)}, u32[]{:S(2)}, u32[]{:S(2)}) async-start(f32[16,1,128]{2,1,0:T(1,128)} %get-tuple-element.11), calls=%async_computation.3 | async-start | bytes 16384 | tf_op jit(solution)/shard_map/all_to_all | solution.py:138
  110.3 0.6 pad_maximum_fusion.fixes_ref
  110.9 0.0 collective-permute-done.1.refs_1_
  110.9 1.3 collective-permute-done.2.refs_3_
  112.3 5.0 %collective-permute-done.3.refs_5_ = f32[108,512]{1,0:T(8,128)S(1)} collective-permute-done((f32[108,512]{1,0:T(8,128)S(1)}, f32[108,512]{1,0:T(8,128)S(1)}, u32[]{:S(2)}, u32[]{:S(2)}) %collective-permute-start.3) | collective-permute-done | bytes 221216 | tf_op jit(solution)/shard_map/ppermute | solution.py:142
  117.2 1.8 %all-to-all-done.3.totals_ref = f32[16,1,128]{2,1,0:T(1,128)S(1)} async-done(((f32[16,1,128]{2,1,0:T(1,128)}), f32[16,1,128]{2,1,0:T(1,128)S(1)}, u32[]{:S(2)}, u32[]{:S(2)}) %all-to-all-start.3) | async-done | bytes 8224 | tf_op jit(solution)/shard_map/all_to_all | solution.py:138
  119.0 0.6 copy-done.10
  119.6 3.1 %shard_map.86 = (f32[108,512]{1,0:T(8,128)}, f32[108,512]{1,0:T(8,128)}, f32[108,512]{1,0:T(8,128)}, bf16[4,112,128]{2,1,0:T(8,128)(2,1)}) custom-call(s32[3]{0:T(128)} %pad_add_fusion.where_ref, f32[2]{0:T(128)} %pad_maximum_fusion.fixes_ref, f32[216,512]{1,0:T(8,128)} %get-tuple-element.10.summed_ref, f32[16,1,128]{2,1,0:T(1,128)} %copy-done.10, ...), custom_call_target="tpu_custom_call" | custom-call | tf_op jit(solution)/shard_map/pallas_call | solution.py:104
  122.7 11.4 %all_to_all.32 = bf16[4,112,128]{2,1,0:T(8,128)(2,1)S(1)} all-to-all(bf16[4,112,128]{2,1,0:T(8,128)(2,1)} %get-tuple-element.15), channel_id=1, replica_groups=mesh['y'=4,'c'=2,'x'=4,'zp'=4,'zl'=2] {'zp'}, dimensions={0} | all-to-all | bytes 229376 | tf_op jit(solution)/shard_map/all_to_all | solution.py:138
  134.1 0.3 broadcast_in_dim.7
  134.5 27.6 %all_to_all.33 = bf16[16,4,112,128]{3,2,1,0:T(8,128)(2,1)S(1)} all-to-all(bf16[16,4,112,128]{3,2,1,0:T(8,128)(2,1)S(1)} %broadcast_in_dim.7), channel_id=1, replica_groups=mesh['y'=4,'c'=2,'x'=4,'zp'=4,'zl'=2] {'x','y'}, dimensions={0} | all-to-all | bytes 3670016 | tf_op jit(solution)/shard_map/all_to_all | solution.py:138
  162.1 4.6 %collective-permute-start.4 = (bf16[16,4,112,128]{3,2,1,0:T(8,128)(2,1)S(1)}, bf16[16,4,112,128]{3,2,1,0:T(8,128)(2,1)S(1)}, u32[]{:S(2)}, u32[]{:S(2)}) collective-permute-start(bf16[16,4,112,128]{3,2,1,0:T(8,128)(2,1)S(1)} %all_to_all.33), channel_id=1, source_target_pairs={{0,32},{32,0},{1,33},{33,1},{2,34},{34,2},{3,35},{35,3},{4,36},{36... | collective-permute-start | bytes 5505032 | tf_op jit(solution)/shard_map/ppermute | solution.py:142
  166.7 3.4 %collective-permute-done.4 = bf16[16,4,112,128]{3,2,1,0:T(8,128)(2,1)S(1)} collective-permute-done((bf16[16,4,112,128]{3,2,1,0:T(8,128)(2,1)S(1)}, bf16[16,4,112,128]{3,2,1,0:T(8,128)(2,1)S(1)}, u32[]{:S(2)}, u32[]{:S(2)}) %collective-permute-start.4) | collective-permute-done | bytes 1835040 | tf_op jit(solution)/shard_map/ppermute | solution.py:142
  170.1 1.2 copy-done.2
  171.3 4.5 %shard_map.87 = bf16[3456,512]{1,0:T(8,128)(2,1)} custom-call(s32[1]{0:T(128)} %bitcast.1.c_ref, bf16[4,4,4,112,128]{4,3,2,1,0:T(8,128)(2,1)} %bitcast.12, bf16[4,4,4,112,128]{4,3,2,1,0:T(8,128)(2,1)} %bitcast.13), custom_call_target="tpu_custom_call" | custom-call | tf_op jit(solution)/shard_map/pallas_call | solution.py:125
  (19 shorter events, 0.0 us)
Async XLA Ops:
  2.9 9.1 %collective-permute-start = (f32[3456,256]{1,0:T(8,128)S(1)}, f32[3456,256]{1,0:T(8,128)S(1)}, u32[]{:S(2)}, u32[]{:S(2)}) collective-permute-start(f32[3456,256]{1,0:T(8,128)S(1)} %dynamic-slice_bitcast_fusion), channel_id=1, source_target_pairs={{0,32},{32,0},{1,33},{33,1},{2,34},{34,2},{3,35},{35,3},{4,36},{36... | collective-permute-start | bytes 10616840 | tf_op jit(solution)/shard_map/ppermute | solution.py:142
  12.0 1.8 %copy-start.1 = (f32[3456,256]{1,0:T(8,128)}, f32[3456,256]{1,0:T(8,128)S(1)}, u32[]{:S(2)}) copy-start(f32[3456,256]{1,0:T(8,128)S(1)} %collective-permute-done.theirs_ref) | copy-start | bytes 10616836
  68.3 26.9 %copy-start.4 = (f32[108,512]{1,0:T(8,128)S(1)}, f32[108,512]{1,0:T(8,128)}, u32[]{:S(2)}) copy-start(f32[108,512]{1,0:T(8,128)} %refs_0_.1) | copy-start | bytes 663556
  68.3 28.4 %copy-start.5 = (f32[108,512]{1,0:T(8,128)S(1)}, f32[108,512]{1,0:T(8,128)}, u32[]{:S(2)}) copy-start(f32[108,512]{1,0:T(8,128)} %refs_2_.1) | copy-start | bytes 663556
  68.3 28.5 %copy-start.6 = (f32[108,512]{1,0:T(8,128)S(1)}, f32[108,512]{1,0:T(8,128)}, u32[]{:S(2)}) copy-start(f32[108,512]{1,0:T(8,128)} %refs_4_.1) | copy-start | bytes 663556
  88.5 15.8 %all-to-all-start.2 = ((f32[16,56,128]{2,1,0:T(8,128)}), f32[16,56,128]{2,1,0:T(8,128)S(1)}, u32[]{:S(2)}, u32[]{:S(2)}) async-start(f32[16,56,128]{2,1,0:T(8,128)} %broadcast_in_dim.6), calls=%async_computation.2 | async-start | bytes 917504 | tf_op jit(solution)/shard_map/all_to_all | solution.py:138
  95.3 15.6 %collective-permute-start.1 = (f32[108,512]{1,0:T(8,128)S(1)}, f32[108,512]{1,0:T(8,128)S(1)}, u32[]{:S(2)}, u32[]{:S(2)}) collective-permute-start(f32[108,512]{1,0:T(8,128)S(1)} %copy-done.4), channel_id=1, source_target_pairs={{0,1},{1,0},{2,3},{3,2},{4,5},{5,4},{6,7},{7,6},{8,9},{9,8},{10,11... | collective-permute-start | bytes 663560 | tf_op jit(solution)/shard_map/ppermute | solution.py:142
  96.7 15.5 %collective-permute-start.2 = (f32[108,512]{1,0:T(8,128)S(1)}, f32[108,512]{1,0:T(8,128)S(1)}, u32[]{:S(2)}, u32[]{:S(2)}) collective-permute-start(f32[108,512]{1,0:T(8,128)S(1)} %copy-done.5), channel_id=1, source_target_pairs={{0,1},{1,0},{2,3},{3,2},{4,5},{5,4},{6,7},{7,6},{8,9},{9,8},{10,11... | collective-permute-start | bytes 663560 | tf_op jit(solution)/shard_map/ppermute | solution.py:142
  96.8 20.4 %collective-permute-start.3 = (f32[108,512]{1,0:T(8,128)S(1)}, f32[108,512]{1,0:T(8,128)S(1)}, u32[]{:S(2)}, u32[]{:S(2)}) collective-permute-start(f32[108,512]{1,0:T(8,128)S(1)} %copy-done.6), channel_id=1, source_target_pairs={{0,1},{1,0},{2,3},{3,2},{4,5},{5,4},{6,7},{7,6},{8,9},{9,8},{10,11... | collective-permute-start | bytes 663560 | tf_op jit(solution)/shard_map/ppermute | solution.py:142
  104.2 0.8 copy-start.3
  106.8 12.2 %all-to-all-start.3 = ((f32[16,1,128]{2,1,0:T(1,128)}), f32[16,1,128]{2,1,0:T(1,128)S(1)}, u32[]{:S(2)}, u32[]{:S(2)}) async-start(f32[16,1,128]{2,1,0:T(1,128)} %get-tuple-element.11), calls=%async_computation.3 | async-start | bytes 16384 | tf_op jit(solution)/shard_map/all_to_all | solution.py:138
  110.9 8.1 %copy-start.7 = (f32[108,512]{1,0:T(8,128)}, f32[108,512]{1,0:T(8,128)S(1)}, u32[]{:S(2)}) copy-start(f32[108,512]{1,0:T(8,128)S(1)} %collective-permute-done.1.refs_1_) | copy-start | bytes 663556
  112.3 6.8 %copy-start.8 = (f32[108,512]{1,0:T(8,128)}, f32[108,512]{1,0:T(8,128)S(1)}, u32[]{:S(2)}) copy-start(f32[108,512]{1,0:T(8,128)S(1)} %collective-permute-done.2.refs_3_) | copy-start | bytes 663556
  117.2 1.8 %copy-start.9 = (f32[108,512]{1,0:T(8,128)}, f32[108,512]{1,0:T(8,128)S(1)}, u32[]{:S(2)}) copy-start(f32[108,512]{1,0:T(8,128)S(1)} %collective-permute-done.3.refs_5_) | copy-start | bytes 663556
  119.0 0.6 copy-start.10
  162.1 9.2 %copy-start = (bf16[16,4,112,128]{3,2,1,0:T(8,128)(2,1)}, bf16[16,4,112,128]{3,2,1,0:T(8,128)(2,1)S(1)}, u32[]{:S(2)}) copy-start(bf16[16,4,112,128]{3,2,1,0:T(8,128)(2,1)S(1)} %all_to_all.33) | copy-start | bytes 5505028
  162.1 8.0 %collective-permute-start.4 = (bf16[16,4,112,128]{3,2,1,0:T(8,128)(2,1)S(1)}, bf16[16,4,112,128]{3,2,1,0:T(8,128)(2,1)S(1)}, u32[]{:S(2)}, u32[]{:S(2)}) collective-permute-start(bf16[16,4,112,128]{3,2,1,0:T(8,128)(2,1)S(1)} %all_to_all.33), channel_id=1, source_target_pairs={{0,32},{32,0},{1,33},{33,1},{2,34},{34,2},{3,35},{35,3},{4,36},{36... | collective-permute-start | bytes 5505032 | tf_op jit(solution)/shard_map/ppermute | solution.py:142
  170.1 1.2 copy-start.2

commit v2 on v1

--- a/solution.py
+++ b/solution.py
@@ -14,33 +14,74 @@
 
 STARTS = (0, 56, 112, 160)
 PART = 56
+COLUMN = 8 * PART
 HALF_STARTS = (0, 104)
 HALF = 112
-
-
-def add_halves_kernel(c_ref, mine_ref, theirs_ref, out_ref):
-    for zp in range(4):
-        for zl in range(2):
-            for y in range(4):
-                rows = pl.ds(zp * 216 + STARTS[y], PART)
-                cols = pl.ds(zl * 128, 128)
-                out_ref[0, y, pl.ds((zp * 2 + zl) * PART, PART), :] = mine_ref[rows, cols] + theirs_ref[rows, cols]
+LIMIT = pltpu.CompilerParams(vmem_limit_bytes=24 * 2**20)
+
+
+def add_halves_kernel(c_ref, mine_ref, theirs_ref, out_ref, sums):
+    base = pl.program_id(0) * 864
+    for y in range(4):
+        peak = jnp.zeros((8, 128), jnp.float32)
+        for z in range(8):
+            start = (z // 2) * 216 + STARTS[y]
+            cols = pl.ds((z % 2) * 128, 128)
+            for t in range(0, PART, 8):
+                rows = pl.ds(start + t, 8)
+                value = mine_ref[rows, cols] + theirs_ref[pl.ds(base + start + t, 8), cols]
+                peak = jnp.maximum(peak, jnp.abs(value))
+                sums[pl.ds(z * PART + t, 8), :] = value
+        peak = jnp.max(peak, axis=0, keepdims=True)
+        level = jnp.maximum(jnp.ceil(4.0 * jnp.log2(peak) + 0.02), -400.0)
+        inverse = 32767.0 * jnp.exp2(-0.25 * level)
+        for t in range(0, COLUMN, PART):
+            scaled = jnp.round(sums[pl.ds(t, PART), :] * inverse)
+            out_ref[0, y, pl.ds(t, PART), :] = scaled.astype(jnp.int32).astype(jnp.int16)
+        level = jnp.broadcast_to(level, (8, 128))
+        out_ref[0, y, pl.ds(COLUMN, 8), :] = level.astype(jnp.int32).astype(jnp.int16)
 
 
 def add_halves(c, local, theirs):
     return pl.pallas_call(
         add_halves_kernel,
+        compiler_params=LIMIT,
         grid_spec=pltpu.PrefetchScalarGridSpec(
             num_scalar_prefetch=1,
             grid=(4,),
             in_specs=[
                 pl.BlockSpec((864, 256), lambda i, c: (i, c[0])),
-                pl.BlockSpec((864, 256), lambda i, c: (i, 0)),
+                pl.BlockSpec(memory_space=pltpu.VMEM),
             ],
-            out_specs=pl.BlockSpec((1, 4, 8 * PART, 128), lambda i, c: (i, 0, 0, 0)),
+            out_specs=pl.BlockSpec((1, 4, COLUMN + 8, 128), lambda i, c: (i, 0, 0, 0)),
+            scratch_shapes=[pltpu.VMEM((COLUMN, 128), jnp.float32)],
         ),
-        out_shape=jax.ShapeDtypeStruct((4, 4, 8 * PART, 128), jnp.float32),
-    )(c, local, theirs)
+        out_shape=jax.ShapeDtypeStruct((4, 4, COLUMN + 8, 128), jnp.int16),
+    )(c, local, in_vmem(theirs))
+
+
+def sum_plane_kernel(coded_ref, out_ref):
+    scales = []
+    for k in range(16):
+        level = coded_ref[k, pl.ds(COLUMN, 8), :].astype(jnp.int32).astype(jnp.float32)
+        scales.append(jnp.exp2(0.25 * level) * (1.0 / 32767.0))
+    for z in range(8):
+        rows = pl.ds(z * PART, PART)
+        total = jnp.zeros((PART // 8, 8, 128), jnp.float32)
+        for k in range(16):
+            value = coded_ref[k, rows, :].astype(jnp.int32).astype(jnp.float32)
+            total = total + value.reshape(PART // 8, 8, 128) * scales[k]
+        out_ref[z] = total.reshape(PART, 128)
+
+
+def sum_plane(coded):
+    return pl.pallas_call(
+        sum_plane_kernel,
+        compiler_params=LIMIT,
+        in_specs=[pl.BlockSpec(memory_space=pltpu.VMEM)],
+        out_specs=pl.BlockSpec(memory_space=pltpu.VMEM),
+        out_shape=jax.ShapeDtypeStruct((8, PART, 128), jnp.float32),
+    )(in_vmem(coded))
 
 
 def place_pair(buf, parts_ref):
@@ -60,13 +101,17 @@
 
 
 def squares(parts):
+    vmem = pl.BlockSpec(memory_space=pltpu.VMEM)
     return pl.pallas_call(
         squares_kernel,
+        compiler_params=LIMIT,
+        in_specs=[vmem],
+        out_specs=(vmem, vmem),
         out_shape=(
             jax.ShapeDtypeStruct((216, 512), jnp.float32),
-            jax.ShapeDtypeStruct((16, 1, 128), jnp.float32),
+            jax.ShapeDtypeStruct((16, 8, 128), jnp.float32),
         ),
-    )(parts)
+    )(in_vmem(parts))
 
 
 def adam_kernel(where_ref, fixes_ref, summed_ref, totals_ref, *refs):
@@ -76,7 +121,7 @@
     for buf, own, other in ((w, w_own, w_other), (a, a_own, a_other), (b, b_own, b_other)):
         buf[pl.ds(0, 108), :] = jnp.where(first, own[...], other[...])
         buf[pl.ds(108, 108), :] = jnp.where(first, other[...], own[...])
-    total = jnp.sum(totals_ref[...], axis=0)
+    total = jnp.sum(totals_ref[...], axis=0)[:1]
     norm = jnp.sqrt(total)
     clip = jnp.minimum(jnp.float32(1.0), 1.0 / (norm + 1e-06))
     clip = clip[:, :1]
@@ -103,35 +148,42 @@
     rows = jax.ShapeDtypeStruct((108, 512), jnp.float32)
     return pl.pallas_call(
         adam_kernel,
+        compiler_params=LIMIT,
         in_specs=[smem, smem] + [vmem] * 8,
         out_shape=(rows, rows, rows, jax.ShapeDtypeStruct((4, HALF, 128), jnp.bfloat16)),
         scratch_shapes=[pltpu.VMEM((216, 512), jnp.float32)] * 3,
-    )(where, fixes, summed, totals, *states)
+    )(where, fixes, in_vmem(summed), in_vmem(totals), *map(in_vmem, states))
 
 
 def assemble_kernel(c_ref, mine_ref, theirs_ref, out_ref):
+    x = pl.program_id(0)
     first = c_ref[0] == 0
     for zp in range(4):
         for y in range(4):
+            mine, theirs = mine_ref[x * 4 + y, zp], theirs_ref[x * 4 + y, zp]
+            cols = pl.ds(y * 128, 128)
             for half in range(2):
                 rows = pl.ds(zp * 216 + HALF_STARTS[half], HALF)
-                mine, theirs = mine_ref[0, y, zp], theirs_ref[0, y, zp]
-                value = jnp.where(first == (half == 0), mine, theirs)
-                out_ref[rows, pl.ds(y * 128, 128)] = value
+                out_ref[rows, cols] = jnp.where(first == (half == 0), mine, theirs)
 
 
 def assemble(c, mine, theirs):
-    block = pl.BlockSpec((1, 4, 4, HALF, 128), lambda i, c: (i, 0, 0, 0, 0))
+    vmem = pl.BlockSpec(memory_space=pltpu.VMEM)
     return pl.pallas_call(
         assemble_kernel,
+        compiler_params=LIMIT,
         grid_spec=pltpu.PrefetchScalarGridSpec(
             num_scalar_prefetch=1,
             grid=(4,),
-            in_specs=[block, block],
+            in_specs=[vmem, vmem],
             out_specs=pl.BlockSpec((864, 512), lambda i, c: (i, 0)),
         ),
         out_shape=jax.ShapeDtypeStruct((3456, 512), jnp.bfloat16),
-    )(c, mine, theirs)
+    )(c, in_vmem(mine), in_vmem(theirs))
+
+
+def in_vmem(value):
+    return pltpu.with_memory_space_constraint(value, pltpu.VMEM)
 
 
 def exchanged(value, axes):
@@ -151,9 +203,9 @@
     states = []
     for own in (master, moment_one, moment_two):
         states += [own, swapped(own, "zl")]
-    chunks = add_halves(side, local, theirs).reshape(16, 8 * PART, 128)
-    columns = exchanged(chunks, PLANE).sum(axis=0)
-    part = exchanged(columns.reshape(8, PART, 128), ("zp", "zl")).sum(axis=0)
+    coded = exchanged(add_halves(side, local, theirs).reshape(16, COLUMN + 8, 128), PLANE)
+    coded, states = lax.optimization_barrier((coded, states))
+    part = exchanged(sum_plane(coded), ("zp", "zl")).sum(axis=0)
     parts = exchanged(jnp.broadcast_to(part, (16, PART, 128)), PAIR)
     summed, total = squares(parts)
     totals = exchanged(total, PAIRS)
@@ -164,8 +216,7 @@
     column = exchanged(sent, "zp")
     mine = exchanged(jnp.broadcast_to(column, (16, *column.shape)), PLANE)
     other = swapped(mine, "c")
-    grouped = (4, 4, 4, HALF, 128)
-    weights = assemble(side, mine.reshape(grouped), other.reshape(grouped))
+    weights = assemble(side, mine, other)
     return (new_master, new_one, new_two, weights)
 
 

time: 177 us -> 142 us (0.80)
  blocking collectives: 105 us -> 51.9 us
  waiting for transfers between devices: 22 us -> 49.6 us
  Pallas kernels: 14.8 us -> 8.57 us
  starting transfers between devices: 21 us -> 26.7 us
  local copies, waits for them, and re-layouts: 7.78 us -> 3.55 us
  other arithmetic: 3.54 us -> 0.17 us
    all_to_all x4 -> x3, blocking collectives: 105 us -> 51.9 us  [exchanged(): return lax.all_to_all(value, axes, split_axis=0, concat_axis=0, tiled=True)]
    all_to_all x2 -> x3, waiting for transfers between devices: 6.46 us -> 26.8 us  [exchanged(): return lax.all_to_all(value, axes, split_axis=0, concat_axis=0, tiled=True)]
    ppermute x5, waiting for transfers between devices: 15.6 us -> 22.8 us  [swapped(): return lax.ppermute(value, axis, [(0, 1), (1, 0)])]
    pallas_call x4 -> x5, Pallas kernels: 14.8 us -> 8.57 us  [the longest x1 2.69 us: add_halves(): pl.pallas_call(add_halves_kernel, compiler_params=LIMIT, grid_spec=pltpu....]
    all_to_all x2 -> x3, starting transfers between devices: 10.3 us -> 15.9 us  [exchanged(): return lax.all_to_all(value, axes, split_axis=0, concat_axis=0, tiled=True)]
    unnamed x22 -> x8, local copies, waits for them, and re-layouts: 4.4 us -> 0.02 us
    reduce_sum x2 -> x1, other arithmetic: 2.31 us -> 0.02 us  [shards(): part = exchanged(sum_plane(coded), ('zp', 'zl')).sum(axis=0)]
  transfers between devices with their start and end apart: 7 -> 8, of which waited for: 6 -> 8; matrix products, arithmetic and copies ran while one was open for 1% -> 0% of each run, Pallas kernels for 1% -> 0%
where the time goes in v2:
time: 142 us
  blocking collectives  51.9 us (37%)
  waiting for transfers between devices  49.6 us (35%)
  starting transfers between devices  26.7 us (19%)
  Pallas kernels  8.57 us (6%)
  local copies, waits for them, and re-layouts  3.55 us (2%)
  between operations  1.44 us (1%)
    all_to_all x3, blocking collectives, exchanged(): return lax.all_to_all(value, axes, split_axis=0, concat_axis=0, tiled=True)  51.9 us
    all_to_all x3, waiting for transfers between devices, exchanged(): return lax.all_to_all(value, axes, split_axis=0, concat_axis=0, tiled=True)  26.8 us
    ppermute x5, waiting for transfers between devices, swapped(): return lax.ppermute(value, axis, [(0, 1), (1, 0)])  22.8 us
    all_to_all x3, starting transfers between devices, exchanged(): return lax.all_to_all(value, axes, split_axis=0, concat_axis=0, tiled=True)  15.9 us
    ppermute x5, starting transfers between devices, swapped(): return lax.ppermute(value, axis, [(0, 1), (1, 0)])  10.8 us
  transfers between devices with their start and end apart: 8, of which 8 were waited for; matrix products, arithmetic and copies ran while one was open for 0% of the time, Pallas kernels for 0%

profile of v2, /device:TPU:1, one launch (start us, length us, event | category | flops | bytes accessed | tf_op | source)
XLA Modules:
  0.0 141.9 jit_solution(11578369130848026257)
XLA Ops:
  0.6 0.0 copy-start
  0.6 2.4 %dynamic-slice_bitcast_fusion = f32[3456,256]{1,0:T(8,128)S(1)} fusion(f32[1,1,3456,512]{3,2,1,0:T(8,128)} %param.5, s32[]{:T(128)S(6)} %select_n.3), kind=kLoop, calls=%fused_computation | loop fusion | bytes 7077892 | tf_op jit(solution)/shard_map/dynamic_slice | solution.py:202
  3.0 3.3 %collective-permute-start = (f32[3456,256]{1,0:T(8,128)S(1)}, f32[3456,256]{1,0:T(8,128)S(1)}, u32[]{:S(2)}, u32[]{:S(2)}) collective-permute-start(f32[3456,256]{1,0:T(8,128)S(1)} %dynamic-slice_bitcast_fusion), channel_id=1, source_target_pairs={{0,32},{32,0},{1,33},{33,1},{2,34},{34,2},{3,35},{35,3},{4,36},{36... | collective-permute-start | bytes 10616840 | tf_op jit(solution)/shard_map/ppermute | solution.py:194
  6.3 5.8 %collective-permute-done.theirs_ref = f32[3456,256]{1,0:T(8,128)S(1)} collective-permute-done((f32[3456,256]{1,0:T(8,128)S(1)}, f32[3456,256]{1,0:T(8,128)S(1)}, u32[]{:S(2)}, u32[]{:S(2)}) %collective-permute-start) | collective-permute-done | bytes 3538976 | tf_op jit(solution)/shard_map/ppermute | solution.py:194
  12.2 0.0 copy-done
  12.2 2.7 %shard_map.84 = s16[4,4,456,128]{3,2,1,0:T(8,128)(2,1)} custom-call(s32[1]{0:T(128)} %bitcast.1.c_ref, f32[3456,512]{1,0:T(8,128)S(1)} %bitcast.7, f32[3456,256]{1,0:T(8,128)S(1)} %collective-permute-done.theirs_ref), custom_call_target="tpu_custom_call" | custom-call | tf_op jit(solution)/shard_map/pallas_call | solution.py:46
  14.9 5.2 %all-to-all-start = ((s16[16,456,128]{2,1,0:T(8,128)(2,1)}), s16[16,456,128]{2,1,0:T(8,128)(2,1)S(1)}, u32[]{:S(2)}, u32[]{:S(2)}) async-start(s16[16,456,128]{2,1,0:T(8,128)(2,1)} %bitcast.5), calls=%async_computation | async-start | bytes 3735552 | tf_op jit(solution)/shard_map/all_to_all | solution.py:190
  20.1 0.0 copy-done.1
  20.1 1.7 %collective-permute-start.1 = (f32[108,512]{1,0:T(8,128)S(1)}, f32[108,512]{1,0:T(8,128)S(1)}, u32[]{:S(2)}, u32[]{:S(2)}) collective-permute-start(f32[108,512]{1,0:T(8,128)S(1)} %copy-done.1), channel_id=1, source_target_pairs={{0,1},{1,0},{2,3},{3,2},{4,5},{5,4},{6,7},{7,6},{8,9},{9,8},{10,11... | collective-permute-start | bytes 663560 | tf_op jit(solution)/shard_map/ppermute | solution.py:194
  21.8 0.1 collective-permute-start.2
  21.9 1.4 collective-permute-start.3
  23.3 3.8 %collective-permute-done.1.refs_1_ = f32[108,512]{1,0:T(8,128)S(1)} collective-permute-done((f32[108,512]{1,0:T(8,128)S(1)}, f32[108,512]{1,0:T(8,128)S(1)}, u32[]{:S(2)}, u32[]{:S(2)}) %collective-permute-start.1) | collective-permute-done | bytes 221216 | tf_op jit(solution)/shard_map/ppermute | solution.py:194
  27.0 4.9 %collective-permute-done.2.refs_3_ = f32[108,512]{1,0:T(8,128)S(1)} collective-permute-done((f32[108,512]{1,0:T(8,128)S(1)}, f32[108,512]{1,0:T(8,128)S(1)}, u32[]{:S(2)}, u32[]{:S(2)}) %collective-permute-start.2) | collective-permute-done | bytes 221216 | tf_op jit(solution)/shard_map/ppermute | solution.py:194
  31.9 4.9 %collective-permute-done.3.refs_5_ = f32[108,512]{1,0:T(8,128)S(1)} collective-permute-done((f32[108,512]{1,0:T(8,128)S(1)}, f32[108,512]{1,0:T(8,128)S(1)}, u32[]{:S(2)}, u32[]{:S(2)}) %collective-permute-start.3) | collective-permute-done | bytes 221216 | tf_op jit(solution)/shard_map/ppermute | solution.py:194
  36.9 9.5 %all-to-all-done.coded_ref = s16[16,456,128]{2,1,0:T(8,128)(2,1)S(1)} async-done(((s16[16,456,128]{2,1,0:T(8,128)(2,1)}), s16[16,456,128]{2,1,0:T(8,128)(2,1)S(1)}, u32[]{:S(2)}, u32[]{:S(2)}) %all-to-all-start) | async-done | bytes 1867808 | tf_op jit(solution)/shard_map/all_to_all | solution.py:190
  46.4 0.5 shard_map.85
  46.9 17.0 %all_to_all.30 = f32[8,56,128]{2,1,0:T(8,128)S(1)} all-to-all(f32[8,56,128]{2,1,0:T(8,128)S(1)} %shard_map.85), channel_id=1, replica_groups=mesh['y'=4,'c'=2,'x'=4,'zp'=4,'zl'=2] {'zp','zl'}, dimensions={0} | all-to-all | bytes 458752 | tf_op jit(solution)/shard_map/all_to_all | solution.py:190
  63.9 0.8 broadcast_in_dim.6
  64.7 7.2 %all-to-all-start.2 = ((f32[16,56,128]{2,1,0:T(8,128)}), f32[16,56,128]{2,1,0:T(8,128)S(1)}, u32[]{:S(2)}, u32[]{:S(2)}) async-start(f32[16,56,128]{2,1,0:T(8,128)} %broadcast_in_dim.6), calls=%async_computation.2 | async-start | bytes 917504 | tf_op jit(solution)/shard_map/all_to_all | solution.py:190
  72.6 8.2 %all-to-all-done.2.parts_ref = f32[16,56,128]{2,1,0:T(8,128)S(1)} async-done(((f32[16,56,128]{2,1,0:T(8,128)}), f32[16,56,128]{2,1,0:T(8,128)S(1)}, u32[]{:S(2)}, u32[]{:S(2)}) %all-to-all-start.2) | async-done | bytes 458784 | tf_op jit(solution)/shard_map/all_to_all | solution.py:190
  80.9 0.8 shard_map.86
  81.7 3.5 %all-to-all-start.3 = ((f32[16,8,128]{2,1,0:T(8,128)}), f32[16,8,128]{2,1,0:T(8,128)S(1)}, u32[]{:S(2)}, u32[]{:S(2)}) async-start(f32[16,8,128]{2,1,0:T(8,128)} %get-tuple-element.19), calls=%async_computation.3 | async-start | bytes 131072 | tf_op jit(solution)/shard_map/all_to_all | solution.py:190
  85.2 0.1 pad_maximum_fusion.fixes_ref
  85.3 0.1 pad_add_fusion.where_ref
  85.3 9.1 %all-to-all-done.3.totals_ref = f32[16,8,128]{2,1,0:T(8,128)S(1)} async-done(((f32[16,8,128]{2,1,0:T(8,128)}), f32[16,8,128]{2,1,0:T(8,128)S(1)}, u32[]{:S(2)}, u32[]{:S(2)}) %all-to-all-start.3) | async-done | bytes 65568 | tf_op jit(solution)/shard_map/all_to_all | solution.py:190
  94.4 2.1 %shard_map.87 = (f32[108,512]{1,0:T(8,128)}, f32[108,512]{1,0:T(8,128)}, f32[108,512]{1,0:T(8,128)}, bf16[4,112,128]{2,1,0:T(8,128)(2,1)S(1)}) custom-call(s32[3]{0:T(128)S(1)} %pad_add_fusion.where_ref, f32[2]{0:T(128)S(1)} %pad_maximum_fusion.fixes_ref, f32[216,512]{1,0:T(8,128)S(1)} %get-tuple-element.18.summed_ref, ...), custom_call_target="tpu_custom_call" | custom-call | tf_op jit(solution)/shard_map/pallas_call | solution.py:149
  96.5 9.8 %all_to_all.31 = bf16[4,112,128]{2,1,0:T(8,128)(2,1)S(1)} all-to-all(bf16[4,112,128]{2,1,0:T(8,128)(2,1)S(1)} %get-tuple-element.29), channel_id=1, replica_groups=mesh['y'=4,'c'=2,'x'=4,'zp'=4,'zl'=2] {'zp'}, dimensions={0} | all-to-all | bytes 229376 | tf_op jit(solution)/shard_map/all_to_all | solution.py:190
  106.3 0.3 broadcast_in_dim.7
  106.7 25.1 %all_to_all.32.mine_ref = bf16[16,4,112,128]{3,2,1,0:T(8,128)(2,1)S(1)} all-to-all(bf16[16,4,112,128]{3,2,1,0:T(8,128)(2,1)S(1)} %broadcast_in_dim.7), channel_id=1, replica_groups=mesh['y'=4,'c'=2,'x'=4,'zp'=4,'zl'=2] {'x','y'}, dimensions={0} | all-to-all | bytes 3670016 | tf_op jit(solution)/shard_map/all_to_all | solution.py:190
  131.7 4.3 %collective-permute-start.4 = (bf16[16,4,112,128]{3,2,1,0:T(8,128)(2,1)S(1)}, bf16[16,4,112,128]{3,2,1,0:T(8,128)(2,1)S(1)}, u32[]{:S(2)}, u32[]{:S(2)}) collective-permute-start(bf16[16,4,112,128]{3,2,1,0:T(8,128)(2,1)S(1)} %all_to_all.32.mine_ref), channel_id=1, source_target_pairs={{0,32},{32,0},{1,33},{33,1},{2,34},{34,2},{3,35},{35,3},{4,36},{36... | collective-permute-start | bytes 5505032 | tf_op jit(solution)/shard_map/ppermute | solution.py:194
  136.1 3.4 %collective-permute-done.4.theirs_ref = bf16[16,4,112,128]{3,2,1,0:T(8,128)(2,1)S(1)} collective-permute-done((bf16[16,4,112,128]{3,2,1,0:T(8,128)(2,1)S(1)}, bf16[16,4,112,128]{3,2,1,0:T(8,128)(2,1)S(1)}, u32[]{:S(2)}, u32[]{:S(2)}) %collective-permute-start.4) | collective-permute-done | bytes 1835040 | tf_op jit(solution)/shard_map/ppermute | solution.py:194
  139.5 2.4 %shard_map.88 = bf16[3456,512]{1,0:T(8,128)(2,1)} custom-call(s32[1]{0:T(128)} %bitcast.1.c_ref, bf16[16,4,112,128]{3,2,1,0:T(8,128)(2,1)S(1)} %all_to_all.32.mine_ref, bf16[16,4,112,128]{3,2,1,0:T(8,128)(2,1)S(1)} %collective-permute-done.4.theirs_ref), custom_call_target="tpu_custom_call" | custom-call | tf_op jit(solution)/shard_map/pallas_call | solution.py:172
  (6 shorter events, 0.0 us)
Async XLA Ops:
  0.6 11.5 %copy-start = (f32[1,1,3456,512]{3,2,1,0:T(8,128)S(1)}, f32[1,1,3456,512]{3,2,1,0:T(8,128)}, u32[]{:S(2)}) copy-start(f32[1,1,3456,512]{3,2,1,0:T(8,128)} %param.5) | copy-start | bytes 21233668
  3.0 9.1 %collective-permute-start = (f32[3456,256]{1,0:T(8,128)S(1)}, f32[3456,256]{1,0:T(8,128)S(1)}, u32[]{:S(2)}, u32[]{:S(2)}) collective-permute-start(f32[3456,256]{1,0:T(8,128)S(1)} %dynamic-slice_bitcast_fusion), channel_id=1, source_target_pairs={{0,32},{32,0},{1,33},{33,1},{2,34},{34,2},{3,35},{35,3},{4,36},{36... | collective-permute-start | bytes 10616840 | tf_op jit(solution)/shard_map/ppermute | solution.py:194
  14.9 5.2 %copy-start.1 = (f32[108,512]{1,0:T(8,128)S(1)}, f32[108,512]{1,0:T(8,128)}, u32[]{:S(2)}) copy-start(f32[108,512]{1,0:T(8,128)} %refs_0_) | copy-start | bytes 663556
  14.9 6.9 %copy-start.2 = (f32[108,512]{1,0:T(8,128)S(1)}, f32[108,512]{1,0:T(8,128)}, u32[]{:S(2)}) copy-start(f32[108,512]{1,0:T(8,128)} %refs_2_) | copy-start | bytes 663556
  14.9 7.0 %copy-start.3 = (f32[108,512]{1,0:T(8,128)S(1)}, f32[108,512]{1,0:T(8,128)}, u32[]{:S(2)}) copy-start(f32[108,512]{1,0:T(8,128)} %refs_4_) | copy-start | bytes 663556
  14.9 31.5 %all-to-all-start = ((s16[16,456,128]{2,1,0:T(8,128)(2,1)}), s16[16,456,128]{2,1,0:T(8,128)(2,1)S(1)}, u32[]{:S(2)}, u32[]{:S(2)}) async-start(s16[16,456,128]{2,1,0:T(8,128)(2,1)} %bitcast.5), calls=%async_computation | async-start | bytes 3735552 | tf_op jit(solution)/shard_map/all_to_all | solution.py:190
  20.1 7.0 %collective-permute-start.1 = (f32[108,512]{1,0:T(8,128)S(1)}, f32[108,512]{1,0:T(8,128)S(1)}, u32[]{:S(2)}, u32[]{:S(2)}) collective-permute-start(f32[108,512]{1,0:T(8,128)S(1)} %copy-done.1), channel_id=1, source_target_pairs={{0,1},{1,0},{2,3},{3,2},{4,5},{5,4},{6,7},{7,6},{8,9},{9,8},{10,11... | collective-permute-start | bytes 663560 | tf_op jit(solution)/shard_map/ppermute | solution.py:194
  21.8 10.1 %collective-permute-start.2 = (f32[108,512]{1,0:T(8,128)S(1)}, f32[108,512]{1,0:T(8,128)S(1)}, u32[]{:S(2)}, u32[]{:S(2)}) collective-permute-start(f32[108,512]{1,0:T(8,128)S(1)} %copy-done.2), channel_id=1, source_target_pairs={{0,1},{1,0},{2,3},{3,2},{4,5},{5,4},{6,7},{7,6},{8,9},{9,8},{10,11... | collective-permute-start | bytes 663560 | tf_op jit(solution)/shard_map/ppermute | solution.py:194
  21.9 14.9 %collective-permute-start.3 = (f32[108,512]{1,0:T(8,128)S(1)}, f32[108,512]{1,0:T(8,128)S(1)}, u32[]{:S(2)}, u32[]{:S(2)}) collective-permute-start(f32[108,512]{1,0:T(8,128)S(1)} %copy-done.3), channel_id=1, source_target_pairs={{0,1},{1,0},{2,3},{3,2},{4,5},{5,4},{6,7},{7,6},{8,9},{9,8},{10,11... | collective-permute-start | bytes 663560 | tf_op jit(solution)/shard_map/ppermute | solution.py:194
  64.7 16.2 %all-to-all-start.2 = ((f32[16,56,128]{2,1,0:T(8,128)}), f32[16,56,128]{2,1,0:T(8,128)S(1)}, u32[]{:S(2)}, u32[]{:S(2)}) async-start(f32[16,56,128]{2,1,0:T(8,128)} %broadcast_in_dim.6), calls=%async_computation.2 | async-start | bytes 917504 | tf_op jit(solution)/shard_map/all_to_all | solution.py:190
  81.7 12.7 %all-to-all-start.3 = ((f32[16,8,128]{2,1,0:T(8,128)}), f32[16,8,128]{2,1,0:T(8,128)S(1)}, u32[]{:S(2)}, u32[]{:S(2)}) async-start(f32[16,8,128]{2,1,0:T(8,128)} %get-tuple-element.19), calls=%async_computation.3 | async-start | bytes 131072 | tf_op jit(solution)/shard_map/all_to_all | solution.py:190
  131.7 7.7 %collective-permute-start.4 = (bf16[16,4,112,128]{3,2,1,0:T(8,128)(2,1)S(1)}, bf16[16,4,112,128]{3,2,1,0:T(8,128)(2,1)S(1)}, u32[]{:S(2)}, u32[]{:S(2)}) collective-permute-start(bf16[16,4,112,128]{3,2,1,0:T(8,128)(2,1)S(1)} %all_to_all.32.mine_ref), channel_id=1, source_target_pairs={{0,32},{32,0},{1,33},{33,1},{2,34},{34,2},{3,35},{35,3},{4,36},{36... | collective-permute-start | bytes 5505032 | tf_op jit(solution)/shard_map/ppermute | solution.py:194

commit v3 on v0

v3 whole, which is shorter than its diff:
```python
import jax
import jax.numpy as jnp
from jax import lax
from jax.experimental import pallas as pl
from jax.experimental.pallas import tpu as pltpu
from jax.sharding import Mesh
from jax.sharding import PartitionSpec as P

GRP = ("y", "c")
SHARD = ("x", "z")
PLANE = ("x", "y")

PART = 56
STARTS = (0, 52)
SHARED = 4
CUTS = ((0, PART),)
LIMIT = pltpu.CompilerParams(vmem_limit_bytes=24 * 2**20)
VMEM = pl.BlockSpec(memory_space=pltpu.VMEM)
SMEM = pl.BlockSpec(memory_space=pltpu.SMEM)


def in_vmem(value):
    return pltpu.with_memory_space_constraint(value, pltpu.VMEM)


def exchanged(value, axes):
    return lax.all_to_all(value, axes, split_axis=0, concat_axis=0, tiled=True)


def swapped(value, axis):
    return lax.ppermute(value, axis, [(0, 1), (1, 0)])


def rotated(value, axis):
    n = lax.axis_size(axis)
    return [value] + [lax.ppermute(value, axis, [(i, (i + k) % n) for i in range(n)]) for k in range(1, n)]


def code_sums(c, local, theirs, cut):
    first, length = cut
    column = 8 * length

    def kernel(c_ref, mine_ref, theirs_ref, out_ref, sums):
        for y in range(4):
            cols = pl.ds((y // 2) * 128, 128)
            peak = jnp.zeros((8, 128), jnp.float32)
            for z in range(8):
                start = 108 * z + STARTS[y % 2] + first
                for t in range(0, length, 8):
                    rows = pl.ds(start + t, 8)
                    value = mine_ref[rows, cols] + theirs_ref[rows, cols]
                    peak = jnp.maximum(peak, jnp.abs(value))
                    sums[pl.ds(z * length + t, 8), :] = value
            peak = jnp.max(peak, axis=0, keepdims=True)
            level = jnp.maximum(jnp.ceil(4.0 * jnp.log2(peak) + 0.02), -400.0)
            inverse = 32767.0 * jnp.exp2(-0.25 * level)
            for t in range(0, column, length):
                scaled = jnp.round(sums[pl.ds(t, length), :] * inverse)
                out_ref[0, y, pl.ds(t, length), :] = scaled.astype(jnp.int32).astype(jnp.int16)
            level = jnp.broadcast_to(level, (8, 128))
            out_ref[0, y, pl.ds(column, 8), :] = level.astype(jnp.int32).astype(jnp.int16)

    coded = pl.pallas_call(
        kernel,
        compiler_params=LIMIT,
        grid_spec=pltpu.PrefetchScalarGridSpec(
            num_scalar_prefetch=1,
            grid=(4,),
            in_specs=[
                pl.BlockSpec((864, 256), lambda i, c: (i, c[0])),
                pl.BlockSpec((864, 256), lambda i, c: (i, 0)),
            ],
            out_specs=pl.BlockSpec((1, 4, column + 8, 128), lambda i, c: (i, 0, 0, 0)),
            scratch_shapes=[pltpu.VMEM((column, 128), jnp.float32)],
        ),
        out_shape=jax.ShapeDtypeStruct((4, 4, column + 8, 128), jnp.int16),
    )(c, local, in_vmem(theirs))
    return coded.reshape(16, column + 8, 128)


def sum_coded(coded, cut):
    length = cut[1]
    column = 8 * length

    def kernel(coded_ref, out_ref):
        scales = []
        for k in range(16):
            level = coded_ref[k, pl.ds(column, 8), :].astype(jnp.int32).astype(jnp.float32)
            scales.append(jnp.exp2(0.25 * level) * (1.0 / 32767.0))
        for z in range(8):
            rows = pl.ds(z * length, length)
            total = jnp.zeros((length // 8, 8, 128), jnp.float32)
            for k in range(16):
                value = coded_ref[k, rows, :].astype(jnp.int32).astype(jnp.float32)
                total = total + value.reshape(length // 8, 8, 128) * scales[k]
            out_ref[z] = total.reshape(length, 128)

    return pl.pallas_call(
        kernel,
        compiler_params=LIMIT,
        in_specs=[VMEM],
        out_specs=VMEM,
        out_shape=jax.ShapeDtypeStruct((8, length, 128), jnp.float32),
    )(in_vmem(coded))


def part_kernel(where_ref, *refs):
    *cut_refs, out_ref, part_ref = refs
    for ref, (first, length) in zip(cut_refs, CUTS):
        total = ref[0]
        for k in range(1, 8):
            total = total + ref[k]
        part_ref[pl.ds(first, length), :] = total
    part = part_ref[...]
    row = lax.broadcasted_iota(jnp.int32, part.shape, 0)
    counted = (row >= SHARED) | (where_ref[0] % 2 == 0)
    total = jnp.sum(jnp.where(counted, part * part, 0.0))
    for k in range(8):
        out_ref[k, pl.ds(0, PART), :] = part
        out_ref[k, pl.ds(PART, 8), :] = jnp.full((8, 128), total, jnp.float32)


def part_sums(where, cuts):
    return pl.pallas_call(
        part_kernel,
        compiler_params=LIMIT,
        in_specs=[SMEM] + [VMEM] * len(cuts),
        out_specs=VMEM,
        out_shape=jax.ShapeDtypeStruct((8, PART + 8, 128), jnp.float32),
        scratch_shapes=[pltpu.VMEM((PART, 128), jnp.float32)],
    )(where, *map(in_vmem, cuts))


def column_kernel(where_ref, column_ref, out_ref):
    total = column_ref[0, pl.ds(PART, 8), :]
    for k in range(1, 8):
        total = total + column_ref[k, pl.ds(PART, 8), :]
    out_ref[pl.ds(0, PART), :] = column_ref[where_ref[2], pl.ds(0, PART), :]
    out_ref[pl.ds(PART, 8), :] = total


def column_total(where, column):
    return pl.pallas_call(
        column_kernel,
        compiler_params=LIMIT,
        in_specs=[SMEM, VMEM],
        out_specs=VMEM,
        out_shape=jax.ShapeDtypeStruct((PART + 8, 128), jnp.float32),
    )(where, in_vmem(column))


def chip_kernel(where_ref, mine_ref, theirs_ref, pair_ref, out_ref):
    first = where_ref[1] == 0
    mine, theirs = mine_ref[pl.ds(0, PART), :], theirs_ref[pl.ds(0, PART), :]
    pair_ref[0] = jnp.where(first, mine, theirs)
    pair_ref[1] = jnp.where(first, theirs, mine)
    total = mine_ref[pl.ds(PART, 8), :] + theirs_ref[pl.ds(PART, 8), :]
    for k in range(16):
        out_ref[k] = total


def chip_total(where, mine, theirs):
    return pl.pallas_call(
        chip_kernel,
        compiler_params=LIMIT,
        in_specs=[SMEM, VMEM, VMEM],
        out_specs=(VMEM, VMEM),
        out_shape=(
            jax.ShapeDtypeStruct((2, PART, 128), jnp.float32),
            jax.ShapeDtypeStruct((16, 8, 128), jnp.float32),
        ),
    )(where, in_vmem(mine), in_vmem(theirs))


def state_kernel(where_ref, *refs):
    *state_refs, out_ref = refs
    y, c = where_ref[0], where_ref[1]
    cols = pl.ds(pl.multiple_of((2 * c + y // 2) * 128, 128), 128)
    for k, ref in enumerate(state_refs):
        low, high = ref[pl.ds(0, PART), cols], ref[pl.ds(STARTS[1], PART), cols]
        part = jnp.where(y % 2 == 0, low, high)
        out_ref[k] = part


def state_parts(where, states):
    return pl.pallas_call(
        state_kernel,
        compiler_params=LIMIT,
        in_specs=[SMEM] + [VMEM] * 3,
        out_specs=VMEM,
        out_shape=jax.ShapeDtypeStruct((3, PART, 128), jnp.float32),
    )(where, *states)


def clip_of(totals_ref):
    total = totals_ref[0]
    for k in range(1, 16):
        total = total + totals_ref[k]
    norm = jnp.sqrt(total)
    return jnp.minimum(jnp.float32(1.0), 1.0 / (norm + 1e-06))[:1, :1]


def stepped(fixes_ref, clip, w, a, b, summed):
    gradient = clip * summed
    new_one = 0.9 * a + 0.1 * gradient
    new_two = 0.999 * b + 0.001 * gradient * gradient
    update = new_one / fixes_ref[0] / (jnp.sqrt(new_two / fixes_ref[1]) + 1e-08)
    return w - 0.01 * (update + 0.01 * w), new_one, new_two


def weights_kernel(where_ref, fixes_ref, totals_ref, column_ref, *refs):
    *state_refs, send_ref = refs
    clip = clip_of(totals_ref)
    for k, ref in enumerate(state_refs):
        z = (where_ref[2] + (8 - k)) % 8
        summed = column_ref[z, pl.ds(0, PART), :]
        part = stepped(fixes_ref, clip, ref[0], ref[1], ref[2], summed)[0].astype(jnp.bfloat16)
        rows = pl.ds(pl.multiple_of(z * PART, 8), PART)
        for j in range(16):
            send_ref[j, rows, :] = part


def new_weights(where, fixes, totals, column, states):
    return pl.pallas_call(
        weights_kernel,
        compiler_params=LIMIT,
        in_specs=[SMEM, SMEM] + [VMEM] * (2 + len(states)),
        out_specs=VMEM,
        out_shape=jax.ShapeDtypeStruct((16, 8 * PART, 128), jnp.bfloat16),
    )(where, fixes, in_vmem(totals), in_vmem(column), *map(in_vmem, states))


def own_kernel(where_ref, fixes_ref, totals_ref, *refs):
    pair_refs, (w_ref, a_ref, b_ref, w_out, a_out, b_out, summed) = refs[:4], refs[4:]
    for half in range(2):
        for y in (half, 2 + half):
            place = (where_ref[0] + (4 - y)) % 4
            for c in range(2):
                value = pair_refs[0][c]
                for k in range(1, 4):
                    value = jnp.where(place == k, pair_refs[k][c], value)
                summed[pl.ds(STARTS[half], PART), pl.ds((2 * c + y // 2) * 128, 128)] = value
    clip = clip_of(totals_ref)
    new = stepped(fixes_ref, clip, w_ref[...], a_ref[...], b_ref[...], summed[...])
    w_out[...], a_out[...], b_out[...] = new


def own_step(where, fixes, totals, pairs, states):
    rows = jax.ShapeDtypeStruct((108, 512), jnp.float32)
    return pl.pallas_call(
        own_kernel,
        compiler_params=LIMIT,
        in_specs=[SMEM, SMEM] + [VMEM] * 8,
        out_specs=(VMEM,) * 3,
        out_shape=(rows, rows, rows),
        scratch_shapes=[pltpu.VMEM((108, 512), jnp.float32)],
    )(where, fixes, in_vmem(totals), *map(in_vmem, pairs), *states)


def assemble_kernel(c_ref, mine_ref, theirs_ref, out_ref):
    x = pl.program_id(0)
    first = c_ref[0] == 0
    for half in range(2):
        for y in (half, 2 + half):
            for z in range(8):
                part = pl.ds(z * PART, PART)
                mine, theirs = mine_ref[x * 4 + y, part, :], theirs_ref[x * 4 + y, part, :]
                rows = pl.ds(108 * z + STARTS[half], PART)
                for c in range(2):
                    cols = pl.ds((2 * c + y // 2) * 128, 128)
                    out_ref[rows, cols] = jnp.where(first == (c == 0), mine, theirs)


def assemble(c, mine, theirs):
    return pl.pallas_call(
        assemble_kernel,
        compiler_params=LIMIT,
        grid_spec=pltpu.PrefetchScalarGridSpec(
            num_scalar_prefetch=1,
            grid=(4,),
            in_specs=[VMEM, VMEM],
            out_specs=pl.BlockSpec((864, 512), lambda i, c: (i, 0)),
        ),
        out_shape=jax.ShapeDtypeStruct((3456, 512), jnp.bfloat16),
    )(c, in_vmem(mine), in_vmem(theirs))


def shards(grads, master, moment_one, moment_two, step_count):
    y, c, z = (lax.axis_index(axis) for axis in ("y", "c", "z"))
    where = jnp.stack([y, c, z]).astype(jnp.int32)
    side = where[1:2]
    states = (master, moment_one, moment_two)
    steps = step_count[0].astype(jnp.float32)
    first_fix = 1.0 - jnp.power(jnp.float32(0.9), steps)
    second_fix = 1.0 - jnp.power(jnp.float32(0.999), steps)
    fixes = jnp.stack([first_fix, second_fix])
    local = grads[0, 0]
    theirs = swapped(lax.dynamic_slice(local, (0, 256 * (1 - c)), (3456, 256)), "c")
    state_columns = rotated(state_parts(where, states), "z")
    cuts = []
    for cut in CUTS:
        coded = exchanged(code_sums(side, local, theirs, cut), PLANE)
        coded, state_columns, fixes = lax.optimization_barrier((coded, state_columns, fixes))
        cuts.append(exchanged(sum_coded(coded, cut), "z"))
    column = exchanged(part_sums(where, cuts), "z")
    part = column_total(where, column)
    pair, total = chip_total(where, part, swapped(part, "c"))
    totals = exchanged(total, PLANE)
    mine = exchanged(new_weights(where, fixes, totals, column, state_columns), PLANE)
    own = own_step(where, fixes, totals, rotated(pair, "y"), states)
    mine, own = lax.optimization_barrier((mine, own))
    weights = assemble(side, mine, swapped(mine, "c"))
    return (*own, weights)


def solution(mesh):
    finer = Mesh(mesh.devices.reshape(4, 2, 4, 8), ("y", "c", "x", "z"))
    in_specs = (P(GRP, SHARD, None, None), P(SHARD, None), P(SHARD, None), P(SHARD, None), P())
    out_specs = (P(SHARD, None), P(SHARD, None), P(SHARD, None), P())
    return jax.shard_map(
        shards, mesh=finer, in_specs=in_specs, out_specs=out_specs, check_vma=False
    )
```

time: 247 us -> 134 us (0.54)
  waiting for transfers between devices: 157 us -> 40 us
  starting transfers between devices: 18.3 us -> 40.5 us
  between operations: 16.3 us -> 1.49 us
  Pallas kernels: 0 us -> 10.8 us
  local copies, waits for them, and re-layouts: 13.4 us -> 3.63 us
    reduce_scatter x1 -> x0, waiting for transfers between devices: 79.3 us -> none  [sum_by_axis(): value = lax.psum_scatter(value, axis, scatter_dimension=dim, tiled=True)]
    all_gather x1 -> x0, waiting for transfers between devices: 46.3 us -> none  [gather_in_order(): blocks = lax.all_gather(blocks, axes[k])]
    all_to_all x0 -> x3, blocking collectives: none -> 37 us  [exchanged(): return lax.all_to_all(value, axes, split_axis=0, concat_axis=0, tiled=True)]
    ppermute x0 -> x13, waiting for transfers between devices: none -> 35.2 us  [the longest x10 25.1 us: rotated(): lax.ppermute(value, axis, [(i, (i + k) % n) for i in range(n)])]
    ppermute x0 -> x13, starting transfers between devices: none -> 31.6 us  [the longest x10 19 us: rotated(): lax.ppermute(value, axis, [(i, (i + k) % n) for i in range(n)])]
    unnamed x1 -> x0, blocking collectives: 26.8 us -> none
    all_to_all x2, waiting for transfers between devices: 31.1 us -> 4.8 us  [exchanged(): return lax.all_to_all(value, axes, split_axis=0, concat_axis=0, tiled=True)]
    all_gather x1 -> x0, blocking collectives: 11.8 us -> none  [gather_in_order(): blocks = lax.all_gather(blocks, axes[k])]
  transfers between devices with their start and end apart: 5 -> 15, of which waited for: 5 -> 11; matrix products, arithmetic and copies ran while one was open for 0% -> 0% of each run, Pallas kernels for 0% -> 2%
where the time goes in v3:
time: 134 us
  starting transfers between devices  40.5 us (30%)
  waiting for transfers between devices  40 us (30%)
  blocking collectives  37 us (28%)
  Pallas kernels  10.8 us (8%)
  local copies, waits for them, and re-layouts  3.63 us (3%)
  between operations  1.49 us (1%)
    all_to_all x3, blocking collectives, exchanged(): return lax.all_to_all(value, axes, split_axis=0, concat_axis=0, tiled=True)  37 us
    ppermute x10, waiting for transfers between devices, rotated(): lax.ppermute(value, axis, [(i, (i + k) % n) for i in range(n)])  25.1 us
    ppermute x10, starting transfers between devices, rotated(): lax.ppermute(value, axis, [(i, (i + k) % n) for i in range(n)])  19 us
    ppermute x3, starting transfers between devices, swapped(): return lax.ppermute(value, axis, [(0, 1), (1, 0)])  12.6 us
    ppermute x3, waiting for transfers between devices, swapped(): return lax.ppermute(value, axis, [(0, 1), (1, 0)])  10.1 us
    all_to_all x2, starting transfers between devices, exchanged(): return lax.all_to_all(value, axes, split_axis=0, concat_axis=0, tiled=True)  8.89 us
    all_to_all x2, waiting for transfers between devices, exchanged(): return lax.all_to_all(value, axes, split_axis=0, concat_axis=0, tiled=True)  4.8 us
    pallas_call x1, Pallas kernels, code_sums(): pl.pallas_call(kernel, compiler_params=LIMIT, grid_spec=pltpu.PrefetchSca...  2.91 us
  transfers between devices with their start and end apart: 15, of which 11 were waited for; matrix products, arithmetic and copies ran while one was open for 0% of the time, Pallas kernels for 2%

profile of v3, /device:TPU:1, one launch (start us, length us, event | category | flops | bytes accessed | tf_op | source)
XLA Modules:
  0.0 133.6 jit_solution(11440793905652622856)
XLA Ops:
  0.6 2.4 %dynamic-slice_bitcast_fusion = f32[3456,256]{1,0:T(8,128)S(1)} fusion(f32[1,1,3456,512]{3,2,1,0:T(8,128)} %param.5, s32[]{:T(128)S(6)} %select_n.3), kind=kLoop, calls=%fused_computation | loop fusion | bytes 7077892 | tf_op jit(solution)/shard_map/dynamic_slice | solution.py:298
  3.0 3.3 %collective-permute-start = (f32[3456,256]{1,0:T(8,128)S(1)}, f32[3456,256]{1,0:T(8,128)S(1)}, u32[]{:S(2)}, u32[]{:S(2)}) collective-permute-start(f32[3456,256]{1,0:T(8,128)S(1)} %dynamic-slice_bitcast_fusion), channel_id=1, source_target_pairs={{0,32},{32,0},{1,33},{33,1},{2,34},{34,2},{3,35},{35,3},{4,36},{36... | collective-permute-start | bytes 10616840 | tf_op jit(solution)/shard_map/ppermute | solution.py:31
  6.3 5.8 %collective-permute-done.theirs_ref = f32[3456,256]{1,0:T(8,128)S(1)} collective-permute-done((f32[3456,256]{1,0:T(8,128)S(1)}, f32[3456,256]{1,0:T(8,128)S(1)}, u32[]{:S(2)}, u32[]{:S(2)}) %collective-permute-start) | collective-permute-done | bytes 3538976 | tf_op jit(solution)/shard_map/ppermute | solution.py:31
  12.2 2.9 %shard_map.84 = s16[4,4,456,128]{3,2,1,0:T(8,128)(2,1)} custom-call(s32[1]{0:T(128)} %bitcast.1.c_ref, f32[3456,512]{1,0:T(8,128)S(1)} %bitcast.7, f32[3456,256]{1,0:T(8,128)S(1)} %collective-permute-done.theirs_ref), custom_call_target="tpu_custom_call" | custom-call | tf_op jit(solution)/shard_map/pallas_call | solution.py:63
  15.1 5.2 %all-to-all-start = ((s16[16,456,128]{2,1,0:T(8,128)(2,1)}), s16[16,456,128]{2,1,0:T(8,128)(2,1)S(1)}, u32[]{:S(2)}, u32[]{:S(2)}) async-start(s16[16,456,128]{2,1,0:T(8,128)(2,1)} %bitcast.5), calls=%async_computation | async-start | bytes 3735552 | tf_op jit(solution)/shard_map/all_to_all | solution.py:27
  21.0 5.7 %collective-permute-start.7 = (f32[3,56,128]{2,1,0:T(8,128)S(1)}, f32[3,56,128]{2,1,0:T(8,128)S(1)}, u32[]{:S(2)}, u32[]{:S(2)}) collective-permute-start(f32[3,56,128]{2,1,0:T(8,128)S(1)} %shard_map.85.refs_0_), channel_id=1, source_target_pairs={{0,7},{1,0},{2,1},{3,2},{4,3},{5,4},{6,5},{7,6},{8,15},{9,8},{10,9... | collective-permute-start | bytes 258056 | tf_op jit(solution)/shard_map/ppermute | solution.py:36
  26.6 1.2 collective-permute-start.6
  28.2 4.5 %collective-permute-start.4 = (f32[3,56,128]{2,1,0:T(8,128)S(1)}, f32[3,56,128]{2,1,0:T(8,128)S(1)}, u32[]{:S(2)}, u32[]{:S(2)}) collective-permute-start(f32[3,56,128]{2,1,0:T(8,128)S(1)} %shard_map.85.refs_0_), channel_id=1, source_target_pairs={{0,4},{1,5},{2,6},{3,7},{4,0},{5,1},{6,2},{7,3},{8,12},{9,13},{10,... | collective-permute-start | bytes 258056 | tf_op jit(solution)/shard_map/ppermute | solution.py:36
  33.5 2.2 %collective-permute-start.2 = (f32[3,56,128]{2,1,0:T(8,128)S(1)}, f32[3,56,128]{2,1,0:T(8,128)S(1)}, u32[]{:S(2)}, u32[]{:S(2)}) collective-permute-start(f32[3,56,128]{2,1,0:T(8,128)S(1)} %shard_map.85.refs_0_), channel_id=1, source_target_pairs={{0,2},{1,3},{2,4},{3,5},{4,6},{5,7},{6,0},{7,1},{8,10},{9,11},{10,... | collective-permute-start | bytes 258056 | tf_op jit(solution)/shard_map/ppermute | solution.py:36
  35.7 1.4 %collective-permute-start.1 = (f32[3,56,128]{2,1,0:T(8,128)S(1)}, f32[3,56,128]{2,1,0:T(8,128)S(1)}, u32[]{:S(2)}, u32[]{:S(2)}) collective-permute-start(f32[3,56,128]{2,1,0:T(8,128)S(1)} %shard_map.85.refs_0_), channel_id=1, source_target_pairs={{0,1},{1,2},{2,3},{3,4},{4,5},{5,6},{6,7},{7,0},{8,9},{9,10},{10,1... | collective-permute-start | bytes 258056 | tf_op jit(solution)/shard_map/ppermute | solution.py:36
  37.2 0.6 collective-permute-done.4.refs_4_
  37.8 2.8 %collective-permute-done.3.refs_3_ = f32[3,56,128]{2,1,0:T(8,128)S(1)} collective-permute-done((f32[3,56,128]{2,1,0:T(8,128)S(1)}, f32[3,56,128]{2,1,0:T(8,128)S(1)}, u32[]{:S(2)}, u32[]{:S(2)}) %collective-permute-start.3) | collective-permute-done | bytes 86048 | tf_op jit(solution)/shard_map/ppermute | solution.py:36
  40.6 6.5 %collective-permute-done.2.refs_2_ = f32[3,56,128]{2,1,0:T(8,128)S(1)} collective-permute-done((f32[3,56,128]{2,1,0:T(8,128)S(1)}, f32[3,56,128]{2,1,0:T(8,128)S(1)}, u32[]{:S(2)}, u32[]{:S(2)}) %collective-permute-start.2) | collective-permute-done | bytes 86048 | tf_op jit(solution)/shard_map/ppermute | solution.py:36
  47.1 1.9 %collective-permute-done.1.refs_1_ = f32[3,56,128]{2,1,0:T(8,128)S(1)} collective-permute-done((f32[3,56,128]{2,1,0:T(8,128)S(1)}, f32[3,56,128]{2,1,0:T(8,128)S(1)}, u32[]{:S(2)}, u32[]{:S(2)}) %collective-permute-start.1) | collective-permute-done | bytes 86048 | tf_op jit(solution)/shard_map/ppermute | solution.py:36
  49.5 14.6 %all_to_all.25.refs_0_ = f32[8,56,128]{2,1,0:T(8,128)S(1)} all-to-all(f32[8,56,128]{2,1,0:T(8,128)S(1)} %shard_map.86), channel_id=1, replica_groups=mesh['y'=4,'c'=2,'x'=4,'z'=8] {'z'}, dimensions={0} | all-to-all | bytes 458752 | tf_op jit(solution)/shard_map/all_to_all | solution.py:27
  64.1 0.7 shard_map.87
  64.8 11.8 %all_to_all.26.column_ref = f32[8,64,128]{2,1,0:T(8,128)S(1)} all-to-all(f32[8,64,128]{2,1,0:T(8,128)S(1)} %shard_map.87), channel_id=1, replica_groups=mesh['y'=4,'c'=2,'x'=4,'z'=8] {'z'}, dimensions={0} | all-to-all | bytes 524288 | tf_op jit(solution)/shard_map/all_to_all | solution.py:27
  77.2 5.0 %collective-permute-start.8 = (f32[64,128]{1,0:T(8,128)S(1)}, f32[64,128]{1,0:T(8,128)S(1)}, u32[]{:S(2)}, u32[]{:S(2)}) collective-permute-start(f32[64,128]{1,0:T(8,128)S(1)} %shard_map.88.mine_ref), channel_id=1, source_target_pairs={{0,32},{32,0},{1,33},{33,1},{2,34},{34,2},{3,35},{35,3},{4,36},{36... | collective-permute-start | bytes 98312 | tf_op jit(solution)/shard_map/ppermute | solution.py:31
  82.2 0.9 collective-permute-done.8.theirs_ref
  83.6 10.5 %all_to_all.27.totals_ref = f32[16,8,128]{2,1,0:T(8,128)S(1)} all-to-all(f32[16,8,128]{2,1,0:T(8,128)S(1)} %get-tuple-element.25), channel_id=1, replica_groups=mesh['y'=4,'c'=2,'x'=4,'z'=8] {'x','y'}, dimensions={0} | all-to-all | bytes 131072 | tf_op jit(solution)/shard_map/all_to_all | solution.py:27
  94.1 0.9 shard_map.90
  95.0 1.2 copy-done.1
  96.2 3.7 %all-to-all-start.4 = ((bf16[16,448,128]{2,1,0:T(8,128)(2,1)}), bf16[16,448,128]{2,1,0:T(8,128)(2,1)S(1)}, u32[]{:S(2)}, u32[]{:S(2)}) async-start(bf16[16,448,128]{2,1,0:T(8,128)(2,1)} %copy-done.1), calls=%async_computation.4 | async-start | bytes 3670016 | tf_op jit(solution)/shard_map/all_to_all | solution.py:27
  99.9 2.5 %collective-permute-start.11 = (f32[2,56,128]{2,1,0:T(8,128)S(1)}, f32[2,56,128]{2,1,0:T(8,128)S(1)}, u32[]{:S(2)}, u32[]{:S(2)}) collective-permute-start(f32[2,56,128]{2,1,0:T(8,128)S(1)} %get-tuple-element.34.refs_0_), channel_id=1, source_target_pairs={{0,192},{64,0},{128,64},{192,128},{1,193},{65,1},{129,65},{193,129... | collective-permute-start | bytes 172040 | tf_op jit(solution)/shard_map/ppermute | solution.py:36
  103.5 4.5 %collective-permute-done.11.refs_3_ = f32[2,56,128]{2,1,0:T(8,128)S(1)} collective-permute-done((f32[2,56,128]{2,1,0:T(8,128)S(1)}, f32[2,56,128]{2,1,0:T(8,128)S(1)}, u32[]{:S(2)}, u32[]{:S(2)}) %collective-permute-start.11) | collective-permute-done | bytes 57376 | tf_op jit(solution)/shard_map/ppermute | solution.py:36
  108.1 3.2 %collective-permute-done.10.refs_2_ = f32[2,56,128]{2,1,0:T(8,128)S(1)} collective-permute-done((f32[2,56,128]{2,1,0:T(8,128)S(1)}, f32[2,56,128]{2,1,0:T(8,128)S(1)}, u32[]{:S(2)}, u32[]{:S(2)}) %collective-permute-start.10) | collective-permute-done | bytes 57376 | tf_op jit(solution)/shard_map/ppermute | solution.py:36
  111.2 5.6 %collective-permute-done.9.refs_1_ = f32[2,56,128]{2,1,0:T(8,128)S(1)} collective-permute-done((f32[2,56,128]{2,1,0:T(8,128)S(1)}, f32[2,56,128]{2,1,0:T(8,128)S(1)}, u32[]{:S(2)}, u32[]{:S(2)}) %collective-permute-start.9) | collective-permute-done | bytes 57376 | tf_op jit(solution)/shard_map/ppermute | solution.py:36
  116.9 1.6 %shard_map.91 = (f32[108,512]{1,0:T(8,128)}, f32[108,512]{1,0:T(8,128)}, f32[108,512]{1,0:T(8,128)}) custom-call(s32[3]{0:T(128)S(1)} %pad_add_fusion.where_ref, f32[2]{0:T(128)S(1)} %pad_maximum_fusion.fixes_ref, f32[16,8,128]{2,1,0:T(8,128)S(1)} %all_to_all.27.totals_ref, f32[2,56,128]{2,1,0:T(8,128)S(1)} %get-tuple-element.34.refs_0_, ...), custom_call_target="tpu_custom_call" | custom-call | tf_op jit(solution)/shard_map/pallas_call | solution.py:250
  118.5 4.8 %all-to-all-done.4.mine_ref = bf16[16,448,128]{2,1,0:T(8,128)(2,1)S(1)} async-done(((bf16[16,448,128]{2,1,0:T(8,128)(2,1)}), bf16[16,448,128]{2,1,0:T(8,128)(2,1)S(1)}, u32[]{:S(2)}, u32[]{:S(2)}) %all-to-all-start.4) | async-done | bytes 1835040 | tf_op jit(solution)/shard_map/all_to_all | solution.py:27
  123.3 4.3 %collective-permute-start.12 = (bf16[16,448,128]{2,1,0:T(8,128)(2,1)S(1)}, bf16[16,448,128]{2,1,0:T(8,128)(2,1)S(1)}, u32[]{:S(2)}, u32[]{:S(2)}) collective-permute-start(bf16[16,448,128]{2,1,0:T(8,128)(2,1)S(1)} %all-to-all-done.4.mine_ref), channel_id=1, source_target_pairs={{0,32},{32,0},{1,33},{33,1},{2,34},{34,2},{3,35},{35,3},{4,36},{36... | collective-permute-start | bytes 5505032 | tf_op jit(solution)/shard_map/ppermute | solution.py:31
  127.6 3.4 %collective-permute-done.12.theirs_ref = bf16[16,448,128]{2,1,0:T(8,128)(2,1)S(1)} collective-permute-done((bf16[16,448,128]{2,1,0:T(8,128)(2,1)S(1)}, bf16[16,448,128]{2,1,0:T(8,128)(2,1)S(1)}, u32[]{:S(2)}, u32[]{:S(2)}) %collective-permute-start.12) | collective-permute-done | bytes 1835040 | tf_op jit(solution)/shard_map/ppermute | solution.py:31
  131.0 2.6 %shard_map.92 = bf16[3456,512]{1,0:T(8,128)(2,1)} custom-call(s32[1]{0:T(128)} %bitcast.1.c_ref, bf16[16,448,128]{2,1,0:T(8,128)(2,1)S(1)} %all-to-all-done.4.mine_ref, bf16[16,448,128]{2,1,0:T(8,128)(2,1)S(1)} %collective-permute-done.12.theirs_ref), custom_call_target="tpu_custom_call" | custom-call | tf_op jit(solution)/shard_map/pallas_call | solution.py:275
  (23 shorter events, 4.0 us)
Async XLA Ops:
  0.6 11.5 %copy-start = (f32[1,1,3456,512]{3,2,1,0:T(8,128)S(1)}, f32[1,1,3456,512]{3,2,1,0:T(8,128)}, u32[]{:S(2)}) copy-start(f32[1,1,3456,512]{3,2,1,0:T(8,128)} %param.5) | copy-start | bytes 21233668
  3.0 9.1 %collective-permute-start = (f32[3456,256]{1,0:T(8,128)S(1)}, f32[3456,256]{1,0:T(8,128)S(1)}, u32[]{:S(2)}, u32[]{:S(2)}) collective-permute-start(f32[3456,256]{1,0:T(8,128)S(1)} %dynamic-slice_bitcast_fusion), channel_id=1, source_target_pairs={{0,32},{32,0},{1,33},{33,1},{2,34},{34,2},{3,35},{35,3},{4,36},{36... | collective-permute-start | bytes 10616840 | tf_op jit(solution)/shard_map/ppermute | solution.py:31
  15.1 5.3 %copy-start.2 = (f32[108,512]{1,0:T(8,128)S(1)}, f32[108,512]{1,0:T(8,128)}, u32[]{:S(2)}) copy-start(f32[108,512]{1,0:T(8,128)} %refs_4_.1) | copy-start | bytes 663556
  15.1 5.3 %copy-start.3 = (f32[108,512]{1,0:T(8,128)S(1)}, f32[108,512]{1,0:T(8,128)}, u32[]{:S(2)}) copy-start(f32[108,512]{1,0:T(8,128)} %refs_5_.1) | copy-start | bytes 663556
  15.1 5.3 %copy-start.4 = (f32[108,512]{1,0:T(8,128)S(1)}, f32[108,512]{1,0:T(8,128)}, u32[]{:S(2)}) copy-start(f32[108,512]{1,0:T(8,128)} %refs_6_.1) | copy-start | bytes 663556
  15.1 33.8 %all-to-all-start = ((s16[16,456,128]{2,1,0:T(8,128)(2,1)}), s16[16,456,128]{2,1,0:T(8,128)(2,1)S(1)}, u32[]{:S(2)}, u32[]{:S(2)}) async-start(s16[16,456,128]{2,1,0:T(8,128)(2,1)} %bitcast.5), calls=%async_computation | async-start | bytes 3735552 | tf_op jit(solution)/shard_map/all_to_all | solution.py:27
  21.0 12.5 %collective-permute-start.7 = (f32[3,56,128]{2,1,0:T(8,128)S(1)}, f32[3,56,128]{2,1,0:T(8,128)S(1)}, u32[]{:S(2)}, u32[]{:S(2)}) collective-permute-start(f32[3,56,128]{2,1,0:T(8,128)S(1)} %shard_map.85.refs_0_), channel_id=1, source_target_pairs={{0,7},{1,0},{2,1},{3,2},{4,3},{5,4},{6,5},{7,6},{8,15},{9,8},{10,9... | collective-permute-start | bytes 258056 | tf_op jit(solution)/shard_map/ppermute | solution.py:36
  26.6 9.1 %collective-permute-start.6 = (f32[3,56,128]{2,1,0:T(8,128)S(1)}, f32[3,56,128]{2,1,0:T(8,128)S(1)}, u32[]{:S(2)}, u32[]{:S(2)}) collective-permute-start(f32[3,56,128]{2,1,0:T(8,128)S(1)} %shard_map.85.refs_0_), channel_id=1, source_target_pairs={{0,6},{1,7},{2,0},{3,1},{4,2},{5,3},{6,4},{7,5},{8,14},{9,15},{10,... | collective-permute-start | bytes 258056 | tf_op jit(solution)/shard_map/ppermute | solution.py:36
  27.8 9.4 %collective-permute-start.5 = (f32[3,56,128]{2,1,0:T(8,128)S(1)}, f32[3,56,128]{2,1,0:T(8,128)S(1)}, u32[]{:S(2)}, u32[]{:S(2)}) collective-permute-start(f32[3,56,128]{2,1,0:T(8,128)S(1)} %shard_map.85.refs_0_), channel_id=1, source_target_pairs={{0,5},{1,6},{2,7},{3,0},{4,1},{5,2},{6,3},{7,4},{8,13},{9,14},{10,... | collective-permute-start | bytes 258056 | tf_op jit(solution)/shard_map/ppermute | solution.py:36
  28.2 9.5 %collective-permute-start.4 = (f32[3,56,128]{2,1,0:T(8,128)S(1)}, f32[3,56,128]{2,1,0:T(8,128)S(1)}, u32[]{:S(2)}, u32[]{:S(2)}) collective-permute-start(f32[3,56,128]{2,1,0:T(8,128)S(1)} %shard_map.85.refs_0_), channel_id=1, source_target_pairs={{0,4},{1,5},{2,6},{3,7},{4,0},{5,1},{6,2},{7,3},{8,12},{9,13},{10,... | collective-permute-start | bytes 258056 | tf_op jit(solution)/shard_map/ppermute | solution.py:36
  32.7 7.9 %collective-permute-start.3 = (f32[3,56,128]{2,1,0:T(8,128)S(1)}, f32[3,56,128]{2,1,0:T(8,128)S(1)}, u32[]{:S(2)}, u32[]{:S(2)}) collective-permute-start(f32[3,56,128]{2,1,0:T(8,128)S(1)} %shard_map.85.refs_0_), channel_id=1, source_target_pairs={{0,3},{1,4},{2,5},{3,6},{4,7},{5,0},{6,1},{7,2},{8,11},{9,12},{10,... | collective-permute-start | bytes 258056 | tf_op jit(solution)/shard_map/ppermute | solution.py:36
  33.5 13.6 %collective-permute-start.2 = (f32[3,56,128]{2,1,0:T(8,128)S(1)}, f32[3,56,128]{2,1,0:T(8,128)S(1)}, u32[]{:S(2)}, u32[]{:S(2)}) collective-permute-start(f32[3,56,128]{2,1,0:T(8,128)S(1)} %shard_map.85.refs_0_), channel_id=1, source_target_pairs={{0,2},{1,3},{2,4},{3,5},{4,6},{5,7},{6,0},{7,1},{8,10},{9,11},{10,... | collective-permute-start | bytes 258056 | tf_op jit(solution)/shard_map/ppermute | solution.py:36
  35.7 13.2 %collective-permute-start.1 = (f32[3,56,128]{2,1,0:T(8,128)S(1)}, f32[3,56,128]{2,1,0:T(8,128)S(1)}, u32[]{:S(2)}, u32[]{:S(2)}) collective-permute-start(f32[3,56,128]{2,1,0:T(8,128)S(1)} %shard_map.85.refs_0_), channel_id=1, source_target_pairs={{0,1},{1,2},{2,3},{3,4},{4,5},{5,6},{6,7},{7,0},{8,9},{9,10},{10,1... | collective-permute-start | bytes 258056 | tf_op jit(solution)/shard_map/ppermute | solution.py:36
  77.2 5.8 %collective-permute-start.8 = (f32[64,128]{1,0:T(8,128)S(1)}, f32[64,128]{1,0:T(8,128)S(1)}, u32[]{:S(2)}, u32[]{:S(2)}) collective-permute-start(f32[64,128]{1,0:T(8,128)S(1)} %shard_map.88.mine_ref), channel_id=1, source_target_pairs={{0,32},{32,0},{1,33},{33,1},{2,34},{34,2},{3,35},{35,3},{4,36},{36... | collective-permute-start | bytes 98312 | tf_op jit(solution)/shard_map/ppermute | solution.py:31
  95.0 1.2 copy-start.1
  96.2 27.1 %all-to-all-start.4 = ((bf16[16,448,128]{2,1,0:T(8,128)(2,1)}), bf16[16,448,128]{2,1,0:T(8,128)(2,1)S(1)}, u32[]{:S(2)}, u32[]{:S(2)}) async-start(bf16[16,448,128]{2,1,0:T(8,128)(2,1)} %copy-done.1), calls=%async_computation.4 | async-start | bytes 3670016 | tf_op jit(solution)/shard_map/all_to_all | solution.py:27
  99.9 8.2 %collective-permute-start.11 = (f32[2,56,128]{2,1,0:T(8,128)S(1)}, f32[2,56,128]{2,1,0:T(8,128)S(1)}, u32[]{:S(2)}, u32[]{:S(2)}) collective-permute-start(f32[2,56,128]{2,1,0:T(8,128)S(1)} %get-tuple-element.34.refs_0_), channel_id=1, source_target_pairs={{0,192},{64,0},{128,64},{192,128},{1,193},{65,1},{129,65},{193,129... | collective-permute-start | bytes 172040 | tf_op jit(solution)/shard_map/ppermute | solution.py:36
  102.4 8.8 %collective-permute-start.10 = (f32[2,56,128]{2,1,0:T(8,128)S(1)}, f32[2,56,128]{2,1,0:T(8,128)S(1)}, u32[]{:S(2)}, u32[]{:S(2)}) collective-permute-start(f32[2,56,128]{2,1,0:T(8,128)S(1)} %get-tuple-element.34.refs_0_), channel_id=1, source_target_pairs={{0,128},{64,192},{128,0},{192,64},{1,129},{65,193},{129,1},{193,65... | collective-permute-start | bytes 172040 | tf_op jit(solution)/shard_map/ppermute | solution.py:36
  103.0 13.9 %collective-permute-start.9 = (f32[2,56,128]{2,1,0:T(8,128)S(1)}, f32[2,56,128]{2,1,0:T(8,128)S(1)}, u32[]{:S(2)}, u32[]{:S(2)}) collective-permute-start(f32[2,56,128]{2,1,0:T(8,128)S(1)} %get-tuple-element.34.refs_0_), channel_id=1, source_target_pairs={{0,64},{64,128},{128,192},{192,0},{1,65},{65,129},{129,193},{193,1... | collective-permute-start | bytes 172040 | tf_op jit(solution)/shard_map/ppermute | solution.py:36
  123.3 7.8 %collective-permute-start.12 = (bf16[16,448,128]{2,1,0:T(8,128)(2,1)S(1)}, bf16[16,448,128]{2,1,0:T(8,128)(2,1)S(1)}, u32[]{:S(2)}, u32[]{:S(2)}) collective-permute-start(bf16[16,448,128]{2,1,0:T(8,128)(2,1)S(1)} %all-to-all-done.4.mine_ref), channel_id=1, source_target_pairs={{0,32},{32,0},{1,33},{33,1},{2,34},{34,2},{3,35},{35,3},{4,36},{36... | collective-permute-start | bytes 5505032 | tf_op jit(solution)/shard_map/ppermute | solution.py:31

commit v4 on v3

v4 whole, which is shorter than its diff:
```python
import jax
import jax.numpy as jnp
from jax import lax
from jax.experimental import pallas as pl
from jax.experimental.pallas import tpu as pltpu
from jax.sharding import Mesh
from jax.sharding import PartitionSpec as P

GRP = ("y", "c")
SHARD = ("x", "z")
PLANE = ("x", "y")

PART = 56
STARTS = (0, 52)
SHARED = 4
COLUMN = 8 * PART
LIMIT = pltpu.CompilerParams(vmem_limit_bytes=24 * 2**20)
VMEM = pl.BlockSpec(memory_space=pltpu.VMEM)
ANY = pl.BlockSpec(memory_space=pl.ANY)
SMEM = pl.BlockSpec(memory_space=pltpu.SMEM)


def in_vmem(value):
    return pltpu.with_memory_space_constraint(value, pltpu.VMEM)


def exchanged(value, axes):
    return lax.all_to_all(value, axes, split_axis=0, concat_axis=0, tiled=True)


def swapped(value, axis):
    return lax.ppermute(value, axis, [(0, 1), (1, 0)])


def rotated(value, axis):
    n = lax.axis_size(axis)
    return [value] + [lax.ppermute(value, axis, [(i, (i + k) % n) for i in range(n)]) for k in range(1, n)]


def code_sums(c, local, theirs, piece, coded):
    def kernel(c_ref, mine_ref, theirs_ref, *refs):
        out_ref, sums = refs[-2:]
        for x, y in ((x, y) for x in range(2) for y in range(4)):
            lane = (y // 2) * 128
            mine_cols = pl.ds(pl.multiple_of(256 * c_ref[0] + lane, 128), 128)
            peak = jnp.zeros((8, 128), jnp.float32)
            for z in range(8):
                start = 864 * x + 108 * z + STARTS[y % 2]
                for t in range(0, PART, 8):
                    mine = mine_ref[pl.ds(1728 * piece + start + t, 8), mine_cols]
                    value = mine + theirs_ref[pl.ds(start + t, 8), pl.ds(lane, 128)]
                    peak = jnp.maximum(peak, jnp.abs(value))
                    sums[pl.ds(z * PART + t, 8), :] = value
            peak = jnp.max(peak, axis=0, keepdims=True)
            level = jnp.maximum(jnp.ceil(4.0 * jnp.log2(peak) + 0.02), -400.0)
            inverse = 32767.0 * jnp.exp2(-0.25 * level)
            for t in range(0, COLUMN, PART):
                scaled = jnp.round(sums[pl.ds(t, PART), :] * inverse)
                out_ref[x, y, pl.ds(t, PART), :] = scaled.astype(jnp.int32).astype(jnp.int16)
            level = jnp.broadcast_to(level, (8, 128))
            out_ref[x, y, pl.ds(COLUMN, 8), :] = level.astype(jnp.int32).astype(jnp.int16)

    return pl.pallas_call(
        kernel,
        compiler_params=LIMIT,
        grid_spec=pltpu.PrefetchScalarGridSpec(
            num_scalar_prefetch=1,
            grid=(1,),
            in_specs=[VMEM, VMEM] + [ANY] * len(coded),
            out_specs=pl.BlockSpec((2, 4, COLUMN + 8, 128), lambda i, c: (piece, 0, 0, 0)),
            scratch_shapes=[pltpu.VMEM((COLUMN, 128), jnp.float32)],
        ),
        out_shape=jax.ShapeDtypeStruct((4, 4, COLUMN + 8, 128), jnp.int16),
        input_output_aliases={3: 0} if coded else {},
    )(c, in_vmem(local), in_vmem(theirs), *coded)


def sum_kernel(coded_ref, out_ref):
    scales = []
    for k in range(16):
        level = coded_ref[k, pl.ds(COLUMN, 8), :].astype(jnp.int32).astype(jnp.float32)
        scales.append(jnp.exp2(0.25 * level) * (1.0 / 32767.0))
    for z in range(8):
        rows = pl.ds(z * PART, PART)
        total = jnp.zeros((PART // 8, 8, 128), jnp.float32)
        for k in range(16):
            value = coded_ref[k, rows, :].astype(jnp.int32).astype(jnp.float32)
            total = total + value.reshape(PART // 8, 8, 128) * scales[k]
        out_ref[z] = total.reshape(PART, 128)


def sum_coded(coded):
    return pl.pallas_call(
        sum_kernel,
        compiler_params=LIMIT,
        in_specs=[VMEM],
        out_specs=VMEM,
        out_shape=jax.ShapeDtypeStruct((8, PART, 128), jnp.float32),
    )(in_vmem(coded))


def part_kernel(where_ref, sums_ref, part_ref, out_ref):
    part = sums_ref[0]
    for k in range(1, 8):
        part = part + sums_ref[k]
    part_ref[...] = part
    row = lax.broadcasted_iota(jnp.int32, part.shape, 0)
    counted = (row >= SHARED) | (where_ref[0] % 2 == 0)
    total = jnp.sum(jnp.where(counted, part * part, 0.0))
    for k in range(8):
        out_ref[k, pl.ds(0, PART), :] = part
        out_ref[k, pl.ds(PART, 8), :] = jnp.full((8, 128), total, jnp.float32)


def part_sum(where, sums):
    return pl.pallas_call(
        part_kernel,
        compiler_params=LIMIT,
        in_specs=[SMEM, VMEM],
        out_specs=(VMEM, VMEM),
        out_shape=(
            jax.ShapeDtypeStruct((PART, 128), jnp.float32),
            jax.ShapeDtypeStruct((8, PART + 8, 128), jnp.float32),
        ),
    )(where, in_vmem(sums))


def column_kernel(column_ref, *refs):
    *part_refs, out_ref = refs
    total = column_ref[0, pl.ds(PART, 8), :]
    for k in range(1, 8):
        total = total + column_ref[k, pl.ds(PART, 8), :]
    for k, ref in enumerate(part_refs):
        out_ref[pl.ds(k * PART, PART), :] = ref[...]
    out_ref[pl.ds(4 * PART, 8), :] = total


def column_total(column, parts):
    return pl.pallas_call(
        column_kernel,
        compiler_params=LIMIT,
        in_specs=[VMEM] * 5,
        out_specs=VMEM,
        out_shape=jax.ShapeDtypeStruct((4 * PART + 8, 128), jnp.float32),
    )(*map(in_vmem, (column, *parts)))


def chip_kernel(mine_ref, theirs_ref, out_ref):
    total = mine_ref[pl.ds(4 * PART, 8), :] + theirs_ref[pl.ds(4 * PART, 8), :]
    for k in range(16):
        out_ref[k] = total


def chip_total(mine, theirs):
    return pl.pallas_call(
        chip_kernel,
        compiler_params=LIMIT,
        in_specs=[VMEM, VMEM],
        out_specs=VMEM,
        out_shape=jax.ShapeDtypeStruct((16, 8, 128), jnp.float32),
    )(in_vmem(mine), in_vmem(theirs))


def state_kernel(where_ref, *refs):
    *state_refs, out_ref = refs
    y, c = where_ref[0], where_ref[1]
    cols = pl.ds(pl.multiple_of((2 * c + y // 2) * 128, 128), 128)
    for k, ref in enumerate(state_refs):
        low, high = ref[pl.ds(0, PART), cols], ref[pl.ds(STARTS[1], PART), cols]
        part = jnp.where(y % 2 == 0, low, high)
        out_ref[k] = part


def state_parts(where, states):
    return pl.pallas_call(
        state_kernel,
        compiler_params=LIMIT,
        in_specs=[SMEM] + [VMEM] * 3,
        out_specs=VMEM,
        out_shape=jax.ShapeDtypeStruct((3, PART, 128), jnp.float32),
    )(where, *states)


def clip_of(totals_ref):
    total = totals_ref[0]
    for k in range(1, 16):
        total = total + totals_ref[k]
    norm = jnp.sqrt(total)
    return jnp.minimum(jnp.float32(1.0), 1.0 / (norm + 1e-06))[:1, :1]


def stepped(fixes_ref, clip, w, a, b, summed):
    gradient = clip * summed
    new_one = 0.9 * a + 0.1 * gradient
    new_two = 0.999 * b + 0.001 * gradient * gradient
    update = new_one / fixes_ref[0] / (jnp.sqrt(new_two / fixes_ref[1]) + 1e-08)
    return w - 0.01 * (update + 0.01 * w), new_one, new_two


def weights_kernel(where_ref, fixes_ref, totals_ref, column_ref, *refs):
    *state_refs, send_ref = refs
    clip = clip_of(totals_ref)
    for k, ref in enumerate(state_refs):
        z = (where_ref[2] + (8 - k)) % 8
        summed = column_ref[z, pl.ds(0, PART), :]
        part = stepped(fixes_ref, clip, ref[0], ref[1], ref[2], summed)[0].astype(jnp.bfloat16)
        rows = pl.ds(pl.multiple_of(z * PART, 8), PART)
        for j in range(16):
            send_ref[j, rows, :] = part


def new_weights(where, fixes, totals, column, states):
    return pl.pallas_call(
        weights_kernel,
        compiler_params=LIMIT,
        in_specs=[SMEM, SMEM] + [VMEM] * (2 + len(states)),
        out_specs=VMEM,
        out_shape=jax.ShapeDtypeStruct((16, 8 * PART, 128), jnp.bfloat16),
    )(where, fixes, in_vmem(totals), in_vmem(column), *map(in_vmem, states))


def own_kernel(where_ref, fixes_ref, totals_ref, mine_ref, theirs_ref, *refs):
    w_ref, a_ref, b_ref, w_out, a_out, b_out, summed = refs
    for half in range(2):
        for y in (half, 2 + half):
            place = (where_ref[0] + (4 - y)) % 4
            rows = pl.ds(pl.multiple_of(place * PART, 8), PART)
            mine, theirs = mine_ref[rows, :], theirs_ref[rows, :]
            for c in range(2):
                value = jnp.where(where_ref[1] == c, mine, theirs)
                summed[pl.ds(STARTS[half], PART), pl.ds((2 * c + y // 2) * 128, 128)] = value
    clip = clip_of(totals_ref)
    new = stepped(fixes_ref, clip, w_ref[...], a_ref[...], b_ref[...], summed[...])
    w_out[...], a_out[...], b_out[...] = new


def own_step(where, fixes, totals, mine, theirs, states):
    rows = jax.ShapeDtypeStruct((108, 512), jnp.float32)
    return pl.pallas_call(
        own_kernel,
        compiler_params=LIMIT,
        in_specs=[SMEM, SMEM] + [VMEM] * 6,
        out_specs=(VMEM,) * 3,
        out_shape=(rows, rows, rows),
        scratch_shapes=[pltpu.VMEM((108, 512), jnp.float32)],
    )(where, fixes, *map(in_vmem, (totals, mine, theirs)), *states)


def assemble(c, mine, theirs, piece, weights):
    def kernel(c_ref, mine_ref, theirs_ref, *refs):
        out_ref = refs[-1]
        first = c_ref[0] == 0
        for half in range(2):
            for x, y in ((x, y) for x in range(2) for y in (half, 2 + half)):
                for z in range(8):
                    part = pl.ds(z * PART, PART)
                    own, other = mine_ref[8 * piece + 4 * x + y, part, :], theirs_ref[4 * x + y, part, :]
                    rows = pl.ds(864 * x + 108 * z + STARTS[half], PART)
                    for c in range(2):
                        cols = pl.ds((2 * c + y // 2) * 128, 128)
                        out_ref[rows, cols] = jnp.where(first == (c == 0), own, other)

    return pl.pallas_call(
        kernel,
        compiler_params=LIMIT,
        grid_spec=pltpu.PrefetchScalarGridSpec(
            num_scalar_prefetch=1,
            grid=(1,),
            in_specs=[VMEM, VMEM] + [ANY] * len(weights),
            out_specs=pl.BlockSpec((1728, 512), lambda i, c: (piece, 0)),
        ),
        out_shape=jax.ShapeDtypeStruct((3456, 512), jnp.bfloat16),
        input_output_aliases={3: 0} if weights else {},
    )(c, in_vmem(mine), in_vmem(theirs), *weights)


def shards(grads, master, moment_one, moment_two, step_count):
    y, c, z = (lax.axis_index(axis) for axis in ("y", "c", "z"))
    where = jnp.stack([y, c, z]).astype(jnp.int32)
    side = where[1:2]
    states = (master, moment_one, moment_two)
    steps = step_count[0].astype(jnp.float32)
    first_fix = 1.0 - jnp.power(jnp.float32(0.9), steps)
    second_fix = 1.0 - jnp.power(jnp.float32(0.999), steps)
    fixes = jnp.stack([first_fix, second_fix])
    local = grads[0, 0]
    theirs = [swapped(lax.dynamic_slice(local, (1728 * k, 256 * (1 - c)), (1728, 256)), "c") for k in range(2)]
    coded = ()
    for k in range(2):
        coded = (code_sums(side, local, theirs[k], k, coded),)
    coded = exchanged(coded[0].reshape(16, COLUMN + 8, 128), PLANE)
    state_columns = rotated(state_parts(where, states), "z")
    coded, state_columns, fixes = lax.optimization_barrier((coded, state_columns, fixes))
    part, sent = part_sum(where, exchanged(sum_coded(coded), "z"))
    column = exchanged(sent, "z")
    own = column_total(column, rotated(part, "y"))
    other = swapped(own, "c")
    totals = exchanged(chip_total(own, other), PLANE)
    mine = exchanged(new_weights(where, fixes, totals, column, state_columns), PLANE)
    new = own_step(where, fixes, totals, own, other, states)
    theirs = [swapped(mine[8 * k : 8 * k + 8], "c") for k in range(2)]
    weights = ()
    for k in range(2):
        weights = (assemble(side, mine, theirs[k], k, weights),)
    return (*new, *weights)


def solution(mesh):
    finer = Mesh(mesh.devices.reshape(4, 2, 4, 8), ("y", "c", "x", "z"))
    in_specs = (P(GRP, SHARD, None, None), P(SHARD, None), P(SHARD, None), P(SHARD, None), P())
    out_specs = (P(SHARD, None), P(SHARD, None), P(SHARD, None), P())
    return jax.shard_map(
        shards, mesh=finer, in_specs=in_specs, out_specs=out_specs, check_vma=False
    )
```

time: 134 us -> 129 us (0.963)
  waiting for transfers between devices: 40 us -> 21.6 us
  blocking collectives: 37 us -> 51.6 us
    all_to_all x3, blocking collectives: 37 us -> 51.6 us  [exchanged(): return lax.all_to_all(value, axes, split_axis=0, concat_axis=0, tiled=True)]
    ppermute x10, waiting for transfers between devices: 25.1 us -> 13.4 us  [rotated(): lax.ppermute(value, axis, [(i, (i + k) % n) for i in range(n)])]
    ppermute x3 -> x5, waiting for transfers between devices: 10.1 us -> 5.51 us  [swapped(): return lax.ppermute(value, axis, [(0, 1), (1, 0)])]
    all_to_all x2, waiting for transfers between devices: 4.8 us -> 2.65 us  [exchanged(): return lax.all_to_all(value, axes, split_axis=0, concat_axis=0, tiled=True)]
    ppermute x3 -> x5, starting transfers between devices: 12.6 us -> 11.9 us  [swapped(): return lax.ppermute(value, axis, [(0, 1), (1, 0)])]
    pallas_call x1 -> x2, Pallas kernels: 2.91 us -> 3.32 us  [code_sums(): pl.pallas_call(kernel, compiler_params=LIMIT, grid_spec=pltpu.PrefetchSca...]
    pallas_call x5 -> x6, Pallas kernels: 4.88 us -> 5.2 us  [the longest x2 3.25 us: assemble(): pl.pallas_call(kernel, compiler_params=LIMIT, grid_spec=pltpu.PrefetchSca...]
  transfers between devices with their start and end apart: 15 -> 17, of which waited for: 11 -> 10; matrix products, arithmetic and copies ran while one was open for 0% -> 0% of each run, Pallas kernels for 2% -> 4%
where the time goes in v4:
time: 129 us
  blocking collectives  51.6 us (40%)
  starting transfers between devices  39.9 us (31%)
  waiting for transfers between devices  21.6 us (17%)
  Pallas kernels  11.5 us (9%)
  local copies, waits for them, and re-layouts  2.53 us (2%)
  between operations  1.47 us (1%)
    all_to_all x3, blocking collectives, exchanged(): return lax.all_to_all(value, axes, split_axis=0, concat_axis=0, tiled=True)  51.6 us
    ppermute x10, starting transfers between devices, rotated(): lax.ppermute(value, axis, [(i, (i + k) % n) for i in range(n)])  19.3 us
    ppermute x10, waiting for transfers between devices, rotated(): lax.ppermute(value, axis, [(i, (i + k) % n) for i in range(n)])  13.4 us
    ppermute x5, starting transfers between devices, swapped(): return lax.ppermute(value, axis, [(0, 1), (1, 0)])  11.9 us
    all_to_all x2, starting transfers between devices, exchanged(): return lax.all_to_all(value, axes, split_axis=0, concat_axis=0, tiled=True)  8.59 us
    ppermute x5, waiting for transfers between devices, swapped(): return lax.ppermute(value, axis, [(0, 1), (1, 0)])  5.51 us
    pallas_call x2, Pallas kernels, code_sums(): pl.pallas_call(kernel, compiler_params=LIMIT, grid_spec=pltpu.PrefetchSca...  3.32 us
    pallas_call x2, Pallas kernels, assemble(): pl.pallas_call(kernel, compiler_params=LIMIT, grid_spec=pltpu.PrefetchSca...  3.25 us
  transfers between devices with their start and end apart: 17, of which 10 were waited for; matrix products, arithmetic and copies ran while one was open for 0% of the time, Pallas kernels for 4%

profile of v4, /device:TPU:1, one launch (start us, length us, event | category | flops | bytes accessed | tf_op | source)
XLA Modules:
  0.0 128.7 jit_solution(17316931283490025704)
XLA Ops:
  0.6 2.4 %dynamic-slice_bitcast_fusion = (f32[1728,256]{1,0:T(8,128)S(1)}, f32[1728,256]{1,0:T(8,128)S(1)}) fusion(f32[1,1,3456,512]{3,2,1,0:T(8,128)} %param.5, s32[]{:T(128)S(6)} %select_n.4), kind=kLoop, calls=%fused_computation | loop fusion | bytes 7077892 | tf_op jit(solution)/shard_map/dynamic_slice | solution.py:287
  3.1 3.3 %collective-permute-start.1 = (f32[1728,256]{1,0:T(8,128)S(1)}, f32[1728,256]{1,0:T(8,128)S(1)}, u32[]{:S(2)}, u32[]{:S(2)}) collective-permute-start(f32[1728,256]{1,0:T(8,128)S(1)} %get-tuple-element.34), channel_id=1, source_target_pairs={{0,32},{32,0},{1,33},{33,1},{2,34},{34,2},{3,35},{35,3},{4,36},{36... | collective-permute-start | bytes 5308424 | tf_op jit(solution)/shard_map/ppermute | solution.py:32
  6.4 3.2 %collective-permute-done.1.theirs_ref = f32[1728,256]{1,0:T(8,128)S(1)} collective-permute-done((f32[1728,256]{1,0:T(8,128)S(1)}, f32[1728,256]{1,0:T(8,128)S(1)}, u32[]{:S(2)}, u32[]{:S(2)}) %collective-permute-start.1) | collective-permute-done | bytes 1769504 | tf_op jit(solution)/shard_map/ppermute | solution.py:32
  9.7 1.7 %shard_map.84.refs_0_ = s16[4,4,456,128]{3,2,1,0:T(8,128)(2,1)} custom-call(s32[1]{0:T(128)} %bitcast.1.c_ref, f32[3456,512]{1,0:T(8,128)S(1)} %bitcast.9, f32[1728,256]{1,0:T(8,128)S(1)} %collective-permute-done.1.theirs_ref), custom_call_target="tpu_custom_call" | custom-call | tf_op jit(solution)/shard_map/pallas_call | solution.py:63
  11.3 0.9 collective-permute-done.theirs_ref
  12.2 1.7 %shard_map.85 = s16[4,4,456,128]{3,2,1,0:T(8,128)(2,1)} custom-call(s32[1]{0:T(128)} %bitcast.1.c_ref, f32[3456,512]{1,0:T(8,128)S(1)} %bitcast.10, f32[1728,256]{1,0:T(8,128)S(1)} %collective-permute-done.theirs_ref, s16[4,4,456,128]{3,2,1,0:T(8,128)(2,1)} %shard_map.84.refs_0_), custom_call_target="tpu_custom_call", output_to_operand_aliasing={{}: (3, {})} | custom-call | tf_op jit(solution)/shard_map/pallas_call | solution.py:63
  13.9 5.2 %all-to-all-start = ((s16[16,456,128]{2,1,0:T(8,128)(2,1)}), s16[16,456,128]{2,1,0:T(8,128)(2,1)S(1)}, u32[]{:S(2)}, u32[]{:S(2)}) async-start(s16[16,456,128]{2,1,0:T(8,128)(2,1)} %bitcast.6), calls=%async_computation | async-start | bytes 3735552 | tf_op jit(solution)/shard_map/all_to_all | solution.py:28
  19.1 0.6 shard_map.86.refs_0_
  19.7 1.7 %collective-permute-start.2 = (f32[3,56,128]{2,1,0:T(8,128)S(1)}, f32[3,56,128]{2,1,0:T(8,128)S(1)}, u32[]{:S(2)}, u32[]{:S(2)}) collective-permute-start(f32[3,56,128]{2,1,0:T(8,128)S(1)} %shard_map.86.refs_0_), channel_id=1, source_target_pairs={{0,1},{1,2},{2,3},{3,4},{4,5},{5,6},{6,7},{7,0},{8,9},{9,10},{10,1... | collective-permute-start | bytes 258056 | tf_op jit(solution)/shard_map/ppermute | solution.py:37
  21.4 3.0 %collective-permute-start.3 = (f32[3,56,128]{2,1,0:T(8,128)S(1)}, f32[3,56,128]{2,1,0:T(8,128)S(1)}, u32[]{:S(2)}, u32[]{:S(2)}) collective-permute-start(f32[3,56,128]{2,1,0:T(8,128)S(1)} %shard_map.86.refs_0_), channel_id=1, source_target_pairs={{0,2},{1,3},{2,4},{3,5},{4,6},{5,7},{6,0},{7,1},{8,10},{9,11},{10,... | collective-permute-start | bytes 258056 | tf_op jit(solution)/shard_map/ppermute | solution.py:37
  24.4 3.8 %collective-permute-start.4 = (f32[3,56,128]{2,1,0:T(8,128)S(1)}, f32[3,56,128]{2,1,0:T(8,128)S(1)}, u32[]{:S(2)}, u32[]{:S(2)}) collective-permute-start(f32[3,56,128]{2,1,0:T(8,128)S(1)} %shard_map.86.refs_0_), channel_id=1, source_target_pairs={{0,3},{1,4},{2,5},{3,6},{4,7},{5,0},{6,1},{7,2},{8,11},{9,12},{10,... | collective-permute-start | bytes 258056 | tf_op jit(solution)/shard_map/ppermute | solution.py:37
  28.6 4.5 %collective-permute-start.6 = (f32[3,56,128]{2,1,0:T(8,128)S(1)}, f32[3,56,128]{2,1,0:T(8,128)S(1)}, u32[]{:S(2)}, u32[]{:S(2)}) collective-permute-start(f32[3,56,128]{2,1,0:T(8,128)S(1)} %shard_map.86.refs_0_), channel_id=1, source_target_pairs={{0,5},{1,6},{2,7},{3,0},{4,1},{5,2},{6,3},{7,4},{8,13},{9,14},{10,... | collective-permute-start | bytes 258056 | tf_op jit(solution)/shard_map/ppermute | solution.py:37
  33.9 2.5 %collective-permute-start.7 = (f32[3,56,128]{2,1,0:T(8,128)S(1)}, f32[3,56,128]{2,1,0:T(8,128)S(1)}, u32[]{:S(2)}, u32[]{:S(2)}) collective-permute-start(f32[3,56,128]{2,1,0:T(8,128)S(1)} %shard_map.86.refs_0_), channel_id=1, source_target_pairs={{0,6},{1,7},{2,0},{3,1},{4,2},{5,3},{6,4},{7,5},{8,14},{9,15},{10,... | collective-permute-start | bytes 258056 | tf_op jit(solution)/shard_map/ppermute | solution.py:37
  36.3 0.7 collective-permute-start.8
  37.1 2.0 %collective-permute-done.5.refs_4_ = f32[3,56,128]{2,1,0:T(8,128)S(1)} collective-permute-done((f32[3,56,128]{2,1,0:T(8,128)S(1)}, f32[3,56,128]{2,1,0:T(8,128)S(1)}, u32[]{:S(2)}, u32[]{:S(2)}) %collective-permute-start.5) | collective-permute-done | bytes 86048 | tf_op jit(solution)/shard_map/ppermute | solution.py:37
  39.2 7.2 %collective-permute-done.7.refs_6_ = f32[3,56,128]{2,1,0:T(8,128)S(1)} collective-permute-done((f32[3,56,128]{2,1,0:T(8,128)S(1)}, f32[3,56,128]{2,1,0:T(8,128)S(1)}, u32[]{:S(2)}, u32[]{:S(2)}) %collective-permute-start.7) | collective-permute-done | bytes 86048 | tf_op jit(solution)/shard_map/ppermute | solution.py:37
  47.1 15.7 %all_to_all.25.sums_ref = f32[8,56,128]{2,1,0:T(8,128)S(1)} all-to-all(f32[8,56,128]{2,1,0:T(8,128)S(1)} %shard_map.87), channel_id=1, replica_groups=mesh['y'=4,'c'=2,'x'=4,'z'=8] {'z'}, dimensions={0} | all-to-all | bytes 458752 | tf_op jit(solution)/shard_map/all_to_all | solution.py:28
  62.8 1.4 %shard_map.88 = (f32[56,128]{1,0:T(8,128)S(1)}, f32[8,64,128]{2,1,0:T(8,128)}) custom-call(s32[3]{0:T(128)S(1)} %pad_add_fusion.where_ref, f32[8,56,128]{2,1,0:T(8,128)S(1)} %all_to_all.25.sums_ref), custom_call_target="tpu_custom_call" | custom-call | tf_op jit(solution)/shard_map/pallas_call | solution.py:116
  64.2 3.4 %all-to-all-start.2 = ((f32[8,64,128]{2,1,0:T(8,128)}), f32[8,64,128]{2,1,0:T(8,128)S(1)}, u32[]{:S(2)}, u32[]{:S(2)}) async-start(f32[8,64,128]{2,1,0:T(8,128)} %get-tuple-element.21), calls=%async_computation.2 | async-start | bytes 524288 | tf_op jit(solution)/shard_map/all_to_all | solution.py:28
  68.0 2.4 %collective-permute-start.11 = (f32[56,128]{1,0:T(8,128)S(1)}, f32[56,128]{1,0:T(8,128)S(1)}, u32[]{:S(2)}, u32[]{:S(2)}) collective-permute-start(f32[56,128]{1,0:T(8,128)S(1)} %get-tuple-element.22.refs_0_), channel_id=1, source_target_pairs={{0,192},{64,0},{128,64},{192,128},{1,193},{65,1},{129,65},{193,129... | collective-permute-start | bytes 86024 | tf_op jit(solution)/shard_map/ppermute | solution.py:37
  70.4 1.5 %collective-permute-done.10.refs_2_ = f32[56,128]{1,0:T(8,128)S(1)} collective-permute-done((f32[56,128]{1,0:T(8,128)S(1)}, f32[56,128]{1,0:T(8,128)S(1)}, u32[]{:S(2)}, u32[]{:S(2)}) %collective-permute-start.10) | collective-permute-done | bytes 28704 | tf_op jit(solution)/shard_map/ppermute | solution.py:37
  72.0 2.4 %collective-permute-done.9.refs_1_ = f32[56,128]{1,0:T(8,128)S(1)} collective-permute-done((f32[56,128]{1,0:T(8,128)S(1)}, f32[56,128]{1,0:T(8,128)S(1)}, u32[]{:S(2)}, u32[]{:S(2)}) %collective-permute-start.9) | collective-permute-done | bytes 28704 | tf_op jit(solution)/shard_map/ppermute | solution.py:37
  74.3 2.6 %all-to-all-done.2.column_ref = f32[8,64,128]{2,1,0:T(8,128)S(1)} async-done(((f32[8,64,128]{2,1,0:T(8,128)}), f32[8,64,128]{2,1,0:T(8,128)S(1)}, u32[]{:S(2)}, u32[]{:S(2)}) %all-to-all-start.2) | async-done | bytes 262176 | tf_op jit(solution)/shard_map/all_to_all | solution.py:28
  77.0 5.0 %collective-permute-start.12 = (f32[232,128]{1,0:T(8,128)S(1)}, f32[232,128]{1,0:T(8,128)S(1)}, u32[]{:S(2)}, u32[]{:S(2)}) collective-permute-start(f32[232,128]{1,0:T(8,128)S(1)} %shard_map.89.mine_ref), channel_id=1, source_target_pairs={{0,32},{32,0},{1,33},{33,1},{2,34},{34,2},{3,35},{35,3},{4,36},{36... | collective-permute-start | bytes 356360 | tf_op jit(solution)/shard_map/ppermute | solution.py:32
  82.0 1.0 collective-permute-done.12.theirs_ref
  83.0 9.7 %all_to_all.26.totals_ref = f32[16,8,128]{2,1,0:T(8,128)S(1)} all-to-all(f32[16,8,128]{2,1,0:T(8,128)S(1)} %shard_map.90), channel_id=1, replica_groups=mesh['y'=4,'c'=2,'x'=4,'z'=8] {'x','y'}, dimensions={0} | all-to-all | bytes 131072 | tf_op jit(solution)/shard_map/all_to_all | solution.py:28
  92.7 0.9 shard_map.92
  93.6 26.2 %all_to_all.27.mine_ref = bf16[16,448,128]{2,1,0:T(8,128)(2,1)S(1)} all-to-all(bf16[16,448,128]{2,1,0:T(8,128)(2,1)S(1)} %shard_map.92), channel_id=1, replica_groups=mesh['y'=4,'c'=2,'x'=4,'z'=8] {'x','y'}, dimensions={0} | all-to-all | bytes 3670016 | tf_op jit(solution)/shard_map/all_to_all | solution.py:28
  119.9 3.5 %collective-permute-start.14 = (bf16[8,448,128]{2,1,0:T(8,128)(2,1)S(1)}, bf16[8,448,128]{2,1,0:T(8,128)(2,1)S(1)}, u32[]{:S(2)}, u32[]{:S(2)}) collective-permute-start(bf16[8,448,128]{2,1,0:T(8,128)(2,1)S(1)} %get-tuple-element.36), channel_id=1, source_target_pairs={{0,32},{32,0},{1,33},{33,1},{2,34},{34,2},{3,35},{35,3},{4,36},{36... | collective-permute-start | bytes 2752520 | tf_op jit(solution)/shard_map/ppermute | solution.py:32
  123.4 1.5 %shard_map.91 = (f32[108,512]{1,0:T(8,128)}, f32[108,512]{1,0:T(8,128)}, f32[108,512]{1,0:T(8,128)}) custom-call(s32[3]{0:T(128)S(1)} %pad_add_fusion.where_ref, f32[2]{0:T(128)S(1)} %pad_maximum_fusion.fixes_ref, f32[16,8,128]{2,1,0:T(8,128)S(1)} %all_to_all.26.totals_ref, f32[232,128]{1,0:T(8,128)S(1)} %shard_map.89.mine_ref, ...), custom_call_target="tpu_custom_call" | custom-call | tf_op jit(solution)/shard_map/pallas_call | solution.py:239
  125.4 1.6 %shard_map.93.refs_0_ = bf16[3456,512]{1,0:T(8,128)(2,1)} custom-call(s32[1]{0:T(128)} %bitcast.1.c_ref, bf16[16,448,128]{2,1,0:T(8,128)(2,1)S(1)} %all_to_all.27.mine_ref, bf16[8,448,128]{2,1,0:T(8,128)(2,1)S(1)} %collective-permute-done.14.theirs_ref), custom_call_target="tpu_custom_call" | custom-call | tf_op jit(solution)/shard_map/pallas_call | solution.py:263
  127.1 1.6 %shard_map.94 = bf16[3456,512]{1,0:T(8,128)(2,1)} custom-call(s32[1]{0:T(128)} %bitcast.1.c_ref, bf16[16,448,128]{2,1,0:T(8,128)(2,1)S(1)} %all_to_all.27.mine_ref, bf16[8,448,128]{2,1,0:T(8,128)(2,1)S(1)} %collective-permute-done.13.theirs_ref, bf16[3456,512]{1,0:T(8,128)(2,1)} %shard_map.93.refs_0_), custom_call_target="tpu_custom_call", output_to_operand_aliasing={{}: (3, {})} | custom-call | tf_op jit(solution)/shard_map/pallas_call | solution.py:263
  (28 shorter events, 2.6 us)
Async XLA Ops:
  0.6 9.0 %copy-start = (f32[1,1,3456,512]{3,2,1,0:T(8,128)S(1)}, f32[1,1,3456,512]{3,2,1,0:T(8,128)}, u32[]{:S(2)}) copy-start(f32[1,1,3456,512]{3,2,1,0:T(8,128)} %param.5) | copy-start | bytes 21233668
  3.1 6.6 %collective-permute-start.1 = (f32[1728,256]{1,0:T(8,128)S(1)}, f32[1728,256]{1,0:T(8,128)S(1)}, u32[]{:S(2)}, u32[]{:S(2)}) collective-permute-start(f32[1728,256]{1,0:T(8,128)S(1)} %get-tuple-element.34), channel_id=1, source_target_pairs={{0,32},{32,0},{1,33},{33,1},{2,34},{34,2},{3,35},{35,3},{4,36},{36... | collective-permute-start | bytes 5308424 | tf_op jit(solution)/shard_map/ppermute | solution.py:32
  6.3 5.8 %collective-permute-start = (f32[1728,256]{1,0:T(8,128)S(1)}, f32[1728,256]{1,0:T(8,128)S(1)}, u32[]{:S(2)}, u32[]{:S(2)}) collective-permute-start(f32[1728,256]{1,0:T(8,128)S(1)} %get-tuple-element.35), channel_id=1, source_target_pairs={{0,32},{32,0},{1,33},{33,1},{2,34},{34,2},{3,35},{35,3},{4,36},{36... | collective-permute-start | bytes 5308424 | tf_op jit(solution)/shard_map/ppermute | solution.py:32
  13.9 5.3 %copy-start.1 = (f32[108,512]{1,0:T(8,128)S(1)}, f32[108,512]{1,0:T(8,128)}, u32[]{:S(2)}) copy-start(f32[108,512]{1,0:T(8,128)} %refs_0_.3) | copy-start | bytes 663556
  13.9 5.3 %copy-start.2 = (f32[108,512]{1,0:T(8,128)S(1)}, f32[108,512]{1,0:T(8,128)}, u32[]{:S(2)}) copy-start(f32[108,512]{1,0:T(8,128)} %refs_1_.3) | copy-start | bytes 663556
  13.9 5.3 %copy-start.3 = (f32[108,512]{1,0:T(8,128)S(1)}, f32[108,512]{1,0:T(8,128)}, u32[]{:S(2)}) copy-start(f32[108,512]{1,0:T(8,128)} %refs_2_.3) | copy-start | bytes 663556
  13.9 32.7 %all-to-all-start = ((s16[16,456,128]{2,1,0:T(8,128)(2,1)}), s16[16,456,128]{2,1,0:T(8,128)(2,1)S(1)}, u32[]{:S(2)}, u32[]{:S(2)}) async-start(s16[16,456,128]{2,1,0:T(8,128)(2,1)} %bitcast.6), calls=%async_computation | async-start | bytes 3735552 | tf_op jit(solution)/shard_map/all_to_all | solution.py:28
  19.7 14.1 %collective-permute-start.2 = (f32[3,56,128]{2,1,0:T(8,128)S(1)}, f32[3,56,128]{2,1,0:T(8,128)S(1)}, u32[]{:S(2)}, u32[]{:S(2)}) collective-permute-start(f32[3,56,128]{2,1,0:T(8,128)S(1)} %shard_map.86.refs_0_), channel_id=1, source_target_pairs={{0,1},{1,2},{2,3},{3,4},{4,5},{5,6},{6,7},{7,0},{8,9},{9,10},{10,1... | collective-permute-start | bytes 258056 | tf_op jit(solution)/shard_map/ppermute | solution.py:37
  21.4 14.9 %collective-permute-start.3 = (f32[3,56,128]{2,1,0:T(8,128)S(1)}, f32[3,56,128]{2,1,0:T(8,128)S(1)}, u32[]{:S(2)}, u32[]{:S(2)}) collective-permute-start(f32[3,56,128]{2,1,0:T(8,128)S(1)} %shard_map.86.refs_0_), channel_id=1, source_target_pairs={{0,2},{1,3},{2,4},{3,5},{4,6},{5,7},{6,0},{7,1},{8,10},{9,11},{10,... | collective-permute-start | bytes 258056 | tf_op jit(solution)/shard_map/ppermute | solution.py:37
  24.4 12.7 %collective-permute-start.4 = (f32[3,56,128]{2,1,0:T(8,128)S(1)}, f32[3,56,128]{2,1,0:T(8,128)S(1)}, u32[]{:S(2)}, u32[]{:S(2)}) collective-permute-start(f32[3,56,128]{2,1,0:T(8,128)S(1)} %shard_map.86.refs_0_), channel_id=1, source_target_pairs={{0,3},{1,4},{2,5},{3,6},{4,7},{5,0},{6,1},{7,2},{8,11},{9,12},{10,... | collective-permute-start | bytes 258056 | tf_op jit(solution)/shard_map/ppermute | solution.py:37
  28.2 11.0 %collective-permute-start.5 = (f32[3,56,128]{2,1,0:T(8,128)S(1)}, f32[3,56,128]{2,1,0:T(8,128)S(1)}, u32[]{:S(2)}, u32[]{:S(2)}) collective-permute-start(f32[3,56,128]{2,1,0:T(8,128)S(1)} %shard_map.86.refs_0_), channel_id=1, source_target_pairs={{0,4},{1,5},{2,6},{3,7},{4,0},{5,1},{6,2},{7,3},{8,12},{9,13},{10,... | collective-permute-start | bytes 258056 | tf_op jit(solution)/shard_map/ppermute | solution.py:37
  28.6 10.5 %collective-permute-start.6 = (f32[3,56,128]{2,1,0:T(8,128)S(1)}, f32[3,56,128]{2,1,0:T(8,128)S(1)}, u32[]{:S(2)}, u32[]{:S(2)}) collective-permute-start(f32[3,56,128]{2,1,0:T(8,128)S(1)} %shard_map.86.refs_0_), channel_id=1, source_target_pairs={{0,5},{1,6},{2,7},{3,0},{4,1},{5,2},{6,3},{7,4},{8,13},{9,14},{10,... | collective-permute-start | bytes 258056 | tf_op jit(solution)/shard_map/ppermute | solution.py:37
  33.9 12.5 %collective-permute-start.7 = (f32[3,56,128]{2,1,0:T(8,128)S(1)}, f32[3,56,128]{2,1,0:T(8,128)S(1)}, u32[]{:S(2)}, u32[]{:S(2)}) collective-permute-start(f32[3,56,128]{2,1,0:T(8,128)S(1)} %shard_map.86.refs_0_), channel_id=1, source_target_pairs={{0,6},{1,7},{2,0},{3,1},{4,2},{5,3},{6,4},{7,5},{8,14},{9,15},{10,... | collective-permute-start | bytes 258056 | tf_op jit(solution)/shard_map/ppermute | solution.py:37
  36.3 10.3 %collective-permute-start.8 = (f32[3,56,128]{2,1,0:T(8,128)S(1)}, f32[3,56,128]{2,1,0:T(8,128)S(1)}, u32[]{:S(2)}, u32[]{:S(2)}) collective-permute-start(f32[3,56,128]{2,1,0:T(8,128)S(1)} %shard_map.86.refs_0_), channel_id=1, source_target_pairs={{0,7},{1,0},{2,1},{3,2},{4,3},{5,4},{6,5},{7,6},{8,15},{9,8},{10,9... | collective-permute-start | bytes 258056 | tf_op jit(solution)/shard_map/ppermute | solution.py:37
  64.2 12.8 %all-to-all-start.2 = ((f32[8,64,128]{2,1,0:T(8,128)}), f32[8,64,128]{2,1,0:T(8,128)S(1)}, u32[]{:S(2)}, u32[]{:S(2)}) async-start(f32[8,64,128]{2,1,0:T(8,128)} %get-tuple-element.21), calls=%async_computation.2 | async-start | bytes 524288 | tf_op jit(solution)/shard_map/all_to_all | solution.py:28
  67.7 4.3 %collective-permute-start.10 = (f32[56,128]{1,0:T(8,128)S(1)}, f32[56,128]{1,0:T(8,128)S(1)}, u32[]{:S(2)}, u32[]{:S(2)}) collective-permute-start(f32[56,128]{1,0:T(8,128)S(1)} %get-tuple-element.22.refs_0_), channel_id=1, source_target_pairs={{0,128},{64,192},{128,0},{192,64},{1,129},{65,193},{129,1},{193,65... | collective-permute-start | bytes 86024 | tf_op jit(solution)/shard_map/ppermute | solution.py:37
  68.0 3.9 %collective-permute-start.11 = (f32[56,128]{1,0:T(8,128)S(1)}, f32[56,128]{1,0:T(8,128)S(1)}, u32[]{:S(2)}, u32[]{:S(2)}) collective-permute-start(f32[56,128]{1,0:T(8,128)S(1)} %get-tuple-element.22.refs_0_), channel_id=1, source_target_pairs={{0,192},{64,0},{128,64},{192,128},{1,193},{65,1},{129,65},{193,129... | collective-permute-start | bytes 86024 | tf_op jit(solution)/shard_map/ppermute | solution.py:37
  70.4 3.9 %collective-permute-start.9 = (f32[56,128]{1,0:T(8,128)S(1)}, f32[56,128]{1,0:T(8,128)S(1)}, u32[]{:S(2)}, u32[]{:S(2)}) collective-permute-start(f32[56,128]{1,0:T(8,128)S(1)} %get-tuple-element.22.refs_0_), channel_id=1, source_target_pairs={{0,64},{64,128},{128,192},{192,0},{1,65},{65,129},{129,193},{193,1... | collective-permute-start | bytes 86024 | tf_op jit(solution)/shard_map/ppermute | solution.py:37
  77.0 6.0 %collective-permute-start.12 = (f32[232,128]{1,0:T(8,128)S(1)}, f32[232,128]{1,0:T(8,128)S(1)}, u32[]{:S(2)}, u32[]{:S(2)}) collective-permute-start(f32[232,128]{1,0:T(8,128)S(1)} %shard_map.89.mine_ref), channel_id=1, source_target_pairs={{0,32},{32,0},{1,33},{33,1},{2,34},{34,2},{3,35},{35,3},{4,36},{36... | collective-permute-start | bytes 356360 | tf_op jit(solution)/shard_map/ppermute | solution.py:32
  119.9 5.6 %collective-permute-start.14 = (bf16[8,448,128]{2,1,0:T(8,128)(2,1)S(1)}, bf16[8,448,128]{2,1,0:T(8,128)(2,1)S(1)}, u32[]{:S(2)}, u32[]{:S(2)}) collective-permute-start(bf16[8,448,128]{2,1,0:T(8,128)(2,1)S(1)} %get-tuple-element.36), channel_id=1, source_target_pairs={{0,32},{32,0},{1,33},{33,1},{2,34},{34,2},{3,35},{35,3},{4,36},{36... | collective-permute-start | bytes 2752520 | tf_op jit(solution)/shard_map/ppermute | solution.py:32
  123.3 3.7 %collective-permute-start.13 = (bf16[8,448,128]{2,1,0:T(8,128)(2,1)S(1)}, bf16[8,448,128]{2,1,0:T(8,128)(2,1)S(1)}, u32[]{:S(2)}, u32[]{:S(2)}) collective-permute-start(bf16[8,448,128]{2,1,0:T(8,128)(2,1)S(1)} %get-tuple-element.37), channel_id=1, source_target_pairs={{0,32},{32,0},{1,33},{33,1},{2,34},{34,2},{3,35},{35,3},{4,36},{36... | collective-permute-start | bytes 2752520 | tf_op jit(solution)/shard_map/ppermute | solution.py:32

commit v5 on v4

--- a/solution.py
+++ b/solution.py
@@ -24,6 +24,10 @@
     return pltpu.with_memory_space_constraint(value, pltpu.VMEM)
 
 
+def in_hbm(value):
+    return pltpu.with_memory_space_constraint(value, pltpu.HBM)
+
+
 def exchanged(value, axes):
     return lax.all_to_all(value, axes, split_axis=0, concat_axis=0, tiled=True)
 
@@ -37,28 +41,63 @@
     return [value] + [lax.ppermute(value, axis, [(i, (i + k) % n) for i in range(n)]) for k in range(1, n)]
 
 
+def scale_of(level):
+    return jnp.exp2(0.25 * level.astype(jnp.int32).astype(jnp.float32)) * (1.0 / 32767.0)
+
+
+def coded_block(value):
+    peak = jnp.max(jnp.abs(value), axis=0, keepdims=True)
+    level = jnp.maximum(jnp.ceil(4.0 * jnp.log2(peak) + 0.02), -400.0)
+    scaled = jnp.round(value * (32767.0 * jnp.exp2(-0.25 * level)))
+    return scaled.astype(jnp.int32).astype(jnp.int16), level
+
+
+def decoded(block, scale):
+    return block.astype(jnp.int32).astype(jnp.float32) * scale
+
+
+def code(out_ref, value_of):
+    row = lax.broadcasted_iota(jnp.int32, (8, 128), 0)
+    levels = jnp.zeros((8, 128), jnp.float32)
+    for z in range(8):
+        block, level = coded_block(value_of(z))
+        levels = jnp.where(row == z, level, levels)
+        out_ref[pl.ds(z * PART, PART), :] = block
+    out_ref[pl.ds(COLUMN, 8), :] = levels.astype(jnp.int32).astype(jnp.int16)
+
+
+def half_kernel(c_ref, local_ref, out_ref):
+    for y in range(4):
+        cols = pl.ds((y // 2) * 128, 128)
+        code(out_ref.at[0, y], lambda z: local_ref[pl.ds(108 * z + STARTS[y % 2], PART), cols])
+
+
+def code_half(c, local, piece):
+    return pl.pallas_call(
+        half_kernel,
+        compiler_params=LIMIT,
+        grid_spec=pltpu.PrefetchScalarGridSpec(
+            num_scalar_prefetch=1,
+            grid=(2,),
+            in_specs=[pl.BlockSpec((864, 256), lambda i, c: (2 * piece + i, 1 - c[0]))],
+            out_specs=pl.BlockSpec((1, 4, COLUMN + 8, 128), lambda i, c: (i, 0, 0, 0)),
+        ),
+        out_shape=jax.ShapeDtypeStruct((2, 4, COLUMN + 8, 128), jnp.int16),
+    )(c, in_hbm(local))
+
+
 def code_sums(c, local, theirs, piece, coded):
     def kernel(c_ref, mine_ref, theirs_ref, *refs):
-        out_ref, sums = refs[-2:]
+        out_ref = refs[-1]
         for x, y in ((x, y) for x in range(2) for y in range(4)):
-            lane = (y // 2) * 128
-            mine_cols = pl.ds(pl.multiple_of(256 * c_ref[0] + lane, 128), 128)
-            peak = jnp.zeros((8, 128), jnp.float32)
-            for z in range(8):
-                start = 864 * x + 108 * z + STARTS[y % 2]
-                for t in range(0, PART, 8):
-                    mine = mine_ref[pl.ds(1728 * piece + start + t, 8), mine_cols]
-                    value = mine + theirs_ref[pl.ds(start + t, 8), pl.ds(lane, 128)]
-                    peak = jnp.maximum(peak, jnp.abs(value))
-                    sums[pl.ds(z * PART + t, 8), :] = value
-            peak = jnp.max(peak, axis=0, keepdims=True)
-            level = jnp.maximum(jnp.ceil(4.0 * jnp.log2(peak) + 0.02), -400.0)
-            inverse = 32767.0 * jnp.exp2(-0.25 * level)
-            for t in range(0, COLUMN, PART):
-                scaled = jnp.round(sums[pl.ds(t, PART), :] * inverse)
-                out_ref[x, y, pl.ds(t, PART), :] = scaled.astype(jnp.int32).astype(jnp.int16)
-            level = jnp.broadcast_to(level, (8, 128))
-            out_ref[x, y, pl.ds(COLUMN, 8), :] = level.astype(jnp.int32).astype(jnp.int16)
+            cols = pl.ds(pl.multiple_of(256 * c_ref[0] + (y // 2) * 128, 128), 128)
+            scales = scale_of(theirs_ref[x, y, pl.ds(COLUMN, 8), :])
+
+            def value_of(z):
+                mine = mine_ref[pl.ds(1728 * piece + 864 * x + 108 * z + STARTS[y % 2], PART), cols]
+                return mine + decoded(theirs_ref[x, y, pl.ds(z * PART, PART), :], scales[z : z + 1])
+
+            code(out_ref.at[x, y], value_of)
 
     return pl.pallas_call(
         kernel,
@@ -68,7 +107,6 @@
             grid=(1,),
             in_specs=[VMEM, VMEM] + [ANY] * len(coded),
             out_specs=pl.BlockSpec((2, 4, COLUMN + 8, 128), lambda i, c: (piece, 0, 0, 0)),
-            scratch_shapes=[pltpu.VMEM((COLUMN, 128), jnp.float32)],
         ),
         out_shape=jax.ShapeDtypeStruct((4, 4, COLUMN + 8, 128), jnp.int16),
         input_output_aliases={3: 0} if coded else {},
@@ -76,17 +114,16 @@
 
 
 def sum_kernel(coded_ref, out_ref):
-    scales = []
-    for k in range(16):
-        level = coded_ref[k, pl.ds(COLUMN, 8), :].astype(jnp.int32).astype(jnp.float32)
-        scales.append(jnp.exp2(0.25 * level) * (1.0 / 32767.0))
+    scales = [scale_of(coded_ref[k, pl.ds(COLUMN, 8), :]) for k in range(16)]
     for z in range(8):
         rows = pl.ds(z * PART, PART)
-        total = jnp.zeros((PART // 8, 8, 128), jnp.float32)
+        total = jnp.zeros((PART, 128), jnp.float32)
         for k in range(16):
-            value = coded_ref[k, rows, :].astype(jnp.int32).astype(jnp.float32)
-            total = total + value.reshape(PART // 8, 8, 128) * scales[k]
-        out_ref[z] = total.reshape(PART, 128)
+            total = total + decoded(coded_ref[k, rows, :], scales[k][z : z + 1])
+        block, level = coded_block(total)
+        out_ref[z, pl.ds(0, PART), :] = block
+        level = jnp.broadcast_to(level, (8, 128))
+        out_ref[z, pl.ds(PART, 8), :] = level.astype(jnp.int32).astype(jnp.int16)
 
 
 def sum_coded(coded):
@@ -95,14 +132,15 @@
         compiler_params=LIMIT,
         in_specs=[VMEM],
         out_specs=VMEM,
-        out_shape=jax.ShapeDtypeStruct((8, PART, 128), jnp.float32),
+        out_shape=jax.ShapeDtypeStruct((8, PART + 8, 128), jnp.int16),
     )(in_vmem(coded))
 
 
 def part_kernel(where_ref, sums_ref, part_ref, out_ref):
-    part = sums_ref[0]
-    for k in range(1, 8):
-        part = part + sums_ref[k]
+    part = jnp.zeros((PART, 128), jnp.float32)
+    for k in range(8):
+        scale = scale_of(sums_ref[k, pl.ds(PART, 8), :])[:1]
+        part = part + decoded(sums_ref[k, pl.ds(0, PART), :], scale)
     part_ref[...] = part
     row = lax.broadcasted_iota(jnp.int32, part.shape, 0)
     counted = (row >= SHARED) | (where_ref[0] % 2 == 0)
@@ -284,7 +322,7 @@
     second_fix = 1.0 - jnp.power(jnp.float32(0.999), steps)
     fixes = jnp.stack([first_fix, second_fix])
     local = grads[0, 0]
-    theirs = [swapped(lax.dynamic_slice(local, (1728 * k, 256 * (1 - c)), (1728, 256)), "c") for k in range(2)]
+    theirs = [swapped(code_half(side, local, k), "c") for k in range(2)]
     coded = ()
     for k in range(2):
         coded = (code_sums(side, local, theirs[k], k, coded),)

time: 129 us -> 128 us (level)
  waiting for transfers between devices: 21.6 us -> 17.2 us
  Pallas kernels: 11.5 us -> 15.7 us
    ppermute x5, waiting for transfers between devices: 5.51 us -> 1.49 us  [swapped(): return lax.ppermute(value, axis, [(0, 1), (1, 0)])]
    pallas_call x0 -> x2, Pallas kernels: none -> 3.7 us  [code_half(): pl.pallas_call(half_kernel, compiler_params=LIMIT, grid_spec=pltpu.Prefet...]
    dynamic_slice x1 -> x0, local copies, waits for them, and re-layouts: 2.4 us -> none  [shards(): lax.dynamic_slice(local, (1728 * k, 256 * (1 - c)), (1728, 256))]
    unnamed x8, local copies, waits for them, and re-layouts: 0.02 us -> 1.43 us
  transfers between devices with their start and end apart: 17 -> 17, of which waited for: 10 -> 11; matrix products, arithmetic and copies ran while one was open for 0% -> 0% of each run, Pallas kernels for 4% -> 6%
where the time goes in v5:
time: 128 us
  blocking collectives  51.8 us (40%)
  starting transfers between devices  39.9 us (31%)
  waiting for transfers between devices  17.2 us (13%)
  Pallas kernels  15.7 us (12%)
  local copies, waits for them, and re-layouts  1.55 us (1%)
  between operations  1.47 us (1%)
    all_to_all x3, blocking collectives, exchanged(): return lax.all_to_all(value, axes, split_axis=0, concat_axis=0, tiled=True)  51.8 us
    ppermute x10, starting transfers between devices, rotated(): lax.ppermute(value, axis, [(i, (i + k) % n) for i in range(n)])  20 us
    ppermute x10, waiting for transfers between devices, rotated(): lax.ppermute(value, axis, [(i, (i + k) % n) for i in range(n)])  13.2 us
    ppermute x5, starting transfers between devices, swapped(): return lax.ppermute(value, axis, [(0, 1), (1, 0)])  11.2 us
    all_to_all x2, starting transfers between devices, exchanged(): return lax.all_to_all(value, axes, split_axis=0, concat_axis=0, tiled=True)  8.59 us
    pallas_call x2, Pallas kernels, code_half(): pl.pallas_call(half_kernel, compiler_params=LIMIT, grid_spec=pltpu.Prefet...  3.7 us
    pallas_call x2, Pallas kernels, code_sums(): pl.pallas_call(kernel, compiler_params=LIMIT, grid_spec=pltpu.PrefetchSca...  3.65 us
    pallas_call x2, Pallas kernels, assemble(): pl.pallas_call(kernel, compiler_params=LIMIT, grid_spec=pltpu.PrefetchSca...  3.25 us
  transfers between devices with their start and end apart: 17, of which 11 were waited for; matrix products, arithmetic and copies ran while one was open for 0% of the time, Pallas kernels for 6%

profile of v5, /device:TPU:1, one launch (start us, length us, event | category | flops | bytes accessed | tf_op | source)
XLA Modules:
  0.0 127.7 jit_solution(3756873321943440593)
XLA Ops:
  0.6 1.8 %shard_map.85 = s16[2,4,456,128]{3,2,1,0:T(8,128)(2,1)S(1)} custom-call(s32[1]{0:T(128)} %bitcast.1.c_ref, f32[3456,512]{1,0:T(8,128)} %bitcast.5), custom_call_target="tpu_custom_call" | custom-call | tf_op jit(solution)/shard_map/pallas_call | solution.py:76
  2.4 3.3 %collective-permute-start.1 = (s16[2,4,456,128]{3,2,1,0:T(8,128)(2,1)S(1)}, s16[2,4,456,128]{3,2,1,0:T(8,128)(2,1)S(1)}, u32[]{:S(2)}, u32[]{:S(2)}) collective-permute-start(s16[2,4,456,128]{3,2,1,0:T(8,128)(2,1)S(1)} %shard_map.85), channel_id=1, source_target_pairs={{0,32},{32,0},{1,33},{33,1},{2,34},{34,2},{3,35},{35,3},{4,36},{36... | collective-permute-start | bytes 2801672 | tf_op jit(solution)/shard_map/ppermute | solution.py:36
  5.7 1.9 %shard_map.84 = s16[2,4,456,128]{3,2,1,0:T(8,128)(2,1)S(1)} custom-call(s32[1]{0:T(128)} %bitcast.1.c_ref, f32[3456,512]{1,0:T(8,128)} %bitcast.6), custom_call_target="tpu_custom_call" | custom-call | tf_op jit(solution)/shard_map/pallas_call | solution.py:76
  7.8 1.4 %copy-done = f32[1,1,3456,512]{3,2,1,0:T(8,128)S(1)} copy-done((f32[1,1,3456,512]{3,2,1,0:T(8,128)S(1)}, f32[1,1,3456,512]{3,2,1,0:T(8,128)}, u32[]{:S(2)}) %copy-start) | copy-done | bytes 7077912
  9.3 1.8 %shard_map.86.refs_0_ = s16[4,4,456,128]{3,2,1,0:T(8,128)(2,1)} custom-call(s32[1]{0:T(128)} %bitcast.1.c_ref, f32[3456,512]{1,0:T(8,128)S(1)} %bitcast.7, s16[2,4,456,128]{3,2,1,0:T(8,128)(2,1)S(1)} %collective-permute-done.1.theirs_ref), custom_call_target="tpu_custom_call" | custom-call | tf_op jit(solution)/shard_map/pallas_call | solution.py:102
  11.1 1.8 %shard_map.87 = s16[4,4,456,128]{3,2,1,0:T(8,128)(2,1)} custom-call(s32[1]{0:T(128)} %bitcast.1.c_ref, f32[3456,512]{1,0:T(8,128)S(1)} %bitcast.8, s16[2,4,456,128]{3,2,1,0:T(8,128)(2,1)S(1)} %collective-permute-done.theirs_ref, s16[4,4,456,128]{3,2,1,0:T(8,128)(2,1)} %shard_map.86.refs_0_), custom_call_target="tpu_custom_call", output_to_operand_aliasing={{}: (3, {})} | custom-call | tf_op jit(solution)/shard_map/pallas_call | solution.py:102
  12.9 5.2 %all-to-all-start = ((s16[16,456,128]{2,1,0:T(8,128)(2,1)}), s16[16,456,128]{2,1,0:T(8,128)(2,1)S(1)}, u32[]{:S(2)}, u32[]{:S(2)}) async-start(s16[16,456,128]{2,1,0:T(8,128)(2,1)} %bitcast.4), calls=%async_computation | async-start | bytes 3735552 | tf_op jit(solution)/shard_map/all_to_all | solution.py:32
  18.8 1.7 %collective-permute-start.2 = (f32[3,56,128]{2,1,0:T(8,128)S(1)}, f32[3,56,128]{2,1,0:T(8,128)S(1)}, u32[]{:S(2)}, u32[]{:S(2)}) collective-permute-start(f32[3,56,128]{2,1,0:T(8,128)S(1)} %shard_map.88.refs_0_), channel_id=1, source_target_pairs={{0,1},{1,2},{2,3},{3,4},{4,5},{5,6},{6,7},{7,0},{8,9},{9,10},{10,1... | collective-permute-start | bytes 258056 | tf_op jit(solution)/shard_map/ppermute | solution.py:41
  20.5 3.0 %collective-permute-start.3 = (f32[3,56,128]{2,1,0:T(8,128)S(1)}, f32[3,56,128]{2,1,0:T(8,128)S(1)}, u32[]{:S(2)}, u32[]{:S(2)}) collective-permute-start(f32[3,56,128]{2,1,0:T(8,128)S(1)} %shard_map.88.refs_0_), channel_id=1, source_target_pairs={{0,2},{1,3},{2,4},{3,5},{4,6},{5,7},{6,0},{7,1},{8,10},{9,11},{10,... | collective-permute-start | bytes 258056 | tf_op jit(solution)/shard_map/ppermute | solution.py:41
  23.5 3.8 %collective-permute-start.4 = (f32[3,56,128]{2,1,0:T(8,128)S(1)}, f32[3,56,128]{2,1,0:T(8,128)S(1)}, u32[]{:S(2)}, u32[]{:S(2)}) collective-permute-start(f32[3,56,128]{2,1,0:T(8,128)S(1)} %shard_map.88.refs_0_), channel_id=1, source_target_pairs={{0,3},{1,4},{2,5},{3,6},{4,7},{5,0},{6,1},{7,2},{8,11},{9,12},{10,... | collective-permute-start | bytes 258056 | tf_op jit(solution)/shard_map/ppermute | solution.py:41
  27.7 4.5 %collective-permute-start.6 = (f32[3,56,128]{2,1,0:T(8,128)S(1)}, f32[3,56,128]{2,1,0:T(8,128)S(1)}, u32[]{:S(2)}, u32[]{:S(2)}) collective-permute-start(f32[3,56,128]{2,1,0:T(8,128)S(1)} %shard_map.88.refs_0_), channel_id=1, source_target_pairs={{0,5},{1,6},{2,7},{3,0},{4,1},{5,2},{6,3},{7,4},{8,13},{9,14},{10,... | collective-permute-start | bytes 258056 | tf_op jit(solution)/shard_map/ppermute | solution.py:41
  32.9 2.5 %collective-permute-start.7 = (f32[3,56,128]{2,1,0:T(8,128)S(1)}, f32[3,56,128]{2,1,0:T(8,128)S(1)}, u32[]{:S(2)}, u32[]{:S(2)}) collective-permute-start(f32[3,56,128]{2,1,0:T(8,128)S(1)} %shard_map.88.refs_0_), channel_id=1, source_target_pairs={{0,6},{1,7},{2,0},{3,1},{4,2},{5,3},{6,4},{7,5},{8,14},{9,15},{10,... | collective-permute-start | bytes 258056 | tf_op jit(solution)/shard_map/ppermute | solution.py:41
  35.4 0.7 collective-permute-start.8
  36.2 2.2 %collective-permute-done.4.refs_3_ = f32[3,56,128]{2,1,0:T(8,128)S(1)} collective-permute-done((f32[3,56,128]{2,1,0:T(8,128)S(1)}, f32[3,56,128]{2,1,0:T(8,128)S(1)}, u32[]{:S(2)}, u32[]{:S(2)}) %collective-permute-start.4) | collective-permute-done | bytes 86048 | tf_op jit(solution)/shard_map/ppermute | solution.py:41
  38.4 7.1 %collective-permute-done.7.refs_6_ = f32[3,56,128]{2,1,0:T(8,128)S(1)} collective-permute-done((f32[3,56,128]{2,1,0:T(8,128)S(1)}, f32[3,56,128]{2,1,0:T(8,128)S(1)}, u32[]{:S(2)}, u32[]{:S(2)}) %collective-permute-start.7) | collective-permute-done | bytes 86048 | tf_op jit(solution)/shard_map/ppermute | solution.py:41
  46.6 14.8 %all_to_all.25.sums_ref = s16[8,64,128]{2,1,0:T(8,128)(2,1)S(1)} all-to-all(s16[8,64,128]{2,1,0:T(8,128)(2,1)S(1)} %shard_map.89), channel_id=1, replica_groups=mesh['y'=4,'c'=2,'x'=4,'z'=8] {'z'}, dimensions={0} | all-to-all | bytes 262144 | tf_op jit(solution)/shard_map/all_to_all | solution.py:32
  61.4 1.4 %shard_map.90 = (f32[56,128]{1,0:T(8,128)S(1)}, f32[8,64,128]{2,1,0:T(8,128)}) custom-call(s32[3]{0:T(128)S(1)} %pad_add_fusion.where_ref, s16[8,64,128]{2,1,0:T(8,128)(2,1)S(1)} %all_to_all.25.sums_ref), custom_call_target="tpu_custom_call" | custom-call | tf_op jit(solution)/shard_map/pallas_call | solution.py:154
  62.8 3.4 %all-to-all-start.2 = ((f32[8,64,128]{2,1,0:T(8,128)}), f32[8,64,128]{2,1,0:T(8,128)S(1)}, u32[]{:S(2)}, u32[]{:S(2)}) async-start(f32[8,64,128]{2,1,0:T(8,128)} %get-tuple-element.21), calls=%async_computation.2 | async-start | bytes 524288 | tf_op jit(solution)/shard_map/all_to_all | solution.py:32
  66.3 2.0 %collective-permute-start.10 = (f32[56,128]{1,0:T(8,128)S(1)}, f32[56,128]{1,0:T(8,128)S(1)}, u32[]{:S(2)}, u32[]{:S(2)}) collective-permute-start(f32[56,128]{1,0:T(8,128)S(1)} %get-tuple-element.22.refs_0_), channel_id=1, source_target_pairs={{0,128},{64,192},{128,0},{192,64},{1,129},{65,193},{129,1},{193,65... | collective-permute-start | bytes 86024 | tf_op jit(solution)/shard_map/ppermute | solution.py:41
  68.2 0.9 collective-permute-start.11
  69.7 0.9 collective-permute-done.10.refs_2_
  71.0 2.1 %collective-permute-done.9.refs_1_ = f32[56,128]{1,0:T(8,128)S(1)} collective-permute-done((f32[56,128]{1,0:T(8,128)S(1)}, f32[56,128]{1,0:T(8,128)S(1)}, u32[]{:S(2)}, u32[]{:S(2)}) %collective-permute-start.9) | collective-permute-done | bytes 28704 | tf_op jit(solution)/shard_map/ppermute | solution.py:41
  73.1 2.6 %all-to-all-done.2.column_ref = f32[8,64,128]{2,1,0:T(8,128)S(1)} async-done(((f32[8,64,128]{2,1,0:T(8,128)}), f32[8,64,128]{2,1,0:T(8,128)S(1)}, u32[]{:S(2)}, u32[]{:S(2)}) %all-to-all-start.2) | async-done | bytes 262176 | tf_op jit(solution)/shard_map/all_to_all | solution.py:32
  75.6 4.3 %collective-permute-start.12 = (f32[232,128]{1,0:T(8,128)S(1)}, f32[232,128]{1,0:T(8,128)S(1)}, u32[]{:S(2)}, u32[]{:S(2)}) collective-permute-start(f32[232,128]{1,0:T(8,128)S(1)} %shard_map.91.mine_ref), channel_id=1, source_target_pairs={{0,32},{32,0},{1,33},{33,1},{2,34},{34,2},{3,35},{35,3},{4,36},{36... | collective-permute-start | bytes 356360 | tf_op jit(solution)/shard_map/ppermute | solution.py:36
  79.9 1.0 collective-permute-done.12.theirs_ref
  80.9 10.8 %all_to_all.26.totals_ref = f32[16,8,128]{2,1,0:T(8,128)S(1)} all-to-all(f32[16,8,128]{2,1,0:T(8,128)S(1)} %shard_map.92), channel_id=1, replica_groups=mesh['y'=4,'c'=2,'x'=4,'z'=8] {'x','y'}, dimensions={0} | all-to-all | bytes 131072 | tf_op jit(solution)/shard_map/all_to_all | solution.py:32
  91.7 0.9 shard_map.94
  92.6 26.2 %all_to_all.27.mine_ref = bf16[16,448,128]{2,1,0:T(8,128)(2,1)S(1)} all-to-all(bf16[16,448,128]{2,1,0:T(8,128)(2,1)S(1)} %shard_map.94), channel_id=1, replica_groups=mesh['y'=4,'c'=2,'x'=4,'z'=8] {'x','y'}, dimensions={0} | all-to-all | bytes 3670016 | tf_op jit(solution)/shard_map/all_to_all | solution.py:32
  118.9 3.5 %collective-permute-start.14 = (bf16[8,448,128]{2,1,0:T(8,128)(2,1)S(1)}, bf16[8,448,128]{2,1,0:T(8,128)(2,1)S(1)}, u32[]{:S(2)}, u32[]{:S(2)}) collective-permute-start(bf16[8,448,128]{2,1,0:T(8,128)(2,1)S(1)} %get-tuple-element.34), channel_id=1, source_target_pairs={{0,32},{32,0},{1,33},{33,1},{2,34},{34,2},{3,35},{35,3},{4,36},{36... | collective-permute-start | bytes 2752520 | tf_op jit(solution)/shard_map/ppermute | solution.py:36
  122.4 1.6 %shard_map.93 = (f32[108,512]{1,0:T(8,128)}, f32[108,512]{1,0:T(8,128)}, f32[108,512]{1,0:T(8,128)}) custom-call(s32[3]{0:T(128)S(1)} %pad_add_fusion.where_ref, f32[2]{0:T(128)S(1)} %pad_maximum_fusion.fixes_ref, f32[16,8,128]{2,1,0:T(8,128)S(1)} %all_to_all.26.totals_ref, f32[232,128]{1,0:T(8,128)S(1)} %shard_map.91.mine_ref, ...), custom_call_target="tpu_custom_call" | custom-call | tf_op jit(solution)/shard_map/pallas_call | solution.py:277
  124.4 1.6 %shard_map.95.refs_0_ = bf16[3456,512]{1,0:T(8,128)(2,1)} custom-call(s32[1]{0:T(128)} %bitcast.1.c_ref, bf16[16,448,128]{2,1,0:T(8,128)(2,1)S(1)} %all_to_all.27.mine_ref, bf16[8,448,128]{2,1,0:T(8,128)(2,1)S(1)} %collective-permute-done.14.theirs_ref), custom_call_target="tpu_custom_call" | custom-call | tf_op jit(solution)/shard_map/pallas_call | solution.py:301
  126.1 1.6 %shard_map.96 = bf16[3456,512]{1,0:T(8,128)(2,1)} custom-call(s32[1]{0:T(128)} %bitcast.1.c_ref, bf16[16,448,128]{2,1,0:T(8,128)(2,1)S(1)} %all_to_all.27.mine_ref, bf16[8,448,128]{2,1,0:T(8,128)(2,1)S(1)} %collective-permute-done.13.theirs_ref, bf16[3456,512]{1,0:T(8,128)(2,1)} %shard_map.95.refs_0_), custom_call_target="tpu_custom_call", output_to_operand_aliasing={{}: (3, {})} | custom-call | tf_op jit(solution)/shard_map/pallas_call | solution.py:301
  (29 shorter events, 4.2 us)
Async XLA Ops:
  2.4 5.4 %collective-permute-start.1 = (s16[2,4,456,128]{3,2,1,0:T(8,128)(2,1)S(1)}, s16[2,4,456,128]{3,2,1,0:T(8,128)(2,1)S(1)}, u32[]{:S(2)}, u32[]{:S(2)}) collective-permute-start(s16[2,4,456,128]{3,2,1,0:T(8,128)(2,1)S(1)} %shard_map.85), channel_id=1, source_target_pairs={{0,32},{32,0},{1,33},{33,1},{2,34},{34,2},{3,35},{35,3},{4,36},{36... | collective-permute-start | bytes 2801672 | tf_op jit(solution)/shard_map/ppermute | solution.py:36
  5.7 3.5 %copy-start = (f32[1,1,3456,512]{3,2,1,0:T(8,128)S(1)}, f32[1,1,3456,512]{3,2,1,0:T(8,128)}, u32[]{:S(2)}) copy-start(f32[1,1,3456,512]{3,2,1,0:T(8,128)} %param.5) | copy-start | bytes 21233668
  7.6 3.4 %collective-permute-start = (s16[2,4,456,128]{3,2,1,0:T(8,128)(2,1)S(1)}, s16[2,4,456,128]{3,2,1,0:T(8,128)(2,1)S(1)}, u32[]{:S(2)}, u32[]{:S(2)}) collective-permute-start(s16[2,4,456,128]{3,2,1,0:T(8,128)(2,1)S(1)} %shard_map.84), channel_id=1, source_target_pairs={{0,32},{32,0},{1,33},{33,1},{2,34},{34,2},{3,35},{35,3},{4,36},{36... | collective-permute-start | bytes 2801672 | tf_op jit(solution)/shard_map/ppermute | solution.py:36
  12.9 5.3 %copy-start.1 = (f32[108,512]{1,0:T(8,128)S(1)}, f32[108,512]{1,0:T(8,128)}, u32[]{:S(2)}) copy-start(f32[108,512]{1,0:T(8,128)} %refs_0_.3) | copy-start | bytes 663556
  12.9 5.3 %copy-start.2 = (f32[108,512]{1,0:T(8,128)S(1)}, f32[108,512]{1,0:T(8,128)}, u32[]{:S(2)}) copy-start(f32[108,512]{1,0:T(8,128)} %refs_1_.3) | copy-start | bytes 663556
  12.9 5.3 %copy-start.3 = (f32[108,512]{1,0:T(8,128)S(1)}, f32[108,512]{1,0:T(8,128)}, u32[]{:S(2)}) copy-start(f32[108,512]{1,0:T(8,128)} %refs_2_.3) | copy-start | bytes 663556
  12.9 33.1 %all-to-all-start = ((s16[16,456,128]{2,1,0:T(8,128)(2,1)}), s16[16,456,128]{2,1,0:T(8,128)(2,1)S(1)}, u32[]{:S(2)}, u32[]{:S(2)}) async-start(s16[16,456,128]{2,1,0:T(8,128)(2,1)} %bitcast.4), calls=%async_computation | async-start | bytes 3735552 | tf_op jit(solution)/shard_map/all_to_all | solution.py:32
  18.8 14.1 %collective-permute-start.2 = (f32[3,56,128]{2,1,0:T(8,128)S(1)}, f32[3,56,128]{2,1,0:T(8,128)S(1)}, u32[]{:S(2)}, u32[]{:S(2)}) collective-permute-start(f32[3,56,128]{2,1,0:T(8,128)S(1)} %shard_map.88.refs_0_), channel_id=1, source_target_pairs={{0,1},{1,2},{2,3},{3,4},{4,5},{5,6},{6,7},{7,0},{8,9},{9,10},{10,1... | collective-permute-start | bytes 258056 | tf_op jit(solution)/shard_map/ppermute | solution.py:41
  20.5 14.9 %collective-permute-start.3 = (f32[3,56,128]{2,1,0:T(8,128)S(1)}, f32[3,56,128]{2,1,0:T(8,128)S(1)}, u32[]{:S(2)}, u32[]{:S(2)}) collective-permute-start(f32[3,56,128]{2,1,0:T(8,128)S(1)} %shard_map.88.refs_0_), channel_id=1, source_target_pairs={{0,2},{1,3},{2,4},{3,5},{4,6},{5,7},{6,0},{7,1},{8,10},{9,11},{10,... | collective-permute-start | bytes 258056 | tf_op jit(solution)/shard_map/ppermute | solution.py:41
  23.5 14.9 %collective-permute-start.4 = (f32[3,56,128]{2,1,0:T(8,128)S(1)}, f32[3,56,128]{2,1,0:T(8,128)S(1)}, u32[]{:S(2)}, u32[]{:S(2)}) collective-permute-start(f32[3,56,128]{2,1,0:T(8,128)S(1)} %shard_map.88.refs_0_), channel_id=1, source_target_pairs={{0,3},{1,4},{2,5},{3,6},{4,7},{5,0},{6,1},{7,2},{8,11},{9,12},{10,... | collective-permute-start | bytes 258056 | tf_op jit(solution)/shard_map/ppermute | solution.py:41
  27.2 11.2 %collective-permute-start.5 = (f32[3,56,128]{2,1,0:T(8,128)S(1)}, f32[3,56,128]{2,1,0:T(8,128)S(1)}, u32[]{:S(2)}, u32[]{:S(2)}) collective-permute-start(f32[3,56,128]{2,1,0:T(8,128)S(1)} %shard_map.88.refs_0_), channel_id=1, source_target_pairs={{0,4},{1,5},{2,6},{3,7},{4,0},{5,1},{6,2},{7,3},{8,12},{9,13},{10,... | collective-permute-start | bytes 258056 | tf_op jit(solution)/shard_map/ppermute | solution.py:41
  27.7 10.7 %collective-permute-start.6 = (f32[3,56,128]{2,1,0:T(8,128)S(1)}, f32[3,56,128]{2,1,0:T(8,128)S(1)}, u32[]{:S(2)}, u32[]{:S(2)}) collective-permute-start(f32[3,56,128]{2,1,0:T(8,128)S(1)} %shard_map.88.refs_0_), channel_id=1, source_target_pairs={{0,5},{1,6},{2,7},{3,0},{4,1},{5,2},{6,3},{7,4},{8,13},{9,14},{10,... | collective-permute-start | bytes 258056 | tf_op jit(solution)/shard_map/ppermute | solution.py:41
  32.9 12.6 %collective-permute-start.7 = (f32[3,56,128]{2,1,0:T(8,128)S(1)}, f32[3,56,128]{2,1,0:T(8,128)S(1)}, u32[]{:S(2)}, u32[]{:S(2)}) collective-permute-start(f32[3,56,128]{2,1,0:T(8,128)S(1)} %shard_map.88.refs_0_), channel_id=1, source_target_pairs={{0,6},{1,7},{2,0},{3,1},{4,2},{5,3},{6,4},{7,5},{8,14},{9,15},{10,... | collective-permute-start | bytes 258056 | tf_op jit(solution)/shard_map/ppermute | solution.py:41
  35.4 10.6 %collective-permute-start.8 = (f32[3,56,128]{2,1,0:T(8,128)S(1)}, f32[3,56,128]{2,1,0:T(8,128)S(1)}, u32[]{:S(2)}, u32[]{:S(2)}) collective-permute-start(f32[3,56,128]{2,1,0:T(8,128)S(1)} %shard_map.88.refs_0_), channel_id=1, source_target_pairs={{0,7},{1,0},{2,1},{3,2},{4,3},{5,4},{6,5},{7,6},{8,15},{9,8},{10,9... | collective-permute-start | bytes 258056 | tf_op jit(solution)/shard_map/ppermute | solution.py:41
  62.8 12.8 %all-to-all-start.2 = ((f32[8,64,128]{2,1,0:T(8,128)}), f32[8,64,128]{2,1,0:T(8,128)S(1)}, u32[]{:S(2)}, u32[]{:S(2)}) async-start(f32[8,64,128]{2,1,0:T(8,128)} %get-tuple-element.21), calls=%async_computation.2 | async-start | bytes 524288 | tf_op jit(solution)/shard_map/all_to_all | solution.py:32
  66.3 4.3 %collective-permute-start.10 = (f32[56,128]{1,0:T(8,128)S(1)}, f32[56,128]{1,0:T(8,128)S(1)}, u32[]{:S(2)}, u32[]{:S(2)}) collective-permute-start(f32[56,128]{1,0:T(8,128)S(1)} %get-tuple-element.22.refs_0_), channel_id=1, source_target_pairs={{0,128},{64,192},{128,0},{192,64},{1,129},{65,193},{129,1},{193,65... | collective-permute-start | bytes 86024 | tf_op jit(solution)/shard_map/ppermute | solution.py:41
  68.2 2.7 %collective-permute-start.11 = (f32[56,128]{1,0:T(8,128)S(1)}, f32[56,128]{1,0:T(8,128)S(1)}, u32[]{:S(2)}, u32[]{:S(2)}) collective-permute-start(f32[56,128]{1,0:T(8,128)S(1)} %get-tuple-element.22.refs_0_), channel_id=1, source_target_pairs={{0,192},{64,0},{128,64},{192,128},{1,193},{65,1},{129,65},{193,129... | collective-permute-start | bytes 86024 | tf_op jit(solution)/shard_map/ppermute | solution.py:41
  69.1 3.9 %collective-permute-start.9 = (f32[56,128]{1,0:T(8,128)S(1)}, f32[56,128]{1,0:T(8,128)S(1)}, u32[]{:S(2)}, u32[]{:S(2)}) collective-permute-start(f32[56,128]{1,0:T(8,128)S(1)} %get-tuple-element.22.refs_0_), channel_id=1, source_target_pairs={{0,64},{64,128},{128,192},{192,0},{1,65},{65,129},{129,193},{193,1... | collective-permute-start | bytes 86024 | tf_op jit(solution)/shard_map/ppermute | solution.py:41
  75.6 5.2 %collective-permute-start.12 = (f32[232,128]{1,0:T(8,128)S(1)}, f32[232,128]{1,0:T(8,128)S(1)}, u32[]{:S(2)}, u32[]{:S(2)}) collective-permute-start(f32[232,128]{1,0:T(8,128)S(1)} %shard_map.91.mine_ref), channel_id=1, source_target_pairs={{0,32},{32,0},{1,33},{33,1},{2,34},{34,2},{3,35},{35,3},{4,36},{36... | collective-permute-start | bytes 356360 | tf_op jit(solution)/shard_map/ppermute | solution.py:36
  118.9 5.6 %collective-permute-start.14 = (bf16[8,448,128]{2,1,0:T(8,128)(2,1)S(1)}, bf16[8,448,128]{2,1,0:T(8,128)(2,1)S(1)}, u32[]{:S(2)}, u32[]{:S(2)}) collective-permute-start(bf16[8,448,128]{2,1,0:T(8,128)(2,1)S(1)} %get-tuple-element.34), channel_id=1, source_target_pairs={{0,32},{32,0},{1,33},{33,1},{2,34},{34,2},{3,35},{35,3},{4,36},{36... | collective-permute-start | bytes 2752520 | tf_op jit(solution)/shard_map/ppermute | solution.py:36
  122.3 3.7 %collective-permute-start.13 = (bf16[8,448,128]{2,1,0:T(8,128)(2,1)S(1)}, bf16[8,448,128]{2,1,0:T(8,128)(2,1)S(1)}, u32[]{:S(2)}, u32[]{:S(2)}) collective-permute-start(bf16[8,448,128]{2,1,0:T(8,128)(2,1)S(1)} %get-tuple-element.35), channel_id=1, source_target_pairs={{0,32},{32,0},{1,33},{33,1},{2,34},{34,2},{3,35},{35,3},{4,36},{36... | collective-permute-start | bytes 2752520 | tf_op jit(solution)/shard_map/ppermute | solution.py:36

commit v6 on v5

--- a/solution.py
+++ b/solution.py
@@ -42,13 +42,13 @@
 
 
 def scale_of(level):
-    return jnp.exp2(0.25 * level.astype(jnp.int32).astype(jnp.float32)) * (1.0 / 32767.0)
+    return jnp.exp2(0.0625 * level.astype(jnp.int32).astype(jnp.float32)) * (1.0 / 32767.0)
 
 
 def coded_block(value):
     peak = jnp.max(jnp.abs(value), axis=0, keepdims=True)
-    level = jnp.maximum(jnp.ceil(4.0 * jnp.log2(peak) + 0.02), -400.0)
-    scaled = jnp.round(value * (32767.0 * jnp.exp2(-0.25 * level)))
+    level = jnp.maximum(jnp.ceil(16.0 * jnp.log2(peak) + 0.02), -1600.0)
+    scaled = jnp.round(value * (32767.0 * jnp.exp2(-0.0625 * level)))
     return scaled.astype(jnp.int32).astype(jnp.int16), level
 
 

time: 128 us -> 128 us (level)
  no operation moved by 1% of the time
where the time goes in v6:
time: 128 us
  blocking collectives  51.8 us (40%)
  starting transfers between devices  39.9 us (31%)
  waiting for transfers between devices  17.2 us (13%)
  Pallas kernels  15.7 us (12%)
  local copies, waits for them, and re-layouts  1.55 us (1%)
  between operations  1.47 us (1%)
    all_to_all x3, blocking collectives, exchanged(): return lax.all_to_all(value, axes, split_axis=0, concat_axis=0, tiled=True)  51.8 us
    ppermute x10, starting transfers between devices, rotated(): lax.ppermute(value, axis, [(i, (i + k) % n) for i in range(n)])  20 us
    ppermute x10, waiting for transfers between devices, rotated(): lax.ppermute(value, axis, [(i, (i + k) % n) for i in range(n)])  13.2 us
    ppermute x5, starting transfers between devices, swapped(): return lax.ppermute(value, axis, [(0, 1), (1, 0)])  11.2 us
    all_to_all x2, starting transfers between devices, exchanged(): return lax.all_to_all(value, axes, split_axis=0, concat_axis=0, tiled=True)  8.59 us
    pallas_call x2, Pallas kernels, code_half(): pl.pallas_call(half_kernel, compiler_params=LIMIT, grid_spec=pltpu.Prefet...  3.7 us
    pallas_call x2, Pallas kernels, code_sums(): pl.pallas_call(kernel, compiler_params=LIMIT, grid_spec=pltpu.PrefetchSca...  3.65 us
    pallas_call x2, Pallas kernels, assemble(): pl.pallas_call(kernel, compiler_params=LIMIT, grid_spec=pltpu.PrefetchSca...  3.25 us
  transfers between devices with their start and end apart: 17, of which 11 were waited for; matrix products, arithmetic and copies ran while one was open for 0% of the time, Pallas kernels for 6%

profile of v6, /device:TPU:1, one launch (start us, length us, event | category | flops | bytes accessed | tf_op | source)
XLA Modules:
  0.0 127.7 jit_solution(13127519539465747245)
XLA Ops:
  0.6 1.8 %shard_map.85 = s16[2,4,456,128]{3,2,1,0:T(8,128)(2,1)S(1)} custom-call(s32[1]{0:T(128)} %bitcast.1.c_ref, f32[3456,512]{1,0:T(8,128)} %bitcast.5), custom_call_target="tpu_custom_call" | custom-call | tf_op jit(solution)/shard_map/pallas_call | solution.py:76
  2.4 3.3 %collective-permute-start.1 = (s16[2,4,456,128]{3,2,1,0:T(8,128)(2,1)S(1)}, s16[2,4,456,128]{3,2,1,0:T(8,128)(2,1)S(1)}, u32[]{:S(2)}, u32[]{:S(2)}) collective-permute-start(s16[2,4,456,128]{3,2,1,0:T(8,128)(2,1)S(1)} %shard_map.85), channel_id=1, source_target_pairs={{0,32},{32,0},{1,33},{33,1},{2,34},{34,2},{3,35},{35,3},{4,36},{36... | collective-permute-start | bytes 2801672 | tf_op jit(solution)/shard_map/ppermute | solution.py:36
  5.7 1.9 %shard_map.84 = s16[2,4,456,128]{3,2,1,0:T(8,128)(2,1)S(1)} custom-call(s32[1]{0:T(128)} %bitcast.1.c_ref, f32[3456,512]{1,0:T(8,128)} %bitcast.6), custom_call_target="tpu_custom_call" | custom-call | tf_op jit(solution)/shard_map/pallas_call | solution.py:76
  7.8 1.4 %copy-done = f32[1,1,3456,512]{3,2,1,0:T(8,128)S(1)} copy-done((f32[1,1,3456,512]{3,2,1,0:T(8,128)S(1)}, f32[1,1,3456,512]{3,2,1,0:T(8,128)}, u32[]{:S(2)}) %copy-start) | copy-done | bytes 7077912
  9.3 1.8 %shard_map.86.refs_0_ = s16[4,4,456,128]{3,2,1,0:T(8,128)(2,1)} custom-call(s32[1]{0:T(128)} %bitcast.1.c_ref, f32[3456,512]{1,0:T(8,128)S(1)} %bitcast.7, s16[2,4,456,128]{3,2,1,0:T(8,128)(2,1)S(1)} %collective-permute-done.1.theirs_ref), custom_call_target="tpu_custom_call" | custom-call | tf_op jit(solution)/shard_map/pallas_call | solution.py:102
  11.1 1.8 %shard_map.87 = s16[4,4,456,128]{3,2,1,0:T(8,128)(2,1)} custom-call(s32[1]{0:T(128)} %bitcast.1.c_ref, f32[3456,512]{1,0:T(8,128)S(1)} %bitcast.8, s16[2,4,456,128]{3,2,1,0:T(8,128)(2,1)S(1)} %collective-permute-done.theirs_ref, s16[4,4,456,128]{3,2,1,0:T(8,128)(2,1)} %shard_map.86.refs_0_), custom_call_target="tpu_custom_call", output_to_operand_aliasing={{}: (3, {})} | custom-call | tf_op jit(solution)/shard_map/pallas_call | solution.py:102
  12.9 5.2 %all-to-all-start = ((s16[16,456,128]{2,1,0:T(8,128)(2,1)}), s16[16,456,128]{2,1,0:T(8,128)(2,1)S(1)}, u32[]{:S(2)}, u32[]{:S(2)}) async-start(s16[16,456,128]{2,1,0:T(8,128)(2,1)} %bitcast.4), calls=%async_computation | async-start | bytes 3735552 | tf_op jit(solution)/shard_map/all_to_all | solution.py:32
  18.8 1.7 %collective-permute-start.2 = (f32[3,56,128]{2,1,0:T(8,128)S(1)}, f32[3,56,128]{2,1,0:T(8,128)S(1)}, u32[]{:S(2)}, u32[]{:S(2)}) collective-permute-start(f32[3,56,128]{2,1,0:T(8,128)S(1)} %shard_map.88.refs_0_), channel_id=1, source_target_pairs={{0,1},{1,2},{2,3},{3,4},{4,5},{5,6},{6,7},{7,0},{8,9},{9,10},{10,1... | collective-permute-start | bytes 258056 | tf_op jit(solution)/shard_map/ppermute | solution.py:41
  20.5 3.0 %collective-permute-start.3 = (f32[3,56,128]{2,1,0:T(8,128)S(1)}, f32[3,56,128]{2,1,0:T(8,128)S(1)}, u32[]{:S(2)}, u32[]{:S(2)}) collective-permute-start(f32[3,56,128]{2,1,0:T(8,128)S(1)} %shard_map.88.refs_0_), channel_id=1, source_target_pairs={{0,2},{1,3},{2,4},{3,5},{4,6},{5,7},{6,0},{7,1},{8,10},{9,11},{10,... | collective-permute-start | bytes 258056 | tf_op jit(solution)/shard_map/ppermute | solution.py:41
  23.5 3.8 %collective-permute-start.4 = (f32[3,56,128]{2,1,0:T(8,128)S(1)}, f32[3,56,128]{2,1,0:T(8,128)S(1)}, u32[]{:S(2)}, u32[]{:S(2)}) collective-permute-start(f32[3,56,128]{2,1,0:T(8,128)S(1)} %shard_map.88.refs_0_), channel_id=1, source_target_pairs={{0,3},{1,4},{2,5},{3,6},{4,7},{5,0},{6,1},{7,2},{8,11},{9,12},{10,... | collective-permute-start | bytes 258056 | tf_op jit(solution)/shard_map/ppermute | solution.py:41
  27.7 4.5 %collective-permute-start.6 = (f32[3,56,128]{2,1,0:T(8,128)S(1)}, f32[3,56,128]{2,1,0:T(8,128)S(1)}, u32[]{:S(2)}, u32[]{:S(2)}) collective-permute-start(f32[3,56,128]{2,1,0:T(8,128)S(1)} %shard_map.88.refs_0_), channel_id=1, source_target_pairs={{0,5},{1,6},{2,7},{3,0},{4,1},{5,2},{6,3},{7,4},{8,13},{9,14},{10,... | collective-permute-start | bytes 258056 | tf_op jit(solution)/shard_map/ppermute | solution.py:41
  32.9 2.5 %collective-permute-start.7 = (f32[3,56,128]{2,1,0:T(8,128)S(1)}, f32[3,56,128]{2,1,0:T(8,128)S(1)}, u32[]{:S(2)}, u32[]{:S(2)}) collective-permute-start(f32[3,56,128]{2,1,0:T(8,128)S(1)} %shard_map.88.refs_0_), channel_id=1, source_target_pairs={{0,6},{1,7},{2,0},{3,1},{4,2},{5,3},{6,4},{7,5},{8,14},{9,15},{10,... | collective-permute-start | bytes 258056 | tf_op jit(solution)/shard_map/ppermute | solution.py:41
  35.4 0.7 collective-permute-start.8
  36.2 2.2 %collective-permute-done.4.refs_3_ = f32[3,56,128]{2,1,0:T(8,128)S(1)} collective-permute-done((f32[3,56,128]{2,1,0:T(8,128)S(1)}, f32[3,56,128]{2,1,0:T(8,128)S(1)}, u32[]{:S(2)}, u32[]{:S(2)}) %collective-permute-start.4) | collective-permute-done | bytes 86048 | tf_op jit(solution)/shard_map/ppermute | solution.py:41
  38.4 7.1 %collective-permute-done.7.refs_6_ = f32[3,56,128]{2,1,0:T(8,128)S(1)} collective-permute-done((f32[3,56,128]{2,1,0:T(8,128)S(1)}, f32[3,56,128]{2,1,0:T(8,128)S(1)}, u32[]{:S(2)}, u32[]{:S(2)}) %collective-permute-start.7) | collective-permute-done | bytes 86048 | tf_op jit(solution)/shard_map/ppermute | solution.py:41
  46.6 14.8 %all_to_all.25.sums_ref = s16[8,64,128]{2,1,0:T(8,128)(2,1)S(1)} all-to-all(s16[8,64,128]{2,1,0:T(8,128)(2,1)S(1)} %shard_map.89), channel_id=1, replica_groups=mesh['y'=4,'c'=2,'x'=4,'z'=8] {'z'}, dimensions={0} | all-to-all | bytes 262144 | tf_op jit(solution)/shard_map/all_to_all | solution.py:32
  61.4 1.4 %shard_map.90 = (f32[56,128]{1,0:T(8,128)S(1)}, f32[8,64,128]{2,1,0:T(8,128)}) custom-call(s32[3]{0:T(128)S(1)} %pad_add_fusion.where_ref, s16[8,64,128]{2,1,0:T(8,128)(2,1)S(1)} %all_to_all.25.sums_ref), custom_call_target="tpu_custom_call" | custom-call | tf_op jit(solution)/shard_map/pallas_call | solution.py:154
  62.8 3.4 %all-to-all-start.2 = ((f32[8,64,128]{2,1,0:T(8,128)}), f32[8,64,128]{2,1,0:T(8,128)S(1)}, u32[]{:S(2)}, u32[]{:S(2)}) async-start(f32[8,64,128]{2,1,0:T(8,128)} %get-tuple-element.21), calls=%async_computation.2 | async-start | bytes 524288 | tf_op jit(solution)/shard_map/all_to_all | solution.py:32
  66.3 2.0 %collective-permute-start.10 = (f32[56,128]{1,0:T(8,128)S(1)}, f32[56,128]{1,0:T(8,128)S(1)}, u32[]{:S(2)}, u32[]{:S(2)}) collective-permute-start(f32[56,128]{1,0:T(8,128)S(1)} %get-tuple-element.22.refs_0_), channel_id=1, source_target_pairs={{0,128},{64,192},{128,0},{192,64},{1,129},{65,193},{129,1},{193,65... | collective-permute-start | bytes 86024 | tf_op jit(solution)/shard_map/ppermute | solution.py:41
  68.2 0.9 collective-permute-start.11
  69.7 0.9 collective-permute-done.10.refs_2_
  71.0 2.1 %collective-permute-done.9.refs_1_ = f32[56,128]{1,0:T(8,128)S(1)} collective-permute-done((f32[56,128]{1,0:T(8,128)S(1)}, f32[56,128]{1,0:T(8,128)S(1)}, u32[]{:S(2)}, u32[]{:S(2)}) %collective-permute-start.9) | collective-permute-done | bytes 28704 | tf_op jit(solution)/shard_map/ppermute | solution.py:41
  73.1 2.6 %all-to-all-done.2.column_ref = f32[8,64,128]{2,1,0:T(8,128)S(1)} async-done(((f32[8,64,128]{2,1,0:T(8,128)}), f32[8,64,128]{2,1,0:T(8,128)S(1)}, u32[]{:S(2)}, u32[]{:S(2)}) %all-to-all-start.2) | async-done | bytes 262176 | tf_op jit(solution)/shard_map/all_to_all | solution.py:32
  75.6 4.3 %collective-permute-start.12 = (f32[232,128]{1,0:T(8,128)S(1)}, f32[232,128]{1,0:T(8,128)S(1)}, u32[]{:S(2)}, u32[]{:S(2)}) collective-permute-start(f32[232,128]{1,0:T(8,128)S(1)} %shard_map.91.mine_ref), channel_id=1, source_target_pairs={{0,32},{32,0},{1,33},{33,1},{2,34},{34,2},{3,35},{35,3},{4,36},{36... | collective-permute-start | bytes 356360 | tf_op jit(solution)/shard_map/ppermute | solution.py:36
  79.9 1.0 collective-permute-done.12.theirs_ref
  80.9 10.8 %all_to_all.26.totals_ref = f32[16,8,128]{2,1,0:T(8,128)S(1)} all-to-all(f32[16,8,128]{2,1,0:T(8,128)S(1)} %shard_map.92), channel_id=1, replica_groups=mesh['y'=4,'c'=2,'x'=4,'z'=8] {'x','y'}, dimensions={0} | all-to-all | bytes 131072 | tf_op jit(solution)/shard_map/all_to_all | solution.py:32
  91.7 0.9 shard_map.94
  92.6 26.2 %all_to_all.27.mine_ref = bf16[16,448,128]{2,1,0:T(8,128)(2,1)S(1)} all-to-all(bf16[16,448,128]{2,1,0:T(8,128)(2,1)S(1)} %shard_map.94), channel_id=1, replica_groups=mesh['y'=4,'c'=2,'x'=4,'z'=8] {'x','y'}, dimensions={0} | all-to-all | bytes 3670016 | tf_op jit(solution)/shard_map/all_to_all | solution.py:32
  118.9 3.5 %collective-permute-start.14 = (bf16[8,448,128]{2,1,0:T(8,128)(2,1)S(1)}, bf16[8,448,128]{2,1,0:T(8,128)(2,1)S(1)}, u32[]{:S(2)}, u32[]{:S(2)}) collective-permute-start(bf16[8,448,128]{2,1,0:T(8,128)(2,1)S(1)} %get-tuple-element.34), channel_id=1, source_target_pairs={{0,32},{32,0},{1,33},{33,1},{2,34},{34,2},{3,35},{35,3},{4,36},{36... | collective-permute-start | bytes 2752520 | tf_op jit(solution)/shard_map/ppermute | solution.py:36
  122.4 1.6 %shard_map.93 = (f32[108,512]{1,0:T(8,128)}, f32[108,512]{1,0:T(8,128)}, f32[108,512]{1,0:T(8,128)}) custom-call(s32[3]{0:T(128)S(1)} %pad_add_fusion.where_ref, f32[2]{0:T(128)S(1)} %pad_maximum_fusion.fixes_ref, f32[16,8,128]{2,1,0:T(8,128)S(1)} %all_to_all.26.totals_ref, f32[232,128]{1,0:T(8,128)S(1)} %shard_map.91.mine_ref, ...), custom_call_target="tpu_custom_call" | custom-call | tf_op jit(solution)/shard_map/pallas_call | solution.py:277
  124.4 1.6 %shard_map.95.refs_0_ = bf16[3456,512]{1,0:T(8,128)(2,1)} custom-call(s32[1]{0:T(128)} %bitcast.1.c_ref, bf16[16,448,128]{2,1,0:T(8,128)(2,1)S(1)} %all_to_all.27.mine_ref, bf16[8,448,128]{2,1,0:T(8,128)(2,1)S(1)} %collective-permute-done.14.theirs_ref), custom_call_target="tpu_custom_call" | custom-call | tf_op jit(solution)/shard_map/pallas_call | solution.py:301
  126.1 1.6 %shard_map.96 = bf16[3456,512]{1,0:T(8,128)(2,1)} custom-call(s32[1]{0:T(128)} %bitcast.1.c_ref, bf16[16,448,128]{2,1,0:T(8,128)(2,1)S(1)} %all_to_all.27.mine_ref, bf16[8,448,128]{2,1,0:T(8,128)(2,1)S(1)} %collective-permute-done.13.theirs_ref, bf16[3456,512]{1,0:T(8,128)(2,1)} %shard_map.95.refs_0_), custom_call_target="tpu_custom_call", output_to_operand_aliasing={{}: (3, {})} | custom-call | tf_op jit(solution)/shard_map/pallas_call | solution.py:301
  (29 shorter events, 4.2 us)
Async XLA Ops:
  2.4 5.4 %collective-permute-start.1 = (s16[2,4,456,128]{3,2,1,0:T(8,128)(2,1)S(1)}, s16[2,4,456,128]{3,2,1,0:T(8,128)(2,1)S(1)}, u32[]{:S(2)}, u32[]{:S(2)}) collective-permute-start(s16[2,4,456,128]{3,2,1,0:T(8,128)(2,1)S(1)} %shard_map.85), channel_id=1, source_target_pairs={{0,32},{32,0},{1,33},{33,1},{2,34},{34,2},{3,35},{35,3},{4,36},{36... | collective-permute-start | bytes 2801672 | tf_op jit(solution)/shard_map/ppermute | solution.py:36
  5.7 3.5 %copy-start = (f32[1,1,3456,512]{3,2,1,0:T(8,128)S(1)}, f32[1,1,3456,512]{3,2,1,0:T(8,128)}, u32[]{:S(2)}) copy-start(f32[1,1,3456,512]{3,2,1,0:T(8,128)} %param.5) | copy-start | bytes 21233668
  7.6 3.4 %collective-permute-start = (s16[2,4,456,128]{3,2,1,0:T(8,128)(2,1)S(1)}, s16[2,4,456,128]{3,2,1,0:T(8,128)(2,1)S(1)}, u32[]{:S(2)}, u32[]{:S(2)}) collective-permute-start(s16[2,4,456,128]{3,2,1,0:T(8,128)(2,1)S(1)} %shard_map.84), channel_id=1, source_target_pairs={{0,32},{32,0},{1,33},{33,1},{2,34},{34,2},{3,35},{35,3},{4,36},{36... | collective-permute-start | bytes 2801672 | tf_op jit(solution)/shard_map/ppermute | solution.py:36
  12.9 5.3 %copy-start.1 = (f32[108,512]{1,0:T(8,128)S(1)}, f32[108,512]{1,0:T(8,128)}, u32[]{:S(2)}) copy-start(f32[108,512]{1,0:T(8,128)} %refs_0_.3) | copy-start | bytes 663556
  12.9 5.3 %copy-start.2 = (f32[108,512]{1,0:T(8,128)S(1)}, f32[108,512]{1,0:T(8,128)}, u32[]{:S(2)}) copy-start(f32[108,512]{1,0:T(8,128)} %refs_1_.3) | copy-start | bytes 663556
  12.9 5.3 %copy-start.3 = (f32[108,512]{1,0:T(8,128)S(1)}, f32[108,512]{1,0:T(8,128)}, u32[]{:S(2)}) copy-start(f32[108,512]{1,0:T(8,128)} %refs_2_.3) | copy-start | bytes 663556
  12.9 33.1 %all-to-all-start = ((s16[16,456,128]{2,1,0:T(8,128)(2,1)}), s16[16,456,128]{2,1,0:T(8,128)(2,1)S(1)}, u32[]{:S(2)}, u32[]{:S(2)}) async-start(s16[16,456,128]{2,1,0:T(8,128)(2,1)} %bitcast.4), calls=%async_computation | async-start | bytes 3735552 | tf_op jit(solution)/shard_map/all_to_all | solution.py:32
  18.8 14.1 %collective-permute-start.2 = (f32[3,56,128]{2,1,0:T(8,128)S(1)}, f32[3,56,128]{2,1,0:T(8,128)S(1)}, u32[]{:S(2)}, u32[]{:S(2)}) collective-permute-start(f32[3,56,128]{2,1,0:T(8,128)S(1)} %shard_map.88.refs_0_), channel_id=1, source_target_pairs={{0,1},{1,2},{2,3},{3,4},{4,5},{5,6},{6,7},{7,0},{8,9},{9,10},{10,1... | collective-permute-start | bytes 258056 | tf_op jit(solution)/shard_map/ppermute | solution.py:41
  20.5 14.9 %collective-permute-start.3 = (f32[3,56,128]{2,1,0:T(8,128)S(1)}, f32[3,56,128]{2,1,0:T(8,128)S(1)}, u32[]{:S(2)}, u32[]{:S(2)}) collective-permute-start(f32[3,56,128]{2,1,0:T(8,128)S(1)} %shard_map.88.refs_0_), channel_id=1, source_target_pairs={{0,2},{1,3},{2,4},{3,5},{4,6},{5,7},{6,0},{7,1},{8,10},{9,11},{10,... | collective-permute-start | bytes 258056 | tf_op jit(solution)/shard_map/ppermute | solution.py:41
  23.5 14.9 %collective-permute-start.4 = (f32[3,56,128]{2,1,0:T(8,128)S(1)}, f32[3,56,128]{2,1,0:T(8,128)S(1)}, u32[]{:S(2)}, u32[]{:S(2)}) collective-permute-start(f32[3,56,128]{2,1,0:T(8,128)S(1)} %shard_map.88.refs_0_), channel_id=1, source_target_pairs={{0,3},{1,4},{2,5},{3,6},{4,7},{5,0},{6,1},{7,2},{8,11},{9,12},{10,... | collective-permute-start | bytes 258056 | tf_op jit(solution)/shard_map/ppermute | solution.py:41
  27.2 11.2 %collective-permute-start.5 = (f32[3,56,128]{2,1,0:T(8,128)S(1)}, f32[3,56,128]{2,1,0:T(8,128)S(1)}, u32[]{:S(2)}, u32[]{:S(2)}) collective-permute-start(f32[3,56,128]{2,1,0:T(8,128)S(1)} %shard_map.88.refs_0_), channel_id=1, source_target_pairs={{0,4},{1,5},{2,6},{3,7},{4,0},{5,1},{6,2},{7,3},{8,12},{9,13},{10,... | collective-permute-start | bytes 258056 | tf_op jit(solution)/shard_map/ppermute | solution.py:41
  27.7 10.7 %collective-permute-start.6 = (f32[3,56,128]{2,1,0:T(8,128)S(1)}, f32[3,56,128]{2,1,0:T(8,128)S(1)}, u32[]{:S(2)}, u32[]{:S(2)}) collective-permute-start(f32[3,56,128]{2,1,0:T(8,128)S(1)} %shard_map.88.refs_0_), channel_id=1, source_target_pairs={{0,5},{1,6},{2,7},{3,0},{4,1},{5,2},{6,3},{7,4},{8,13},{9,14},{10,... | collective-permute-start | bytes 258056 | tf_op jit(solution)/shard_map/ppermute | solution.py:41
  32.9 12.6 %collective-permute-start.7 = (f32[3,56,128]{2,1,0:T(8,128)S(1)}, f32[3,56,128]{2,1,0:T(8,128)S(1)}, u32[]{:S(2)}, u32[]{:S(2)}) collective-permute-start(f32[3,56,128]{2,1,0:T(8,128)S(1)} %shard_map.88.refs_0_), channel_id=1, source_target_pairs={{0,6},{1,7},{2,0},{3,1},{4,2},{5,3},{6,4},{7,5},{8,14},{9,15},{10,... | collective-permute-start | bytes 258056 | tf_op jit(solution)/shard_map/ppermute | solution.py:41
  35.4 10.6 %collective-permute-start.8 = (f32[3,56,128]{2,1,0:T(8,128)S(1)}, f32[3,56,128]{2,1,0:T(8,128)S(1)}, u32[]{:S(2)}, u32[]{:S(2)}) collective-permute-start(f32[3,56,128]{2,1,0:T(8,128)S(1)} %shard_map.88.refs_0_), channel_id=1, source_target_pairs={{0,7},{1,0},{2,1},{3,2},{4,3},{5,4},{6,5},{7,6},{8,15},{9,8},{10,9... | collective-permute-start | bytes 258056 | tf_op jit(solution)/shard_map/ppermute | solution.py:41
  62.8 12.8 %all-to-all-start.2 = ((f32[8,64,128]{2,1,0:T(8,128)}), f32[8,64,128]{2,1,0:T(8,128)S(1)}, u32[]{:S(2)}, u32[]{:S(2)}) async-start(f32[8,64,128]{2,1,0:T(8,128)} %get-tuple-element.21), calls=%async_computation.2 | async-start | bytes 524288 | tf_op jit(solution)/shard_map/all_to_all | solution.py:32
  66.3 4.3 %collective-permute-start.10 = (f32[56,128]{1,0:T(8,128)S(1)}, f32[56,128]{1,0:T(8,128)S(1)}, u32[]{:S(2)}, u32[]{:S(2)}) collective-permute-start(f32[56,128]{1,0:T(8,128)S(1)} %get-tuple-element.22.refs_0_), channel_id=1, source_target_pairs={{0,128},{64,192},{128,0},{192,64},{1,129},{65,193},{129,1},{193,65... | collective-permute-start | bytes 86024 | tf_op jit(solution)/shard_map/ppermute | solution.py:41
  68.2 2.7 %collective-permute-start.11 = (f32[56,128]{1,0:T(8,128)S(1)}, f32[56,128]{1,0:T(8,128)S(1)}, u32[]{:S(2)}, u32[]{:S(2)}) collective-permute-start(f32[56,128]{1,0:T(8,128)S(1)} %get-tuple-element.22.refs_0_), channel_id=1, source_target_pairs={{0,192},{64,0},{128,64},{192,128},{1,193},{65,1},{129,65},{193,129... | collective-permute-start | bytes 86024 | tf_op jit(solution)/shard_map/ppermute | solution.py:41
  69.1 3.9 %collective-permute-start.9 = (f32[56,128]{1,0:T(8,128)S(1)}, f32[56,128]{1,0:T(8,128)S(1)}, u32[]{:S(2)}, u32[]{:S(2)}) collective-permute-start(f32[56,128]{1,0:T(8,128)S(1)} %get-tuple-element.22.refs_0_), channel_id=1, source_target_pairs={{0,64},{64,128},{128,192},{192,0},{1,65},{65,129},{129,193},{193,1... | collective-permute-start | bytes 86024 | tf_op jit(solution)/shard_map/ppermute | solution.py:41
  75.6 5.2 %collective-permute-start.12 = (f32[232,128]{1,0:T(8,128)S(1)}, f32[232,128]{1,0:T(8,128)S(1)}, u32[]{:S(2)}, u32[]{:S(2)}) collective-permute-start(f32[232,128]{1,0:T(8,128)S(1)} %shard_map.91.mine_ref), channel_id=1, source_target_pairs={{0,32},{32,0},{1,33},{33,1},{2,34},{34,2},{3,35},{35,3},{4,36},{36... | collective-permute-start | bytes 356360 | tf_op jit(solution)/shard_map/ppermute | solution.py:36
  118.9 5.6 %collective-permute-start.14 = (bf16[8,448,128]{2,1,0:T(8,128)(2,1)S(1)}, bf16[8,448,128]{2,1,0:T(8,128)(2,1)S(1)}, u32[]{:S(2)}, u32[]{:S(2)}) collective-permute-start(bf16[8,448,128]{2,1,0:T(8,128)(2,1)S(1)} %get-tuple-element.34), channel_id=1, source_target_pairs={{0,32},{32,0},{1,33},{33,1},{2,34},{34,2},{3,35},{35,3},{4,36},{36... | collective-permute-start | bytes 2752520 | tf_op jit(solution)/shard_map/ppermute | solution.py:36
  122.3 3.7 %collective-permute-start.13 = (bf16[8,448,128]{2,1,0:T(8,128)(2,1)S(1)}, bf16[8,448,128]{2,1,0:T(8,128)(2,1)S(1)}, u32[]{:S(2)}, u32[]{:S(2)}) collective-permute-start(bf16[8,448,128]{2,1,0:T(8,128)(2,1)S(1)} %get-tuple-element.35), channel_id=1, source_target_pairs={{0,32},{32,0},{1,33},{33,1},{2,34},{34,2},{3,35},{35,3},{4,36},{36... | collective-permute-start | bytes 2752520 | tf_op jit(solution)/shard_map/ppermute | solution.py:36
